TPU v7x, 512 devices: a whole 4x8x8 slice. The times are simulated.
512 devices in a mesh: grp: 2 (over x_lo), dom: 256 (over z, y, x_hi, core).
Axes of the slice: x: 4 (x_hi: 2, x_lo: 2; x = x_hi * 2 + x_lo), y: 8, z: 8, core: 2. Of those that a mesh axis runs over, the one named last changes fastest.
Arguments:
- surplus: float32 [48, 64, 65536], P('grp', None, 'dom'), may hold values from -40 to 40
- levels: int32 [48, 3], P('grp'), may hold values from 0 to 3
Outputs:
- updated: float32 [48, 64, 65536], P('grp', None, 'dom')
- coefficients: float32 [48], replicated
All inputs are finite; a program needn't handle non-finite values.
Results may differ from a plain program's by a relative error of at most 0.0003.
Values sent between devices are 32-bit elements; how exact they have to be, the bound alone decides.
No kernel may reach another device: no remote copies, remote signals or barrier semaphores. Data moves between devices by JAX's collectives and lax.ppermute only.
A program may use at most 64 MiB of HBM per device.

v0:
```python
import functools

import jax
import jax.numpy as jnp
from jax import lax
from jax.sharding import Mesh
from jax.sharding import PartitionSpec as P

GRP_DOM = ("grp", "dom_0", "dom_1", "dom_2", "dom_3")
DOM = ("dom_0", "dom_1", "dom_2", "dom_3")


def cut_along(array, dim, devices):
    shape = array.shape
    tiles = array.reshape(*shape[:dim], devices, shape[dim] // devices, *shape[dim + 1 :])
    return jnp.moveaxis(tiles, dim, 0)


def cut_rows(length, count):
    unit = 8 if length >= 8 * count else 1
    return [length // unit * k // count * unit for k in range(1, count)]


def in_order(tiles, dim):
    tiles = jnp.moveaxis(tiles, 0, dim)
    shape = tiles.shape
    return tiles.reshape(*shape[:dim], shape[dim] * shape[dim + 1], *shape[dim + 2 :])


def several_exchanges(array, axis, pieces, split_dim, concat_dim):
    tiles = cut_along(array, split_dim, lax.axis_size(axis))
    cut = max(range(1, max(2, tiles.ndim - 1)), key=lambda d: tiles.shape[d])
    finished = []
    for section in jnp.split(tiles, cut_rows(tiles.shape[cut], pieces), axis=cut):
        if section.size:
            finished.append(lax.all_to_all(section, axis, split_axis=0, concat_axis=0, tiled=True))
    return in_order(jnp.concatenate(finished, axis=cut), concat_dim)


def by_axis(array, axes):
    return functools.reduce(lax.psum, axes, array)


def copy_for_each(array, axis):
    copies = jnp.broadcast_to(array, (lax.axis_size(axis), *array.shape))
    return lax.all_to_all(copies, axis, split_axis=0, concat_axis=0, tiled=True)


def of_everyone(array, axis):
    everything = copy_for_each(array, axis)
    return jnp.sum(everything, axis=0)


def owned(levels, count):
    indices = jnp.arange(count, dtype=jnp.int32)
    digits = jnp.stack([indices // 16, indices // 4 % 4, indices % 4])
    return jnp.all(digits[None] <= levels[:, :, None], axis=1).astype(jnp.float32)


def solve_weights(gram_matrix):
    number = gram_matrix.shape[0]
    diagonal_part = jnp.diagonal(gram_matrix) + 1e-06
    scaling = 1.0 / jnp.sqrt(diagonal_part)
    system = scaling[:, None] * gram_matrix * scaling[None, :] + 0.1 * jnp.eye(
        number, dtype=jnp.float32
    )
    factor = jnp.linalg.cholesky(system)
    target = jnp.sqrt(diagonal_part)[:, None]
    halfway = lax.linalg.triangular_solve(factor, target, left_side=True, lower=True)
    weights = lax.linalg.triangular_solve(
        factor, halfway, left_side=True, lower=True, transpose_a=True
    )
    return scaling * weights[:, 0]


def inner_rows(left_rows, right_rows):
    return lax.dot_general(
        left_rows,
        right_rows,
        (((1,), (1,)), ((), ())),
        precision=lax.Precision.HIGHEST,
        preferred_element_type=jnp.float32,
    )


def shards(surplus, levels):
    local_count = surplus.shape[0]
    subspaces = surplus.shape[1]
    grid_total = local_count * lax.axis_size("grp")
    owners = owned(levels, subspaces)
    masked = surplus * owners[:, :, None]
    swapped = several_exchanges(masked, "grp", 2, 2, 0)
    swapped_rows = swapped.reshape(grid_total, -1)
    gram_matrix = by_axis(inner_rows(swapped_rows, swapped_rows), GRP_DOM)
    coefficients = solve_weights(gram_matrix)
    own_weights = lax.dynamic_slice_in_dim(
        coefficients, lax.axis_index("grp") * local_count, local_count
    )
    partial_sum = jnp.tensordot(own_weights, masked, axes=1, precision=lax.Precision.HIGHEST)
    combined = of_everyone(partial_sum, "grp")
    updated = owners[:, :, None] * combined[None]
    return (updated, coefficients)


def solution(mesh):
    torus = Mesh(
        mesh.devices.reshape(mesh.shape["grp"], 8, 8, 2, 2),
        ("grp", "dom_0", "dom_1", "dom_2", "dom_3"),
    )
    return jax.shard_map(
        shards,
        mesh=torus,
        in_specs=(P("grp", None, DOM), P("grp", None)),
        out_specs=(P("grp", None, DOM), P()),
        check_vma=False,
    )
```

profile of v0, /device:TPU:1, one launch (start us, length us, event | category | flops | bytes accessed | tf_op | source)
XLA Modules:
  0.0 147.6 jit_solution(6044541803464647579)
XLA Ops:
  0.7 0.8 compare_reduce_fusion
  1.5 1.7 %bitcast_bitcast_fusion = f32[2,24,64,128]{3,2,1,0:T(8,128)S(1)} fusion(f32[24,64,256]{2,1,0:T(8,128)} %param.2, f32[24,64]{1,0:T(8,128)S(1)} %convert_element_type.8), kind=kLoop, calls=%fused_computation.4 | loop fusion | flops 393216 | bytes 3151872 | tf_op jit(solution)/shard_map/transpose | solution.py:16
  3.2 1.3 fusion.18
  4.5 0.0 copy-start
  4.5 3.7 %all-to-all-start = ((f32[2,24,32,128]{3,2,1,0:T(8,128)}), f32[2,24,32,128]{3,2,1,0:T(8,128)S(1)}, u32[]{:S(2)}, u32[]{:S(2)}) async-start(f32[2,24,32,128]{3,2,1,0:T(8,128)} %get-tuple-element.2), calls=%async_computation | async-start | bytes 1572864 | tf_op jit(solution)/shard_map/all_to_all | solution.py:36
  8.2 7.4 %all-to-all-done = f32[2,24,32,128]{3,2,1,0:T(8,128)S(1)} async-done(((f32[2,24,32,128]{3,2,1,0:T(8,128)}), f32[2,24,32,128]{3,2,1,0:T(8,128)S(1)}, u32[]{:S(2)}, u32[]{:S(2)}) %all-to-all-start) | async-done | bytes 786464 | tf_op jit(solution)/shard_map/all_to_all | solution.py:36
  15.6 0.0 copy-start.1
  15.6 4.3 %all-to-all-start.1 = ((f32[2,24,32,128]{3,2,1,0:T(8,128)}), f32[2,24,32,128]{3,2,1,0:T(8,128)}, u32[]{:S(2)}, u32[]{:S(2)}) async-start(f32[2,24,32,128]{3,2,1,0:T(8,128)} %get-tuple-element.3), calls=%async_computation.1 | async-start | bytes 1572864 | tf_op jit(solution)/shard_map/all_to_all | solution.py:36
  19.9 0.0 copy-done.1
  19.9 0.0 copy-done
  19.9 0.3 broadcast_multiply_fusion.1
  20.2 6.6 %all-to-all-done.1 = f32[2,24,32,128]{3,2,1,0:T(8,128)} async-done(((f32[2,24,32,128]{3,2,1,0:T(8,128)}), f32[2,24,32,128]{3,2,1,0:T(8,128)}, u32[]{:S(2)}, u32[]{:S(2)}) %all-to-all-start.1) | async-done | bytes 786464 | tf_op jit(solution)/shard_map/all_to_all | solution.py:36
  26.8 1.5 %pad_maximum_fusion = f32[2,24,64,128]{3,2,1,0:T(8,128)S(1)} fusion(f32[2,24,32,128]{3,2,1,0:T(8,128)} %all-to-all-done.1, f32[2,24,32,128]{3,2,1,0:T(8,128)} %copy-done.1), kind=kLoop, calls=%fused_computation.5 | loop fusion | flops 393216 | bytes 3145728 | tf_op jit(solution)/shard_map/concatenate | solution.py:37
  28.3 2.6 %fusion = f32[48,48]{1,0:T(8,128)S(1)} fusion(f32[6,8,64,128]{3,2,1,0:T(8,128)S(1)} %bitcast.42), kind=kOutput, calls=%fused_computation.1 | convolution fusion | flops 226492416 | bytes 1582080 | tf_op jit(solution)/shard_map/dot_general | solution.py:77
  30.9 5.1 %psum.35 = f32[48,48]{1,0:T(8,128)S(1)} all-reduce(f32[48,48]{1,0:T(8,128)S(1)} %fusion), channel_id=1, replica_groups=mesh['grp'=2,'dom_0'=8,'dom_1'=8,'dom_2'=2,'dom_3'=2] {'grp'}, use_global_device_ids=true, to_apply=%region_1.2 | all-reduce | flops 2304 | bytes 18432 | tf_op jit(solution)/shard_map/psum | solution.py:41
  36.0 35.3 %psum.36 = f32[48,48]{1,0:T(8,128)S(1)} all-reduce(f32[48,48]{1,0:T(8,128)S(1)} %psum.35), channel_id=1, replica_groups=mesh['grp'=2,'dom_0'=8,'dom_1'=8,'dom_2'=2,'dom_3'=2] {'dom_0'}, use_global_device_ids=true, to_apply=%region_2.3 | all-reduce | flops 2304 | bytes 18432 | tf_op jit(solution)/shard_map/psum | solution.py:41
  71.3 23.1 %psum.37 = f32[48,48]{1,0:T(8,128)S(1)} all-reduce(f32[48,48]{1,0:T(8,128)S(1)} %psum.36), channel_id=1, replica_groups=mesh['grp'=2,'dom_0'=8,'dom_1'=8,'dom_2'=2,'dom_3'=2] {'dom_1'}, use_global_device_ids=true, to_apply=%region_3.4 | all-reduce | flops 2304 | bytes 18432 | tf_op jit(solution)/shard_map/psum | solution.py:41
  94.4 9.3 %psum.38 = f32[48,48]{1,0:T(8,128)S(1)} all-reduce(f32[48,48]{1,0:T(8,128)S(1)} %psum.37), channel_id=1, replica_groups=mesh['grp'=2,'dom_0'=8,'dom_1'=8,'dom_2'=2,'dom_3'=2] {'dom_2'}, use_global_device_ids=true, to_apply=%region_4.5 | all-reduce | flops 2304 | bytes 18432 | tf_op jit(solution)/shard_map/psum | solution.py:41
  103.7 23.6 %psum.39 = f32[48,48]{1,0:T(8,128)S(1)} all-reduce(f32[48,48]{1,0:T(8,128)S(1)} %psum.38), channel_id=1, replica_groups=mesh['grp'=2,'dom_0'=8,'dom_1'=8,'dom_2'=2,'dom_3'=2] {'dom_3'}, use_global_device_ids=true, to_apply=%region_5.6 | all-reduce | flops 2304 | bytes 18432 | tf_op jit(solution)/shard_map/psum | solution.py:41
  127.3 1.0 gather_fusion
  128.3 0.1 select_add_fusion
  128.4 0.1 copy.10
  128.5 0.1 fusion.9
  128.6 4.4 %cholesky.16 = f32[48,48]{1,0:T(8,128)S(1)} custom-call(f32[48,48]{1,0:T(8,128)S(1)} %fusion.9), custom_call_target="Cholesky" | custom-call | tf_op jit(solution)/shard_map/jit(cholesky)/cholesky | solution.py:67
  133.0 0.6 compare_reduce_fusion.1
  133.6 0.7 fusion.6
  134.3 3.7 %custom-call.8 = f32[1,48,48]{1,2,0:T(8,128)S(1)} custom-call(f32[1,48,48]{2,1,0:T(8,128)S(1)} %fusion.6), custom_call_target="InvertDiagBlocksLowerTriangular" | custom-call | tf_op jit(solution)/shard_map/triangular_solve | solution.py:70
  137.9 0.1 convolution_bitcast_fusion.1
  138.1 0.2 fusion.5
  138.3 0.0 copy-start.2
  138.3 1.8 %fusion.3 = f32[1,64,256]{2,0,1:T(1,128)S(1)} fusion(f32[24,64,256]{2,1,0:T(8,128)S(1)} %broadcast_multiply_fusion.1, f32[48]{0:T(128)S(1)} %fusion.5, s32[]{:T(128)S(6)} %select_n.63), kind=kOutput, calls=%fused_computation.6 | convolution fusion | flops 4718592 | bytes 1638596 | tf_op jit(solution)/shard_map/dot_general | solution.py:99
  140.1 6.1 %all_to_all.15 = f32[2,64,256]{2,1,0:T(8,128)S(1)} all-to-all(f32[2,64,256]{2,1,0:T(8,128)S(1)} %broadcast_in_dim.7), channel_id=1, replica_groups=mesh['grp'=2,'dom_0'=8,'dom_1'=8,'dom_2'=2,'dom_3'=2] {'grp'}, dimensions={0} | all-to-all | bytes 262144 | tf_op jit(solution)/shard_map/all_to_all | solution.py:46
  146.1 1.4 broadcast_multiply_fusion
  147.6 0.0 copy-done.2
  (10 shorter events, 0.1 us)
Async XLA Ops:
  4.5 15.4 %copy-start = (f32[24,64,256]{2,1,0:T(8,128)S(1)}, f32[24,64,256]{2,1,0:T(8,128)}, u32[]{:S(2)}) copy-start(f32[24,64,256]{2,1,0:T(8,128)} %param.2) | copy-start | bytes 4718596
  4.5 11.1 %all-to-all-start = ((f32[2,24,32,128]{3,2,1,0:T(8,128)}), f32[2,24,32,128]{3,2,1,0:T(8,128)S(1)}, u32[]{:S(2)}, u32[]{:S(2)}) async-start(f32[2,24,32,128]{3,2,1,0:T(8,128)} %get-tuple-element.2), calls=%async_computation | async-start | bytes 1572864 | tf_op jit(solution)/shard_map/all_to_all | solution.py:36
  15.6 4.3 %copy-start.1 = (f32[2,24,32,128]{3,2,1,0:T(8,128)}, f32[2,24,32,128]{3,2,1,0:T(8,128)S(1)}, u32[]{:S(2)}) copy-start(f32[2,24,32,128]{3,2,1,0:T(8,128)S(1)} %all-to-all-done) | copy-start | bytes 2359300
  15.6 11.2 %all-to-all-start.1 = ((f32[2,24,32,128]{3,2,1,0:T(8,128)}), f32[2,24,32,128]{3,2,1,0:T(8,128)}, u32[]{:S(2)}, u32[]{:S(2)}) async-start(f32[2,24,32,128]{3,2,1,0:T(8,128)} %get-tuple-element.3), calls=%async_computation.1 | async-start | bytes 1572864 | tf_op jit(solution)/shard_map/all_to_all | solution.py:36
  138.3 9.3 %copy-start.2 = (f32[48]{0:T(128)}, f32[48]{0:T(128)S(1)}, u32[]{:S(2)}) copy-start(f32[48]{0:T(128)S(1)} %fusion.5) | copy-start | bytes 580
where the time goes:
time: 148 us
  blocking collectives  102 us (69%)
  other arithmetic  15.3 us (10%)
  waiting for transfers between devices  14 us (9%)
  starting transfers between devices  7.96 us (5%)
  matrix products  4.68 us (3%)
  local copies, waits for them, and re-layouts  2.36 us (2%)
    psum x5, blocking collectives, by_axis(): return functools.reduce(lax.psum, axes, array)  96.4 us
    all_to_all x2, waiting for transfers between devices, several_exchanges(): lax.all_to_all(section, axis, split_axis=0, concat_axis=0, tiled=True)  14 us
    all_to_all x2, starting transfers between devices, several_exchanges(): lax.all_to_all(section, axis, split_axis=0, concat_axis=0, tiled=True)  7.96 us
    all_to_all x1, blocking collectives, copy_for_each(): return lax.all_to_all(copies, axis, split_axis=0, concat_axis=0, tiled=True)  6.06 us
    another operation x3, other arithmetic, solve_weights(): factor = jnp.linalg.cholesky(system)  5.06 us
    another operation x2, other arithmetic, solve_weights(): lax.linalg.triangular_solve(factor, halfway, left_side=True, lower=True,...  4.32 us
  transfers between devices with their start and end apart: 2, of which 2 were waited for; matrix products, arithmetic and copies ran while one was open for 0% of the time, Pallas kernels for 0%

commit v1 on v0

v1 whole, which is shorter than its diff:
```python
import jax
import jax.numpy as jnp
from jax import lax
from jax.sharding import Mesh
from jax.sharding import PartitionSpec as P

DOM = ("dom_0", "dom_1", "dom_2", "dom_3")
STAGES = (("dom_0",), ("dom_1",), ("grp", "dom_2", "dom_3"))
SWAP = ((0, 1), (1, 0))


def owned(levels, count):
    indices = jnp.arange(count, dtype=jnp.int32)
    digits = jnp.stack([indices // 16, indices // 4 % 4, indices % 4])
    return jnp.all(digits[None] <= levels[:, :, None], axis=1).astype(jnp.float32)


def solve_weights(gram_matrix):
    number = gram_matrix.shape[0]
    diagonal_part = jnp.diagonal(gram_matrix) + 1e-06
    scaling = 1.0 / jnp.sqrt(diagonal_part)
    system = scaling[:, None] * gram_matrix * scaling[None, :] + 0.1 * jnp.eye(
        number, dtype=jnp.float32
    )
    factor = jnp.linalg.cholesky(system)
    target = jnp.sqrt(diagonal_part)[:, None]
    halfway = lax.linalg.triangular_solve(factor, target, left_side=True, lower=True)
    weights = lax.linalg.triangular_solve(
        factor, halfway, left_side=True, lower=True, transpose_a=True
    )
    return scaling * weights[:, 0]


def inner(left, right):
    return lax.dot_general(
        left,
        right,
        (((1, 2), (1, 2)), ((), ())),
        precision=lax.Precision.HIGHEST,
        preferred_element_type=jnp.float32,
    )


def summed(array, axes):
    count = lax.axis_size(axes)
    copies = jnp.broadcast_to(array, (count, *array.shape))
    return jnp.sum(lax.all_to_all(copies, axes, split_axis=0, concat_axis=0, tiled=True), axis=0)


def weighted(weights, grids):
    return jnp.sum(weights[:, None, None] * grids, axis=0)


def shards(surplus, levels):
    local, subspaces, cells = surplus.shape
    half = cells // 2
    second = lax.axis_index("grp") == 1
    owners = owned(levels, subspaces)
    masked = surplus * owners[:, :, None]
    low, high = masked[:, :, :half], masked[:, :, half:]
    near = jnp.where(second, high, low)
    far = jnp.where(second, low, high)
    got_near = lax.ppermute(far, "grp", SWAP)
    got_far = lax.ppermute(near, "grp", SWAP)
    own_block = inner(masked, masked)
    cross = inner(near, got_near)
    cross = jnp.where(second, cross.T, cross)
    zero = jnp.zeros_like(own_block)
    parts = jnp.concatenate(
        [
            jnp.where(second, zero, own_block),
            cross,
            jnp.where(second, own_block, zero),
            jnp.zeros((local, 128 - 3 * local), jnp.float32),
        ],
        axis=1,
    )
    for axes in STAGES:
        parts = summed(parts, axes)
    first, cross, last = (parts[:, k * local : (k + 1) * local] for k in range(3))
    gram_matrix = jnp.concatenate(
        [jnp.concatenate([first, cross], axis=1), jnp.concatenate([cross.T, last], axis=1)], axis=0
    )
    coefficients = solve_weights(gram_matrix)
    start, stop = coefficients[:local], coefficients[local:]
    own = jnp.where(second, stop, start)
    other = jnp.where(second, start, stop)
    sum_near = weighted(own, near) + weighted(other, got_near)
    sum_far = weighted(own, far) + weighted(other, got_far)
    combined = jnp.concatenate(
        [jnp.where(second, sum_far, sum_near), jnp.where(second, sum_near, sum_far)], axis=1
    )
    return owners[:, :, None] * combined[None], coefficients


def solution(mesh):
    torus = Mesh(
        mesh.devices.reshape(mesh.shape["grp"], 8, 8, 2, 2),
        ("grp", *DOM),
    )
    return jax.shard_map(
        shards,
        mesh=torus,
        in_specs=(P("grp", None, DOM), P("grp", None)),
        out_specs=(P("grp", None, DOM), P()),
        check_vma=False,
    )
```

time: 148 us -> 89.6 us (0.61)
  blocking collectives: 102 us -> 22.3 us
  starting transfers between devices: 7.96 us -> 22.5 us
  waiting for transfers between devices: 14 us -> 22.1 us
  local copies, waits for them, and re-layouts: 2.36 us -> 4.35 us
  matrix products: 4.68 us -> 2.9 us
    psum x5 -> x0, blocking collectives: 96.4 us -> none  [by_axis(): return functools.reduce(lax.psum, axes, array)]
    all_to_all x1, blocking collectives: 6.06 us -> 22.3 us  [summed(): lax.all_to_all(copies, axes, split_axis=0, concat_axis=0, tiled=True)]
    ppermute x0 -> x2, waiting for transfers between devices: none -> 10.5 us  [the longest x1 10.5 us: shards(): got_near = lax.ppermute(far, 'grp', SWAP)]
    all_to_all x2, starting transfers between devices: 7.96 us -> 15.4 us  [summed(): lax.all_to_all(copies, axes, split_axis=0, concat_axis=0, tiled=True)]
    ppermute x0 -> x2, starting transfers between devices: none -> 7.05 us  [the longest x1 3.94 us: shards(): got_near = lax.ppermute(far, 'grp', SWAP)]
    all_to_all x2, waiting for transfers between devices: 14 us -> 11.6 us  [summed(): lax.all_to_all(copies, axes, split_axis=0, concat_axis=0, tiled=True)]
    mul x1, other arithmetic: 0.27 us -> 2.36 us  [shards(): masked = surplus * owners[:, :, None]]
    dot_general x2, matrix products: 4.37 us -> 2.6 us  [inner(): lax.dot_general(left, right, (((1, 2), (1, 2)), ((), ())), precision=lax....]
  transfers between devices with their start and end apart: 2 -> 4, of which waited for: 2 -> 3; matrix products, arithmetic and copies ran while one was open for 0% -> 16% of each run, Pallas kernels for 0% -> 0%
where the time goes in v1:
time: 89.6 us; the launch traced here: 89.1 us
  starting transfers between devices  22.5 us (25%)
  blocking collectives  22.3 us (25%)
  waiting for transfers between devices  22.1 us (25%)
  other arithmetic  14.1 us (16%)
  local copies, waits for them, and re-layouts  4.35 us (5%)
  matrix products  2.9 us (3%)
    all_to_all x1, blocking collectives, summed(): lax.all_to_all(copies, axes, split_axis=0, concat_axis=0, tiled=True)  22.3 us
    all_to_all x2, starting transfers between devices, summed(): lax.all_to_all(copies, axes, split_axis=0, concat_axis=0, tiled=True)  15.4 us
    all_to_all x2, waiting for transfers between devices, summed(): lax.all_to_all(copies, axes, split_axis=0, concat_axis=0, tiled=True)  11.6 us
    ppermute x1, waiting for transfers between devices, shards(): got_near = lax.ppermute(far, 'grp', SWAP)  10.5 us
    another operation x3, other arithmetic, solve_weights(): factor = jnp.linalg.cholesky(system)  5.05 us
    another operation x2, other arithmetic, solve_weights(): lax.linalg.triangular_solve(factor, halfway, left_side=True, lower=True,...  4.32 us
    ppermute x1, starting transfers between devices, shards(): got_near = lax.ppermute(far, 'grp', SWAP)  3.94 us
    ppermute x1, starting transfers between devices, shards(): got_far = lax.ppermute(near, 'grp', SWAP)  3.11 us
  transfers between devices with their start and end apart: 4, of which 3 were waited for; matrix products, arithmetic and copies ran while one was open for 16% of the time, Pallas kernels for 0%

profile of v1, /device:TPU:1, one launch (start us, length us, event | category | flops | bytes accessed | tf_op | source)
XLA Modules:
  0.0 89.1 jit_solution(847404895742147005)
XLA Ops:
  0.7 0.8 compare_reduce_fusion
  1.5 0.1 copy.16
  1.5 2.4 %copy_multiply_fusion = f32[24,64,256]{2,0,1:T(8,128)S(1)} fusion(f32[24,64,256]{2,1,0:T(8,128)} %param.2, f32[24,64]{0,1:T(8,128)S(1)} %copy.16), kind=kLoop, calls=%fused_computation.1 | loop fusion | flops 393216 | bytes 3151872 | tf_op jit(solution)/shard_map/mul | solution.py:59
  3.9 0.1 slice_select_fusion.1
  4.0 3.9 %collective-permute-start = (f32[24,64,128]{2,0,1:T(8,128)S(1)}, f32[24,64,128]{2,0,1:T(8,128)S(1)}, u32[]{:S(2)}, u32[]{:S(2)}) collective-permute-start(f32[24,64,128]{2,0,1:T(8,128)S(1)} %get-tuple-element.13), channel_id=1, source_target_pairs={{0,256},{256,0},{1,257},{257,1},{2,258},{258,2},{3,259},{259,3},{4... | collective-permute-start | bytes 2359304 | tf_op jit(solution)/shard_map/ppermute | solution.py:63
  8.0 0.1 pad.8.clone
  8.1 1.7 %broadcast_select_fusion.3 = (f32[24,24]{1,0:T(8,128)S(1)}, f32[24,24]{1,0:T(8,128)S(1)}) fusion(pred[]{:T(512)S(6)} %eq.7, f32[24,64,256]{2,0,1:T(8,128)S(1)} %copy_multiply_fusion), kind=kOutput, calls=%fused_computation.32 | convolution fusion | flops 113247360 | bytes 1577473 | tf_op jit(solution)/shard_map/dot_general | solution.py:35
  9.8 10.5 %collective-permute-done = f32[24,64,128]{2,0,1:T(8,128)S(1)} collective-permute-done((f32[24,64,128]{2,0,1:T(8,128)S(1)}, f32[24,64,128]{2,0,1:T(8,128)S(1)}, u32[]{:S(2)}, u32[]{:S(2)}) %collective-permute-start) | collective-permute-done | bytes 786464 | tf_op jit(solution)/shard_map/ppermute | solution.py:63
  20.3 0.9 convolution_bitcast_fusion
  21.2 0.1 copy.18
  21.3 0.1 maximum_maximum_fusion.1
  21.4 22.3 %all_to_all.15 = f32[8,24,128]{2,1,0:T(8,128)S(1)} all-to-all(f32[8,24,128]{2,1,0:T(8,128)S(1)} %broadcast_in_dim.18), channel_id=1, replica_groups=mesh['grp'=2,'dom_0'=8,'dom_1'=8,'dom_2'=2,'dom_3'=2] {'dom_0'}, dimensions={0} | all-to-all | bytes 196608 | tf_op jit(solution)/shard_map/all_to_all | solution.py:47
  43.7 0.6 broadcast_in_dim.19
  44.4 6.8 %all-to-all-start.1 = ((f32[8,24,128]{2,1,0:T(8,128)}), f32[8,24,128]{2,1,0:T(8,128)S(1)}, u32[]{:S(2)}, u32[]{:S(2)}) async-start(f32[8,24,128]{2,1,0:T(8,128)} %broadcast_in_dim.19), calls=%async_computation.1 | async-start | bytes 196608 | tf_op jit(solution)/shard_map/all_to_all | solution.py:47
  51.2 3.1 %collective-permute-start.1 = (f32[24,64,128]{2,0,1:T(8,128)S(1)}, f32[24,64,128]{2,0,1:T(8,128)S(1)}, u32[]{:S(2)}, u32[]{:S(2)}) collective-permute-start(f32[24,64,128]{2,0,1:T(8,128)S(1)} %get-tuple-element.12), channel_id=1, source_target_pairs={{0,256},{256,0},{1,257},{257,1},{2,258},{258,2},{3,259},{259,3},{4... | collective-permute-start | bytes 2359304 | tf_op jit(solution)/shard_map/ppermute | solution.py:64
  54.3 4.5 %all-to-all-done.1 = f32[8,24,128]{2,1,0:T(8,128)S(1)} async-done(((f32[8,24,128]{2,1,0:T(8,128)}), f32[8,24,128]{2,1,0:T(8,128)S(1)}, u32[]{:S(2)}, u32[]{:S(2)}) %all-to-all-start.1) | async-done | bytes 98336 | tf_op jit(solution)/shard_map/all_to_all | solution.py:47
  58.8 0.6 broadcast_in_dim.20
  59.5 8.6 %all-to-all-start.2 = ((f32[8,24,128]{2,1,0:T(8,128)}), f32[8,24,128]{2,1,0:T(8,128)S(1)}, u32[]{:S(2)}, u32[]{:S(2)}) async-start(f32[8,24,128]{2,1,0:T(8,128)} %broadcast_in_dim.20), calls=%async_computation.2 | async-start | bytes 196608 | tf_op jit(solution)/shard_map/all_to_all | solution.py:47
  68.1 7.1 %all-to-all-done.2 = f32[8,24,128]{2,1,0:T(8,128)S(1)} async-done(((f32[8,24,128]{2,1,0:T(8,128)}), f32[8,24,128]{2,1,0:T(8,128)S(1)}, u32[]{:S(2)}, u32[]{:S(2)}) %all-to-all-start.2) | async-done | bytes 98336 | tf_op jit(solution)/shard_map/all_to_all | solution.py:47
  75.2 0.1 fusion.11
  75.3 0.1 copy.22
  75.4 0.1 maximum_maximum_fusion
  75.4 1.0 %gather_fusion = f32[48]{0:T(128)S(1)} fusion(f32[48,48]{1,0:T(8,128)S(1)} %maximum_maximum_fusion, s32[48]{0:T(128)S(1)} %or_bitcast_fusion), kind=kCustom, calls=%fused_computation | custom fusion | bytes 768 | tf_op jit(solution)/shard_map/jit(diagonal)/cond/branch_0_fun/gather | solution.py:20
  76.4 0.1 select_add_fusion
  76.5 0.1 copy.20
  76.6 0.1 fusion.4
  76.7 4.4 %cholesky.16 = f32[48,48]{1,0:T(8,128)S(1)} custom-call(f32[48,48]{1,0:T(8,128)S(1)} %fusion.4), custom_call_target="Cholesky" | custom-call | tf_op jit(solution)/shard_map/jit(cholesky)/cholesky | solution.py:25
  81.1 0.6 compare_reduce_fusion.1
  81.7 0.7 fusion.1
  82.4 3.7 %custom-call.8 = f32[1,48,48]{1,2,0:T(8,128)S(1)} custom-call(f32[1,48,48]{2,1,0:T(8,128)S(1)} %fusion.1), custom_call_target="InvertDiagBlocksLowerTriangular" | custom-call | tf_op jit(solution)/shard_map/triangular_solve | solution.py:28
  86.1 0.1 convolution_bitcast_fusion.3
  86.2 0.2 fusion
  86.4 0.0 copy-start
  86.4 0.1 broadcast_select_fusion.4
  86.5 0.3 multiply_reduce_fusion.3
  86.8 0.0 collective-permute-done.1
  86.8 0.4 multiply_reduce_fusion.2
  87.2 0.0 copy-done
  87.2 0.3 broadcast_multiply_fusion
  87.5 1.6 %copy.21 = f32[24,64,256]{2,1,0:T(8,128)} copy(f32[24,64,256]{2,0,1:T(8,128)S(1)} %broadcast_multiply_fusion) | data formatting | bytes 3145728
  (15 shorter events, 0.2 us)
Async XLA Ops:
  4.0 16.3 %collective-permute-start = (f32[24,64,128]{2,0,1:T(8,128)S(1)}, f32[24,64,128]{2,0,1:T(8,128)S(1)}, u32[]{:S(2)}, u32[]{:S(2)}) collective-permute-start(f32[24,64,128]{2,0,1:T(8,128)S(1)} %get-tuple-element.13), channel_id=1, source_target_pairs={{0,256},{256,0},{1,257},{257,1},{2,258},{258,2},{3,259},{259,3},{4... | collective-permute-start | bytes 2359304 | tf_op jit(solution)/shard_map/ppermute | solution.py:63
  44.4 14.4 %all-to-all-start.1 = ((f32[8,24,128]{2,1,0:T(8,128)}), f32[8,24,128]{2,1,0:T(8,128)S(1)}, u32[]{:S(2)}, u32[]{:S(2)}) async-start(f32[8,24,128]{2,1,0:T(8,128)} %broadcast_in_dim.19), calls=%async_computation.1 | async-start | bytes 196608 | tf_op jit(solution)/shard_map/all_to_all | solution.py:47
  51.2 35.6 %collective-permute-start.1 = (f32[24,64,128]{2,0,1:T(8,128)S(1)}, f32[24,64,128]{2,0,1:T(8,128)S(1)}, u32[]{:S(2)}, u32[]{:S(2)}) collective-permute-start(f32[24,64,128]{2,0,1:T(8,128)S(1)} %get-tuple-element.12), channel_id=1, source_target_pairs={{0,256},{256,0},{1,257},{257,1},{2,258},{258,2},{3,259},{259,3},{4... | collective-permute-start | bytes 2359304 | tf_op jit(solution)/shard_map/ppermute | solution.py:64
  59.5 15.7 %all-to-all-start.2 = ((f32[8,24,128]{2,1,0:T(8,128)}), f32[8,24,128]{2,1,0:T(8,128)S(1)}, u32[]{:S(2)}, u32[]{:S(2)}) async-start(f32[8,24,128]{2,1,0:T(8,128)} %broadcast_in_dim.20), calls=%async_computation.2 | async-start | bytes 196608 | tf_op jit(solution)/shard_map/all_to_all | solution.py:47
  86.4 0.8 copy-start

commit v2 on v1

v2 whole, which is shorter than its diff:
```python
import jax
import jax.numpy as jnp
from jax import lax
from jax.experimental import pallas as pl
from jax.experimental.pallas import tpu as pltpu
from jax.sharding import Mesh
from jax.sharding import PartitionSpec as P

DOM = ("dom_0", "dom_1", "dom_2", "dom_3")
STAGES = (("dom_0",), ("dom_1",), ("grp", "dom_2", "dom_3"))
SWAP = ((0, 1), (1, 0))
LANES = 128


def owned(levels, count):
    indices = jnp.arange(count, dtype=jnp.int32)
    digits = jnp.stack([indices // 16, indices // 4 % 4, indices % 4])
    return jnp.all(digits[None] <= levels[:, :, None], axis=1).astype(jnp.float32)


def solve_kernel(parts_ref, out_ref):
    number = 2 * parts_ref.shape[1]
    folded = parts_ref[0]
    for k in range(1, parts_ref.shape[0]):
        folded = folded + parts_ref[k]
    gram = jnp.concatenate([folded, pltpu.roll(folded, LANES - number, 1)], axis=0)
    rows = lax.broadcasted_iota(jnp.int32, gram.shape, 0)
    lanes = lax.broadcasted_iota(jnp.int32, gram.shape, 1)
    on_diagonal = rows == lanes
    diagonal = jnp.sum(jnp.where(on_diagonal, gram, 0.0), axis=1, keepdims=True) + 1e-06
    system = jnp.where(lanes < number, gram, 0.0) + jnp.where(on_diagonal, 0.1 * diagonal, 0.0)
    system = jnp.where(lanes == number, diagonal, system)
    for k in range(number):
        row = system[k : k + 1, :]
        column = jnp.broadcast_to(system[:, k : k + 1], system.shape)
        scaled = row * (1.0 / column[k : k + 1, :])
        system = system - jnp.where(rows == k, 0.0, column) * jnp.broadcast_to(scaled, system.shape)
    last = jnp.broadcast_to(system[:, number : number + 1], system.shape)
    out_ref[...] = jnp.sum(jnp.where(on_diagonal, last / system, 0.0), axis=0, keepdims=True)


def solve_parts(parts):
    whole = pl.BlockSpec(memory_space=pltpu.VMEM)
    return pl.pallas_call(
        solve_kernel,
        out_shape=jax.ShapeDtypeStruct((1, LANES), jnp.float32),
        in_specs=[whole],
        out_specs=whole,
    )(parts)


def inner(left, right):
    return lax.dot_general(
        left,
        right,
        (((1, 2), (1, 2)), ((), ())),
        precision=lax.Precision.HIGHEST,
        preferred_element_type=jnp.float32,
    )


def exchanged(array, axes):
    copies = jnp.broadcast_to(array, (lax.axis_size(axes), *array.shape))
    return lax.all_to_all(copies, axes, split_axis=0, concat_axis=0, tiled=True)


def weighted(weights, grids):
    return jnp.sum(weights[:, None, None] * grids, axis=0)


def shards(surplus, levels):
    local, subspaces, cells = surplus.shape
    half = cells // 2
    second = lax.axis_index("grp") == 1
    owners = owned(levels, subspaces)
    masked = surplus * owners[:, :, None]
    low, high = masked[:, :, :half], masked[:, :, half:]
    near = jnp.where(second, high, low)
    far = jnp.where(second, low, high)
    got_near = lax.ppermute(far, "grp", SWAP)
    got_far = lax.ppermute(near, "grp", SWAP)
    own_block = inner(masked, masked)
    cross = inner(near, got_near)
    zero = jnp.zeros_like(own_block)
    parts = jnp.concatenate(
        [
            jnp.where(second, zero, own_block),
            jnp.where(second, cross.T, cross),
            jnp.where(second, cross, cross.T),
            jnp.where(second, own_block, zero),
            jnp.zeros((local, LANES - 4 * local), jnp.float32),
        ],
        axis=1,
    )
    for axes in STAGES[:-1]:
        parts = jnp.sum(exchanged(parts, axes), axis=0)
    coefficients = solve_parts(exchanged(parts, STAGES[-1]))[0, : 2 * local]
    start, stop = coefficients[:local], coefficients[local:]
    own = jnp.where(second, stop, start)
    other = jnp.where(second, start, stop)
    sum_near = weighted(own, near) + weighted(other, got_near)
    sum_far = weighted(own, far) + weighted(other, got_far)
    combined = jnp.concatenate(
        [jnp.where(second, sum_far, sum_near), jnp.where(second, sum_near, sum_far)], axis=1
    )
    return owners[:, :, None] * combined[None], coefficients


def solution(mesh):
    torus = Mesh(
        mesh.devices.reshape(mesh.shape["grp"], 8, 8, 2, 2),
        ("grp", *DOM),
    )
    return jax.shard_map(
        shards,
        mesh=torus,
        in_specs=(P("grp", None, DOM), P("grp", None)),
        out_specs=(P("grp", None, DOM), P()),
        check_vma=False,
    )
```

time: 89.6 us -> 85.3 us (0.952)
  blocking collectives: 22.3 us -> 38.8 us
  other arithmetic: 14.1 us -> 5.04 us
  starting transfers between devices: 22.5 us -> 13.9 us
  waiting for transfers between devices: 22.1 us -> 15.1 us
  Pallas kernels: 0 us -> 5.61 us
  local copies, waits for them, and re-layouts: 4.35 us -> 3.05 us
    all_to_all x1 -> x2, blocking collectives: 22.3 us -> 38.8 us  [exchanged(): return lax.all_to_all(copies, axes, split_axis=0, concat_axis=0, tiled=True)]
    another operation x5 -> x0, other arithmetic: 9.37 us -> none  [the longest x3 5.05 us: solve_weights(): factor = jnp.linalg.cholesky(system)]
    all_to_all x2 -> x1, starting transfers between devices: 15.4 us -> 6.82 us  [exchanged(): return lax.all_to_all(copies, axes, split_axis=0, concat_axis=0, tiled=True)]
    all_to_all x2 -> x1, waiting for transfers between devices: 11.6 us -> 4.47 us  [exchanged(): return lax.all_to_all(copies, axes, split_axis=0, concat_axis=0, tiled=True)]
    pallas_call x0 -> x1, Pallas kernels: none -> 5.61 us  [solve_parts(): pl.pallas_call(solve_kernel, out_shape=jax.ShapeDtypeStruct((1, LANES), j...]
    gather x1 -> x0, local copies, waits for them, and re-layouts: 0.96 us -> none  [solve_weights(): diagonal_part = jnp.diagonal(gram_matrix) + 1e-06]
  transfers between devices with their start and end apart: 4 -> 3, of which waited for: 3 -> 2; matrix products, arithmetic and copies ran while one was open for 16% -> 4% of each run, Pallas kernels for 0% -> 7%
where the time goes in v2:
time: 85.3 us; the launch traced here: 84.9 us
  blocking collectives  38.8 us (45%)
  waiting for transfers between devices  15.1 us (18%)
  starting transfers between devices  13.9 us (16%)
  Pallas kernels  5.61 us (7%)
  other arithmetic  5.04 us (6%)
  local copies, waits for them, and re-layouts  3.05 us (4%)
  matrix products  2.6 us (3%)
    all_to_all x2, blocking collectives, exchanged(): return lax.all_to_all(copies, axes, split_axis=0, concat_axis=0, tiled=True)  38.8 us
    ppermute x1, waiting for transfers between devices, shards(): got_near = lax.ppermute(far, 'grp', SWAP)  10.6 us
    all_to_all x1, starting transfers between devices, exchanged(): return lax.all_to_all(copies, axes, split_axis=0, concat_axis=0, tiled=True)  6.82 us
    pallas_call x1, Pallas kernels, solve_parts(): pl.pallas_call(solve_kernel, out_shape=jax.ShapeDtypeStruct((1, LANES), j...  5.61 us
    all_to_all x1, waiting for transfers between devices, exchanged(): return lax.all_to_all(copies, axes, split_axis=0, concat_axis=0, tiled=True)  4.47 us
    ppermute x1, starting transfers between devices, shards(): got_near = lax.ppermute(far, 'grp', SWAP)  3.94 us
    ppermute x1, starting transfers between devices, shards(): got_far = lax.ppermute(near, 'grp', SWAP)  3.11 us
    dot_general x2, matrix products, inner(): lax.dot_general(left, right, (((1, 2), (1, 2)), ((), ())), precision=lax....  2.6 us
  transfers between devices with their start and end apart: 3, of which 2 were waited for; matrix products, arithmetic and copies ran while one was open for 4% of the time, Pallas kernels for 7%

profile of v2, /device:TPU:1, one launch (start us, length us, event | category | flops | bytes accessed | tf_op | source)
XLA Modules:
  0.0 84.9 jit_solution(8009128817869206419)
XLA Ops:
  0.7 0.8 compare_reduce_fusion
  1.5 0.1 copy.8
  1.5 2.4 %copy_multiply_fusion = f32[24,64,256]{2,0,1:T(8,128)S(1)} fusion(f32[24,64,256]{2,1,0:T(8,128)} %param.2, f32[24,64]{0,1:T(8,128)S(1)} %copy.8), kind=kLoop, calls=%fused_computation | loop fusion | flops 393216 | bytes 3151872 | tf_op jit(solution)/shard_map/mul | solution.py:76
  3.9 0.1 slice_select_fusion.1
  4.0 3.9 %collective-permute-start = (f32[24,64,128]{2,0,1:T(8,128)S(1)}, f32[24,64,128]{2,0,1:T(8,128)S(1)}, u32[]{:S(2)}, u32[]{:S(2)}) collective-permute-start(f32[24,64,128]{2,0,1:T(8,128)S(1)} %get-tuple-element.11), channel_id=1, source_target_pairs={{0,256},{256,0},{1,257},{257,1},{2,258},{258,2},{3,259},{259,3},{4... | collective-permute-start | bytes 2359304 | tf_op jit(solution)/shard_map/ppermute | solution.py:80
  8.0 1.7 %broadcast_select_fusion.2 = (f32[24,24]{1,0:T(8,128)S(1)}, f32[24,24]{1,0:T(8,128)S(1)}) fusion(pred[]{:T(512)S(6)} %eq.6, f32[24,64,256]{2,0,1:T(8,128)S(1)} %copy_multiply_fusion), kind=kOutput, calls=%fused_computation.16 | convolution fusion | flops 113247360 | bytes 1577473 | tf_op jit(solution)/shard_map/dot_general | solution.py:53
  9.7 10.6 %collective-permute-done = f32[24,64,128]{2,0,1:T(8,128)S(1)} collective-permute-done((f32[24,64,128]{2,0,1:T(8,128)S(1)}, f32[24,64,128]{2,0,1:T(8,128)S(1)}, u32[]{:S(2)}, u32[]{:S(2)}) %collective-permute-start) | collective-permute-done | bytes 786464 | tf_op jit(solution)/shard_map/ppermute | solution.py:80
  20.3 0.9 %convolution_bitcast_fusion = f32[24,24]{1,0:T(8,128)S(1)} fusion(f32[24,64,128]{2,0,1:T(8,128)S(1)} %get-tuple-element.10, f32[24,64,128]{2,0,1:T(8,128)S(1)} %collective-permute-done), kind=kOutput, calls=%fused_computation.1 | convolution fusion | flops 56623104 | bytes 1575168 | tf_op jit(solution)/shard_map/dot_general | solution.py:53
  21.2 0.1 copy.10
  21.3 0.1 concatenate.6
  21.4 22.3 %all_to_all.15 = f32[8,24,128]{2,1,0:T(8,128)S(1)} all-to-all(f32[8,24,128]{2,1,0:T(8,128)S(1)} %broadcast_in_dim.12), channel_id=1, replica_groups=mesh['grp'=2,'dom_0'=8,'dom_1'=8,'dom_2'=2,'dom_3'=2] {'dom_0'}, dimensions={0} | all-to-all | bytes 196608 | tf_op jit(solution)/shard_map/all_to_all | solution.py:64
  43.7 0.6 broadcast_in_dim.13
  44.4 6.8 %all-to-all-start.1 = ((f32[8,24,128]{2,1,0:T(8,128)}), f32[8,24,128]{2,1,0:T(8,128)S(1)}, u32[]{:S(2)}, u32[]{:S(2)}) async-start(f32[8,24,128]{2,1,0:T(8,128)} %broadcast_in_dim.13), calls=%async_computation.1 | async-start | bytes 196608 | tf_op jit(solution)/shard_map/all_to_all | solution.py:64
  51.2 3.1 %collective-permute-start.1 = (f32[24,64,128]{2,0,1:T(8,128)S(1)}, f32[24,64,128]{2,0,1:T(8,128)S(1)}, u32[]{:S(2)}, u32[]{:S(2)}) collective-permute-start(f32[24,64,128]{2,0,1:T(8,128)S(1)} %get-tuple-element.10), channel_id=1, source_target_pairs={{0,256},{256,0},{1,257},{257,1},{2,258},{258,2},{3,259},{259,3},{4... | collective-permute-start | bytes 2359304 | tf_op jit(solution)/shard_map/ppermute | solution.py:81
  54.3 4.5 %all-to-all-done.1 = f32[8,24,128]{2,1,0:T(8,128)S(1)} async-done(((f32[8,24,128]{2,1,0:T(8,128)}), f32[8,24,128]{2,1,0:T(8,128)S(1)}, u32[]{:S(2)}, u32[]{:S(2)}) %all-to-all-start.1) | async-done | bytes 98336 | tf_op jit(solution)/shard_map/all_to_all | solution.py:64
  58.8 16.5 %all_to_all.16.parts_ref = f32[8,24,128]{2,1,0:T(8,128)} all-to-all(f32[8,24,128]{2,1,0:T(8,128)S(1)} %broadcast_in_dim.28), channel_id=1, replica_groups=mesh['grp'=2,'dom_0'=8,'dom_1'=8,'dom_2'=2,'dom_3'=2] {'grp','dom_2','do..., dimensions={0} | all-to-all | bytes 196608 | tf_op jit(solution)/shard_map/all_to_all | solution.py:64
  75.3 5.6 %shard_map.41 = f32[1,128]{1,0:T(1,128)} custom-call(f32[8,24,128]{2,1,0:T(8,128)} %all_to_all.16.parts_ref), custom_call_target="tpu_custom_call" | custom-call | tf_op jit(solution)/shard_map/pallas_call | solution.py:44
  80.9 0.0 copy-start
  80.9 0.8 fusion.1
  81.8 0.3 multiply_reduce_fusion.3
  82.1 0.0 copy-done
  82.1 0.5 slice_bitcast_fusion
  82.6 0.0 collective-permute-done.1
  82.6 0.3 multiply_reduce_fusion.2
  82.9 0.3 broadcast_multiply_fusion
  83.2 1.6 %copy.11 = f32[24,64,256]{2,1,0:T(8,128)} copy(f32[24,64,256]{2,0,1:T(8,128)S(1)} %broadcast_multiply_fusion) | data formatting | bytes 3145728
  (12 shorter events, 0.1 us)
Async XLA Ops:
  4.0 16.3 %collective-permute-start = (f32[24,64,128]{2,0,1:T(8,128)S(1)}, f32[24,64,128]{2,0,1:T(8,128)S(1)}, u32[]{:S(2)}, u32[]{:S(2)}) collective-permute-start(f32[24,64,128]{2,0,1:T(8,128)S(1)} %get-tuple-element.11), channel_id=1, source_target_pairs={{0,256},{256,0},{1,257},{257,1},{2,258},{258,2},{3,259},{259,3},{4... | collective-permute-start | bytes 2359304 | tf_op jit(solution)/shard_map/ppermute | solution.py:80
  44.4 14.4 %all-to-all-start.1 = ((f32[8,24,128]{2,1,0:T(8,128)}), f32[8,24,128]{2,1,0:T(8,128)S(1)}, u32[]{:S(2)}, u32[]{:S(2)}) async-start(f32[8,24,128]{2,1,0:T(8,128)} %broadcast_in_dim.13), calls=%async_computation.1 | async-start | bytes 196608 | tf_op jit(solution)/shard_map/all_to_all | solution.py:64
  51.2 31.4 %collective-permute-start.1 = (f32[24,64,128]{2,0,1:T(8,128)S(1)}, f32[24,64,128]{2,0,1:T(8,128)S(1)}, u32[]{:S(2)}, u32[]{:S(2)}) collective-permute-start(f32[24,64,128]{2,0,1:T(8,128)S(1)} %get-tuple-element.10), channel_id=1, source_target_pairs={{0,256},{256,0},{1,257},{257,1},{2,258},{258,2},{3,259},{259,3},{4... | collective-permute-start | bytes 2359304 | tf_op jit(solution)/shard_map/ppermute | solution.py:81
  80.9 1.2 %copy-start = (f32[1,128]{1,0:T(1,128)S(1)}, f32[1,128]{1,0:T(1,128)}, u32[]{:S(2)}) copy-start(f32[1,128]{1,0:T(1,128)} %shard_map.41) | copy-start | bytes 1540

commit v3 on v2

v3 whole, which is shorter than its diff:
```python
import jax
import jax.numpy as jnp
from jax import lax
from jax.experimental import pallas as pl
from jax.experimental.pallas import tpu as pltpu
from jax.sharding import Mesh
from jax.sharding import PartitionSpec as P

DOM = ("dom_0", "dom_1", "dom_2", "dom_3")
STAGES = (("dom_0",), ("dom_1",), ("grp", "dom_2", "dom_3"))
SWAP = ((0, 1), (1, 0))
LANES = 128
SUBSPACES = 64
TILES = 8
HEAD = 8
ROOM = 592
ROWS = HEAD + ROOM + 8
VMEM = pl.BlockSpec(memory_space=pltpu.VMEM)
SMEM = pl.BlockSpec(memory_space=pltpu.SMEM)
ANY = pl.BlockSpec(memory_space=pl.ANY)


def positions(levels, i, start):
    l0, l1, l2 = (levels[d, i].astype(jnp.int32) for d in range(3))
    width = l2 + 1
    rows = []
    for a in range(4):
        for b in range(4):
            at = jnp.minimum(start + (a * (l1 + 1) + b) * width, HEAD + ROOM)
            rows.append(jnp.where((a <= l0) & (b <= l1), at, HEAD + ROOM))
    return rows, start + (l0 + 1) * (l1 + 1) * width


def owner_tiles(levels, i):
    l0, l1, l2 = (levels[d, i].astype(jnp.int32) for d in range(3))
    row = lax.broadcasted_iota(jnp.int32, (8, LANES), 0)
    fits = (row & 3) <= l2
    return [fits & (k % 2 * 2 + (row >> 2) <= l1) & (k // 2 <= l0) for k in range(TILES)]


def tile_rows(i, k):
    return pl.ds(pl.multiple_of(i * SUBSPACES + k * 8, 8), 8)


def packed_tile(packed_ref, rows, k):
    row = lax.broadcasted_iota(jnp.int32, (8, LANES), 0)
    upper = packed_ref[pl.ds(rows[2 * k], 8), :]
    lower = packed_ref[pl.ds(rows[2 * k + 1] - 4, 8), :]
    return jnp.where(row < 4, upper, lower)


def half_copies(surplus_ref, held, sems):
    side = lax.axis_index("grp")

    def copy(i, slot):
        lanes = pl.ds(pl.multiple_of((1 - side if slot else side) * LANES, LANES), LANES)
        rows = pl.ds(i * SUBSPACES, SUBSPACES)
        return pltpu.make_async_copy(surplus_ref.at[i, :, lanes], held.at[slot, rows, :], sems.at[slot, i])

    return copy


def held_scratch(grids):
    return [
        pltpu.VMEM((2, grids * SUBSPACES, LANES), jnp.float32),
        pltpu.SemaphoreType.DMA((2, grids)),
    ]


def pack_kernel(levels_ref, surplus_ref, far_ref, near_ref, held, sems):
    grids = surplus_ref.shape[0]
    copy = half_copies(surplus_ref, held, sems)
    for i in range(grids):
        copy(i, 0).start()
        copy(i, 1).start()
    head = jnp.zeros((HEAD, LANES), jnp.float32)
    row = lax.broadcasted_iota(jnp.int32, head.shape, 0)
    lane = lax.broadcasted_iota(jnp.int32, head.shape, 1)
    for d in range(3):
        for i in range(grids):
            head = jnp.where((row == d) & (lane == i), levels_ref[d, i].astype(jnp.float32), head)
    far_ref[0:HEAD, :] = head
    near_ref[0:HEAD, :] = head

    def pack(i, start):
        copy(i, 0).wait()
        copy(i, 1).wait()
        rows, stop = positions(levels_ref, i, start)
        for k in range(TILES):
            for slot, out in ((0, near_ref), (1, far_ref)):
                tile = held[slot, tile_rows(i, k), :]
                out[pl.ds(rows[2 * k], 4), :] = tile[0:4]
                out[pl.ds(rows[2 * k + 1], 4), :] = tile[4:8]
        return stop

    lax.fori_loop(0, grids, pack, jnp.int32(HEAD))


def pack(levels, surplus):
    packed = jax.ShapeDtypeStruct((ROWS, LANES), jnp.float32)
    return pl.pallas_call(
        pack_kernel,
        out_shape=(packed, packed),
        in_specs=[SMEM, ANY],
        out_specs=(VMEM, VMEM),
        scratch_shapes=held_scratch(surplus.shape[0]),
    )(levels, surplus)


def products(left_ref, right_ref, grids):
    def pair(ref, s):
        rows = [ref[pl.ds(s + k, grids, stride=SUBSPACES), :] for k in range(2)]
        return jnp.concatenate(rows, axis=1)

    total = jnp.zeros((grids, grids), jnp.float32)
    for s in range(0, SUBSPACES, 2):
        total = total + lax.dot_general(
            pair(left_ref, s),
            pair(right_ref, s),
            (((1,), (1,)), ((), ())),
            precision=lax.Precision.HIGHEST,
            preferred_element_type=jnp.float32,
        )
    return total


def own_kernel(levels_ref, surplus_ref, near_ref, block_ref, held, sems, far_ref):
    grids = surplus_ref.shape[0]
    copy = half_copies(surplus_ref, held, sems)
    for i in range(grids):
        copy(i, 0).start()
        copy(i, 1).start()

    def mask(i, carry):
        copy(i, 0).wait()
        copy(i, 1).wait()
        tiles = owner_tiles(levels_ref, i)
        for k in range(TILES):
            at = tile_rows(i, k)
            near_ref[at, :] = jnp.where(tiles[k], held[0, at, :], 0.0)
            far_ref[at, :] = jnp.where(tiles[k], held[1, at, :], 0.0)
        return carry

    lax.fori_loop(0, grids, mask, 0)
    block_ref[...] = products(near_ref, near_ref, grids) + products(far_ref, far_ref, grids)


def own_products(levels, surplus):
    grids = surplus.shape[0]
    half = (grids * SUBSPACES, LANES)
    return pl.pallas_call(
        own_kernel,
        out_shape=(
            jax.ShapeDtypeStruct(half, jnp.float32),
            jax.ShapeDtypeStruct((grids, grids), jnp.float32),
        ),
        in_specs=[SMEM, ANY],
        out_specs=(VMEM, VMEM),
        scratch_shapes=[*held_scratch(grids), pltpu.VMEM(half, jnp.float32)],
    )(levels, surplus)


def fold(block, cross, turned, second):
    zero = jnp.zeros_like(block)
    return jnp.concatenate(
        [
            jnp.where(second, zero, block),
            jnp.where(second, turned, cross),
            jnp.where(second, cross, turned),
            jnp.where(second, block, zero),
            jnp.zeros((block.shape[0], LANES - 4 * block.shape[0]), jnp.float32),
        ],
        axis=1,
    )


def cross_kernel(levels_ref, near_ref, block_ref, got_ref, parts_ref, full_ref, other_ref, head, sem):
    grids = block_ref.shape[0]
    fetch = pltpu.make_async_copy(got_ref.at[0:HEAD, :], head, sem)
    fetch.start()
    own = jnp.int32(HEAD)
    for i in range(grids):
        own = own + (levels_ref[0, i] + 1) * (levels_ref[1, i] + 1) * (levels_ref[2, i] + 1)
    fetch.wait()

    def unpack(i, start):
        rows, stop = positions(head, i, start)
        tiles = owner_tiles(head, i)
        for k in range(TILES):
            tile = packed_tile(got_ref, rows, k)
            other_ref[tile_rows(i, k), :] = jnp.where(tiles[k], tile, 0.0)
        return stop

    stop = lax.fori_loop(0, grids, unpack, jnp.int32(HEAD))
    full_ref[0] = (jnp.maximum(own, stop) > HEAD + ROOM).astype(jnp.int32)
    cross = products(near_ref, other_ref, grids)
    folded = fold(block_ref[...], cross, cross.T, lax.axis_index("grp") == 1)
    for k in range(parts_ref.shape[0]):
        parts_ref[k] = folded


def cross_products(levels, near, block, got, copies):
    grids = block.shape[0]
    return pl.pallas_call(
        cross_kernel,
        out_shape=(
            jax.ShapeDtypeStruct((copies, grids, LANES), jnp.float32),
            jax.ShapeDtypeStruct((1,), jnp.int32),
        ),
        in_specs=[SMEM, VMEM, VMEM, VMEM],
        out_specs=(VMEM, SMEM),
        scratch_shapes=[
            pltpu.VMEM((grids * SUBSPACES, LANES), jnp.float32),
            pltpu.SMEM((HEAD, LANES), jnp.float32),
            pltpu.SemaphoreType.DMA,
        ],
    )(levels, near, block, got)


def eliminate(parts_ref):
    number = 2 * parts_ref.shape[1]
    folded = parts_ref[0]
    for k in range(1, parts_ref.shape[0]):
        folded = folded + parts_ref[k]
    gram = jnp.concatenate([folded, pltpu.roll(folded, LANES - number, 1)], axis=0)
    rows = lax.broadcasted_iota(jnp.int32, gram.shape, 0)
    lanes = lax.broadcasted_iota(jnp.int32, gram.shape, 1)
    on_diagonal = rows == lanes
    diagonal = jnp.sum(jnp.where(on_diagonal, gram, 0.0), axis=1, keepdims=True) + 1e-06
    system = jnp.where(lanes < number, gram, 0.0) + jnp.where(on_diagonal, 0.1 * diagonal, 0.0)
    system = jnp.where(lanes == number, diagonal, system)
    for k in range(number):
        row = system[k : k + 1, :]
        column = jnp.broadcast_to(system[:, k : k + 1], system.shape)
        scaled = row * (1.0 / column[k : k + 1, :])
        system = system - jnp.where(rows == k, 0.0, column) * jnp.broadcast_to(scaled, system.shape)
    last = jnp.broadcast_to(system[:, number : number + 1], system.shape)
    solved = jnp.where(on_diagonal, last / system, 0.0)
    return jnp.broadcast_to(jnp.sum(solved, axis=1, keepdims=True), system.shape), on_diagonal


def solve_kernel(parts_ref, out_ref):
    solution_rows, on_diagonal = eliminate(parts_ref)
    out_ref[...] = jnp.sum(jnp.where(on_diagonal, solution_rows, 0.0), axis=0, keepdims=True)


def solve_parts(parts):
    return pl.pallas_call(
        solve_kernel,
        out_shape=jax.ShapeDtypeStruct((1, LANES), jnp.float32),
        in_specs=[VMEM],
        out_specs=VMEM,
    )(parts)


def finish_kernel(
    levels_ref,
    parts_ref,
    surplus_ref,
    got_near_ref,
    got_far_ref,
    updated_ref,
    out_ref,
    held,
    sems,
    head,
    head_sem,
    weights,
    result,
    out_sems,
):
    grids = surplus_ref.shape[0]
    side = lax.axis_index("grp")
    copy = half_copies(surplus_ref, held, sems)
    fetch = pltpu.make_async_copy(got_near_ref.at[0:HEAD, :], head, head_sem)
    fetch.start()
    for i in range(grids):
        copy(i, 0).start()
        copy(i, 1).start()
    solution_rows, on_diagonal = eliminate(parts_ref)
    out_ref[...] = jnp.sum(jnp.where(on_diagonal, solution_rows, 0.0), axis=0, keepdims=True)
    weights[...] = solution_rows
    fetch.wait()

    def add(i, carry):
        start, sums = carry
        copy(i, 0).wait()
        copy(i, 1).wait()
        rows, stop = positions(head, i, start)
        own_tiles = owner_tiles(levels_ref, i)
        other_tiles = owner_tiles(head, i)
        own = jnp.broadcast_to(weights[pl.ds(side * grids + i, 1), :], (8, LANES))
        other = jnp.broadcast_to(weights[pl.ds((1 - side) * grids + i, 1), :], (8, LANES))
        added = []
        for slot, got in ((0, got_near_ref), (1, got_far_ref)):
            for k in range(TILES):
                mine = jnp.where(own_tiles[k], held[slot, tile_rows(i, k), :], 0.0)
                theirs = jnp.where(other_tiles[k], packed_tile(got, rows, k), 0.0)
                added.append(sums[slot * TILES + k] + own * mine + other * theirs)
        return stop, tuple(added)

    zero = jnp.zeros((8, LANES), jnp.float32)
    _, sums = lax.fori_loop(0, grids, add, (jnp.int32(HEAD), (zero,) * (2 * TILES)))

    def put(i, slot):
        lanes = pl.ds(pl.multiple_of((1 - side if slot else side) * LANES, LANES), LANES)
        rows = pl.ds(i * SUBSPACES, SUBSPACES)
        return pltpu.make_async_copy(result.at[slot, rows, :], updated_ref.at[i, :, lanes], out_sems.at[slot, i])

    def spread(i, carry):
        tiles = owner_tiles(levels_ref, i)
        for slot in range(2):
            for k in range(TILES):
                result[slot, tile_rows(i, k), :] = jnp.where(tiles[k], sums[slot * TILES + k], 0.0)
            put(i, slot).start()
        return carry

    lax.fori_loop(0, grids, spread, 0)
    for i in range(grids):
        put(i, 0).wait()
        put(i, 1).wait()


def finish(levels, parts, surplus, got_near, got_far):
    grids = surplus.shape[0]
    return pl.pallas_call(
        finish_kernel,
        out_shape=(
            jax.ShapeDtypeStruct(surplus.shape, jnp.float32),
            jax.ShapeDtypeStruct((1, LANES), jnp.float32),
        ),
        in_specs=[SMEM, VMEM, ANY, VMEM, VMEM],
        out_specs=(ANY, VMEM),
        scratch_shapes=[
            *held_scratch(grids),
            pltpu.SMEM((HEAD, LANES), jnp.float32),
            pltpu.SemaphoreType.DMA,
            pltpu.VMEM((2 * grids, LANES), jnp.float32),
            *held_scratch(grids),
        ],
    )(levels, parts, surplus, got_near, got_far)


def owned(levels, count):
    indices = jnp.arange(count, dtype=jnp.int32)
    digits = jnp.stack([indices // 16, indices // 4 % 4, indices % 4])
    return jnp.all(digits[:, None] <= levels[:, :, None], axis=0).astype(jnp.float32)


def halves(levels, surplus):
    second = lax.axis_index("grp") == 1
    masked = surplus * owned(levels, SUBSPACES)[:, :, None]
    low, high = masked[:, :, :LANES], masked[:, :, LANES:]
    return jnp.where(second, high, low), jnp.where(second, low, high)


def dense_parts(levels, surplus, block, copies):
    near, far = halves(levels, surplus)
    cross = lax.dot_general(
        near,
        lax.ppermute(far, "grp", SWAP),
        (((1, 2), (1, 2)), ((), ())),
        precision=lax.Precision.HIGHEST,
        preferred_element_type=jnp.float32,
    )
    folded = fold(block, cross, cross.T, lax.axis_index("grp") == 1)
    return jnp.broadcast_to(folded, (copies, *folded.shape))


def dense_finish(levels, parts, surplus):
    grids = surplus.shape[0]
    second = lax.axis_index("grp") == 1
    near, far = halves(levels, surplus)
    got_near = lax.ppermute(far, "grp", SWAP)
    got_far = lax.ppermute(near, "grp", SWAP)
    coefficients = solve_parts(parts)
    start, stop = coefficients[0, :grids], coefficients[0, grids : 2 * grids]
    own = jnp.where(second, stop, start)[:, None, None]
    other = jnp.where(second, start, stop)[:, None, None]
    sum_near = jnp.sum(own * near + other * got_near, axis=0)
    sum_far = jnp.sum(own * far + other * got_far, axis=0)
    combined = jnp.concatenate(
        [jnp.where(second, sum_far, sum_near), jnp.where(second, sum_near, sum_far)], axis=1
    )
    return owned(levels, SUBSPACES)[:, :, None] * combined[None], coefficients


def exchanged(copies, axes):
    return lax.all_to_all(copies, axes, split_axis=0, concat_axis=0, tiled=True)


def shards(surplus, levels):
    grids = surplus.shape[0]
    levels = levels.T
    far, near = pack(levels, surplus)
    got_near = lax.ppermute(far, "grp", SWAP)
    got_far = lax.ppermute(near, "grp", SWAP)
    own, block = own_products(levels, surplus)
    parts, full = cross_products(levels, own, block, got_near, lax.axis_size(STAGES[0]))
    dense = full[0] > 0
    parts = lax.cond(
        dense, lambda: dense_parts(levels, surplus, block, parts.shape[0]), lambda: parts
    )
    for axes, following in zip(STAGES, STAGES[1:]):
        folded = jnp.sum(exchanged(parts, axes), axis=0)
        parts = jnp.broadcast_to(folded, (lax.axis_size(following), *folded.shape))
    parts = exchanged(parts, STAGES[-1])
    updated, coefficients = lax.cond(
        dense,
        lambda: dense_finish(levels, parts, surplus),
        lambda: tuple(finish(levels, parts, surplus, got_near, got_far)),
    )
    return updated, coefficients[0, : 2 * grids]


def solution(mesh):
    torus = Mesh(
        mesh.devices.reshape(mesh.shape["grp"], 8, 8, 2, 2),
        ("grp", *DOM),
    )
    return jax.shard_map(
        shards,
        mesh=torus,
        in_specs=(P("grp", None, DOM), P("grp", None)),
        out_specs=(P("grp", None, DOM), P()),
        check_vma=False,
    )
```

time: 85.3 us -> 77.2 us (0.905)
  Pallas kernels: 5.61 us -> 21.8 us
  blocking collectives: 38.8 us -> 27.4 us
  waiting for transfers between devices: 15.1 us -> 5.53 us
  starting transfers between devices: 13.9 us -> 20 us
  other arithmetic: 5.04 us -> 0.02 us
  matrix products: 2.6 us -> 0 us
  local copies, waits for them, and re-layouts: 3.05 us -> 0.54 us
    pallas_call x1 -> x4, Pallas kernels: 5.61 us -> 21.8 us  [the longest x1 9.01 us: finish(): pl.pallas_call(finish_kernel, out_shape=(jax.ShapeDtypeStruct(surplus.sha...]
    all_to_all x2, blocking collectives: 38.8 us -> 27.4 us  [exchanged(): return lax.all_to_all(copies, axes, split_axis=0, concat_axis=0, tiled=True)]
    ppermute x1, waiting for transfers between devices: 10.6 us -> 1 us  [shards(): got_near = lax.ppermute(far, 'grp', SWAP)]
    all_to_all x1, starting transfers between devices: 6.82 us -> 12.9 us  [exchanged(): return lax.all_to_all(copies, axes, split_axis=0, concat_axis=0, tiled=True)]
    mul x2 -> x0, other arithmetic: 2.63 us -> none  [the longest x1 2.35 us: shards(): masked = surplus * owners[:, :, None]]
    dot_general x2 -> x0, matrix products: 2.6 us -> none  [inner(): lax.dot_general(left, right, (((1, 2), (1, 2)), ((), ())), precision=lax....]
    unnamed x3 -> x6, local copies, waits for them, and re-layouts: 1.63 us -> 0.01 us
    select_n x6 -> x0, other arithmetic: 0.98 us -> none  [the longest x1 0.83 us: shards(): other = jnp.where(second, start, stop)]
  transfers between devices with their start and end apart: 3 -> 3, of which waited for: 2 -> 2; matrix products, arithmetic and copies ran while one was open for 4% -> 0% of each run, Pallas kernels for 7% -> 4%
where the time goes in v3:
time: 77.2 us; the launch traced here: 76.8 us
  blocking collectives  27.4 us (35%)
  Pallas kernels  21.8 us (28%)
  starting transfers between devices  20 us (26%)
  waiting for transfers between devices  5.53 us (7%)
  between operations  1.4 us (2%)
    all_to_all x2, blocking collectives, exchanged(): return lax.all_to_all(copies, axes, split_axis=0, concat_axis=0, tiled=True)  27.4 us
    all_to_all x1, starting transfers between devices, exchanged(): return lax.all_to_all(copies, axes, split_axis=0, concat_axis=0, tiled=True)  12.9 us
    pallas_call x1, Pallas kernels, finish(): pl.pallas_call(finish_kernel, out_shape=(jax.ShapeDtypeStruct(surplus.sha...  9.01 us
    pallas_call x1, Pallas kernels, cross_products(): pl.pallas_call(cross_kernel, out_shape=(jax.ShapeDtypeStruct((copies, gri...  5.32 us
    all_to_all x1, waiting for transfers between devices, exchanged(): return lax.all_to_all(copies, axes, split_axis=0, concat_axis=0, tiled=True)  4.53 us
    pallas_call x1, Pallas kernels, pack(): pl.pallas_call(pack_kernel, out_shape=(packed, packed), in_specs=[SMEM, A...  4.07 us
    ppermute x1, starting transfers between devices, shards(): got_near = lax.ppermute(far, 'grp', SWAP)  3.94 us
    pallas_call x1, Pallas kernels, own_products(): pl.pallas_call(own_kernel, out_shape=(jax.ShapeDtypeStruct(half, jnp.floa...  3.45 us
  transfers between devices with their start and end apart: 3, of which 2 were waited for; matrix products, arithmetic and copies ran while one was open for 0% of the time, Pallas kernels for 4%

profile of v3, /device:TPU:1, one launch (start us, length us, event | category | flops | bytes accessed | tf_op | source)
XLA Modules:
  0.0 76.8 jit_solution(11679853561844745966)
XLA Ops:
  0.6 0.0 copy-start
  0.6 0.0 copy-start.1
  0.6 4.1 %shard_map.42 = (f32[608,128]{1,0:T(8,128)}, f32[608,128]{1,0:T(8,128)}) custom-call(s32[3,24]{1,0:T(4,128)} %bitcast.14, f32[24,64,256]{2,1,0:T(8,128)} %surplus_ref.3), custom_call_target="tpu_custom_call" | custom-call | tf_op jit(solution)/shard_map/pallas_call | solution.py:101
  4.7 3.9 %collective-permute-start.3 = (f32[608,128]{1,0:T(8,128)}, f32[608,128]{1,0:T(8,128)S(1)}, u32[]{:S(2)}, u32[]{:S(2)}) collective-permute-start(f32[608,128]{1,0:T(8,128)} %get-tuple-element.52), channel_id=1, source_target_pairs={{0,256},{256,0},{1,257},{257,1},{2,258},{258,2},{3,259},{259,3},{4... | collective-permute-start | bytes 933896 | tf_op jit(solution)/shard_map/ppermute | solution.py:396
  8.7 0.0 copy-done
  8.7 0.0 copy-done.1
  8.7 3.5 %shard_map.41 = (f32[1536,128]{1,0:T(8,128)}, f32[24,24]{1,0:T(8,128)S(1)}) custom-call(s32[3,24]{1,0:T(4,128)S(1)} %bitcast.15, f32[24,64,256]{2,1,0:T(8,128)S(1)} %copy-done), custom_call_target="tpu_custom_call" | custom-call | tf_op jit(solution)/shard_map/pallas_call | solution.py:151
  12.1 1.0 %collective-permute-done.3.got_ref = f32[608,128]{1,0:T(8,128)S(1)} collective-permute-done((f32[608,128]{1,0:T(8,128)}, f32[608,128]{1,0:T(8,128)S(1)}, u32[]{:S(2)}, u32[]{:S(2)}) %collective-permute-start.3) | collective-permute-done | bytes 311328 | tf_op jit(solution)/shard_map/ppermute | solution.py:396
  13.2 5.3 %shard_map.43 = (f32[8,24,128]{2,1,0:T(8,128)}, s32[1]{0:T(128)}) custom-call(s32[3,24]{1,0:T(4,128)S(1)} %bitcast.16, f32[1536,128]{1,0:T(8,128)} %get-tuple-element.50.near_ref, f32[24,24]{1,0:T(8,128)S(1)} %get-tuple-element.51.block_ref, f32[608,128]{1,0:T(8,128)S(1)} %collective-permute-done.3.got_ref), custom_call_target="tpu_custom_call" | custom-call | tf_op jit(solution)/shard_map/pallas_call | solution.py:204
  19.1 0.0 copy-start.4
  19.2 12.9 %all-to-all-start = ((f32[8,24,128]{2,1,0:T(8,128)}), f32[8,24,128]{2,1,0:T(8,128)S(1)}, u32[]{:S(2)}, u32[]{:S(2)}) async-start(f32[8,24,128]{2,1,0:T(8,128)} %get-tuple-element.84), calls=%async_computation | async-start | bytes 196608 | tf_op jit(solution)/shard_map/all_to_all | solution.py:389
  32.1 0.0 copy-done.4
  32.1 3.1 %collective-permute-start.4 = (f32[608,128]{1,0:T(8,128)S(1)}, f32[608,128]{1,0:T(8,128)S(1)}, u32[]{:S(2)}, u32[]{:S(2)}) collective-permute-start(f32[608,128]{1,0:T(8,128)S(1)} %copy-done.4), channel_id=1, source_target_pairs={{0,256},{256,0},{1,257},{257,1},{2,258},{258,2},{3,259},{259,3},{4... | collective-permute-start | bytes 933896 | tf_op jit(solution)/shard_map/ppermute | solution.py:397
  35.2 4.5 %all-to-all-done = f32[8,24,128]{2,1,0:T(8,128)S(1)} async-done(((f32[8,24,128]{2,1,0:T(8,128)}), f32[8,24,128]{2,1,0:T(8,128)S(1)}, u32[]{:S(2)}, u32[]{:S(2)}) %all-to-all-start) | async-done | bytes 98336 | tf_op jit(solution)/shard_map/all_to_all | solution.py:389
  39.8 14.2 %all_to_all.15 = f32[8,24,128]{2,1,0:T(8,128)S(1)} all-to-all(f32[8,24,128]{2,1,0:T(8,128)S(1)} %broadcast_in_dim.10), channel_id=1, replica_groups=mesh['grp'=2,'dom_0'=8,'dom_1'=8,'dom_2'=2,'dom_3'=2] {'dom_1'}, dimensions={0} | all-to-all | bytes 196608 | tf_op jit(solution)/shard_map/all_to_all | solution.py:389
  54.0 13.2 %all_to_all.16 = f32[8,24,128]{2,1,0:T(8,128)S(1)} all-to-all(f32[8,24,128]{2,1,0:T(8,128)S(1)} %broadcast_in_dim.11), channel_id=1, replica_groups=mesh['grp'=2,'dom_0'=8,'dom_1'=8,'dom_2'=2,'dom_3'=2] {'grp','dom_2','do..., dimensions={0} | all-to-all | bytes 196608 | tf_op jit(solution)/shard_map/all_to_all | solution.py:389
  67.2 0.0 collective-permute-done.4
  67.2 9.0 %conditional.3 = ((f32[24,64,256]{2,1,0:T(8,128)}, f32[1,128]{1,0:T(1,128)S(1)})) conditional(s32[]{:T(128)} %bitcast.5, (s32[3,24]{1,0:T(4,128)S(1)}, f32[8,24,128]{2,1,0:T(8,128)S(1)}, f32[24,64,256]{2,1,0:T(8,128)S(1)}, f32[608,128]{1,0:T(8,128)S(1)}, f32[608,128]{1,0:T(8,128)S(1)}) %tuple.49, (s32[3,24]{1,0:T(4,128)S(1)}, ...), branch_computations={%region_5.6_spmd, %region_6.10_spmd} | conditional | flops 2780532 | bytes 17724460 | solution.py:408
  67.2 9.0 %branch_0_fun.1 = (f32[24,64,256]{2,1,0:T(8,128)}, f32[1,128]{1,0:T(1,128)S(1)}) custom-call(s32[3,24]{1,0:T(4,128)S(1)} %get-tuple-element.32.levels_ref, f32[8,24,128]{2,1,0:T(8,128)S(1)} %get-tuple-element.33.parts_ref, f32[24,64,256]{2,1,0:T(8,128)S(1)} %get-tuple-element.34.surplus_ref, f32[608,128]{1,0:T(8,128)S(1)} %get-tuple-element.35.got_near_ref, ...), custom_call_target="tpu_custom_call" | custom-call | tf_op jit(solution)/shard_map/cond/branch_0_fun/pallas_call | solution.py:326
  76.3 0.5 slice_bitcast_fusion
  (5 shorter events, 0.0 us)
Async XLA Ops:
  0.6 8.0 %copy-start = (f32[24,64,256]{2,1,0:T(8,128)S(1)}, f32[24,64,256]{2,1,0:T(8,128)}, u32[]{:S(2)}) copy-start(f32[24,64,256]{2,1,0:T(8,128)} %surplus_ref.3) | copy-start | bytes 4718596
  0.6 8.0 %copy-start.1 = (s32[24,3]{0,1:T(4,128)S(1)}, s32[24,3]{0,1:T(4,128)}, u32[]{:S(2)}) copy-start(s32[24,3]{0,1:T(4,128)} %param.7) | copy-start | bytes 868
  4.7 8.4 %collective-permute-start.3 = (f32[608,128]{1,0:T(8,128)}, f32[608,128]{1,0:T(8,128)S(1)}, u32[]{:S(2)}, u32[]{:S(2)}) collective-permute-start(f32[608,128]{1,0:T(8,128)} %get-tuple-element.52), channel_id=1, source_target_pairs={{0,256},{256,0},{1,257},{257,1},{2,258},{258,2},{3,259},{259,3},{4... | collective-permute-start | bytes 933896 | tf_op jit(solution)/shard_map/ppermute | solution.py:396
  19.1 12.9 %copy-start.4 = (f32[608,128]{1,0:T(8,128)S(1)}, f32[608,128]{1,0:T(8,128)}, u32[]{:S(2)}) copy-start(f32[608,128]{1,0:T(8,128)} %get-tuple-element.55) | copy-start | bytes 933892
  19.2 20.6 %all-to-all-start = ((f32[8,24,128]{2,1,0:T(8,128)}), f32[8,24,128]{2,1,0:T(8,128)S(1)}, u32[]{:S(2)}, u32[]{:S(2)}) async-start(f32[8,24,128]{2,1,0:T(8,128)} %get-tuple-element.84), calls=%async_computation | async-start | bytes 196608 | tf_op jit(solution)/shard_map/all_to_all | solution.py:389
  32.1 35.2 %collective-permute-start.4 = (f32[608,128]{1,0:T(8,128)S(1)}, f32[608,128]{1,0:T(8,128)S(1)}, u32[]{:S(2)}, u32[]{:S(2)}) collective-permute-start(f32[608,128]{1,0:T(8,128)S(1)} %copy-done.4), channel_id=1, source_target_pairs={{0,256},{256,0},{1,257},{257,1},{2,258},{258,2},{3,259},{259,3},{4... | collective-permute-start | bytes 933896 | tf_op jit(solution)/shard_map/ppermute | solution.py:397

commit v4 on v3

--- a/solution.py
+++ b/solution.py
@@ -6,8 +6,8 @@
 from jax.sharding import Mesh
 from jax.sharding import PartitionSpec as P
 
-DOM = ("dom_0", "dom_1", "dom_2", "dom_3")
-STAGES = (("dom_0",), ("dom_1",), ("grp", "dom_2", "dom_3"))
+DOM = ("z_hi", "z_lo", "y_hi", "y_lo", "x_hi", "core")
+STAGES = (("z_hi", "y_hi"), ("grp", "x_hi", "core", "z_lo", "y_lo"))
 SWAP = ((0, 1), (1, 0))
 LANES = 128
 SUBSPACES = 64
@@ -49,96 +49,112 @@
     return jnp.where(row < 4, upper, lower)
 
 
-def half_copies(surplus_ref, held, sems):
+def half_lanes(slot):
     side = lax.axis_index("grp")
-
-    def copy(i, slot):
-        lanes = pl.ds(pl.multiple_of((1 - side if slot else side) * LANES, LANES), LANES)
+    return pl.ds(pl.multiple_of((1 - side if slot else side) * LANES, LANES), LANES)
+
+
+def cell_tile(surplus_ref, i, k, slot):
+    return surplus_ref[i, k * 8 : k * 8 + 8, half_lanes(slot)]
+
+
+def store_packed(out_ref, rows, k, tile):
+    out_ref[pl.ds(rows[2 * k], 4), :] = tile[0:4]
+    out_ref[pl.ds(rows[2 * k + 1], 4), :] = tile[4:8]
+
+
+def pack_far_kernel(levels_ref, surplus_ref, out_ref, held, sems):
+    grids = surplus_ref.shape[0]
+
+    def copy(i):
         rows = pl.ds(i * SUBSPACES, SUBSPACES)
-        return pltpu.make_async_copy(surplus_ref.at[i, :, lanes], held.at[slot, rows, :], sems.at[slot, i])
-
-    return copy
-
-
-def held_scratch(grids):
-    return [
-        pltpu.VMEM((2, grids * SUBSPACES, LANES), jnp.float32),
-        pltpu.SemaphoreType.DMA((2, grids)),
-    ]
-
-
-def pack_kernel(levels_ref, surplus_ref, far_ref, near_ref, held, sems):
-    grids = surplus_ref.shape[0]
-    copy = half_copies(surplus_ref, held, sems)
+        return pltpu.make_async_copy(surplus_ref.at[i, :, half_lanes(1)], held.at[rows, :], sems.at[i])
+
     for i in range(grids):
-        copy(i, 0).start()
-        copy(i, 1).start()
+        copy(i).start()
     head = jnp.zeros((HEAD, LANES), jnp.float32)
     row = lax.broadcasted_iota(jnp.int32, head.shape, 0)
     lane = lax.broadcasted_iota(jnp.int32, head.shape, 1)
     for d in range(3):
         for i in range(grids):
             head = jnp.where((row == d) & (lane == i), levels_ref[d, i].astype(jnp.float32), head)
-    far_ref[0:HEAD, :] = head
-    near_ref[0:HEAD, :] = head
+    out_ref[0:HEAD, :] = head
 
     def pack(i, start):
-        copy(i, 0).wait()
-        copy(i, 1).wait()
+        copy(i).wait()
         rows, stop = positions(levels_ref, i, start)
         for k in range(TILES):
-            for slot, out in ((0, near_ref), (1, far_ref)):
-                tile = held[slot, tile_rows(i, k), :]
-                out[pl.ds(rows[2 * k], 4), :] = tile[0:4]
-                out[pl.ds(rows[2 * k + 1], 4), :] = tile[4:8]
+            store_packed(out_ref, rows, k, held[tile_rows(i, k), :])
         return stop
 
     lax.fori_loop(0, grids, pack, jnp.int32(HEAD))
 
 
-def pack(levels, surplus):
-    packed = jax.ShapeDtypeStruct((ROWS, LANES), jnp.float32)
-    return pl.pallas_call(
-        pack_kernel,
-        out_shape=(packed, packed),
+def pack_far(levels, surplus):
+    grids = surplus.shape[0]
+    return pl.pallas_call(
+        pack_far_kernel,
+        out_shape=jax.ShapeDtypeStruct((ROWS, LANES), jnp.float32),
         in_specs=[SMEM, ANY],
-        out_specs=(VMEM, VMEM),
-        scratch_shapes=held_scratch(surplus.shape[0]),
+        out_specs=VMEM,
+        scratch_shapes=[
+            pltpu.VMEM((grids * SUBSPACES, LANES), jnp.float32),
+            pltpu.SemaphoreType.DMA((grids,)),
+        ],
     )(levels, surplus)
 
 
+def pack_near_kernel(levels_ref, surplus_ref, out_ref):
+    grids = surplus_ref.shape[0]
+    out_ref[0:HEAD, :] = jnp.zeros((HEAD, LANES), jnp.float32)
+
+    def pack(i, start):
+        rows, stop = positions(levels_ref, i, start)
+        for k in range(TILES):
+            store_packed(out_ref, rows, k, cell_tile(surplus_ref, i, k, 0))
+        return stop
+
+    lax.fori_loop(0, grids, pack, jnp.int32(HEAD))
+
+
+def pack_near(levels, surplus):
+    return pl.pallas_call(
+        pack_near_kernel,
+        out_shape=jax.ShapeDtypeStruct((ROWS, LANES), jnp.float32),
+        in_specs=[SMEM, VMEM],
+        out_specs=VMEM,
+    )(levels, surplus)
+
+
 def products(left_ref, right_ref, grids):
-    def pair(ref, s):
-        rows = [ref[pl.ds(s + k, grids, stride=SUBSPACES), :] for k in range(2)]
-        return jnp.concatenate(rows, axis=1)
+    def split(ref, s):
+        rows = [ref[pl.ds(s + k, grids, stride=SUBSPACES), :] for k in range(8)]
+        rows = jnp.concatenate(rows, axis=1)
+        high = rows.astype(jnp.bfloat16)
+        return high, (rows - high.astype(jnp.float32)).astype(jnp.bfloat16)
 
     total = jnp.zeros((grids, grids), jnp.float32)
-    for s in range(0, SUBSPACES, 2):
+    for s in range(0, SUBSPACES, 8):
+        left_high, left_low = split(left_ref, s)
+        right_high, right_low = (left_high, left_low) if left_ref is right_ref else split(right_ref, s)
         total = total + lax.dot_general(
-            pair(left_ref, s),
-            pair(right_ref, s),
+            jnp.concatenate([left_high, left_high, left_low], axis=1),
+            jnp.concatenate([right_high, right_low, right_high], axis=1),
             (((1,), (1,)), ((), ())),
-            precision=lax.Precision.HIGHEST,
             preferred_element_type=jnp.float32,
         )
     return total
 
 
-def own_kernel(levels_ref, surplus_ref, near_ref, block_ref, held, sems, far_ref):
+def own_kernel(levels_ref, surplus_ref, near_ref, block_ref, far_ref):
     grids = surplus_ref.shape[0]
-    copy = half_copies(surplus_ref, held, sems)
-    for i in range(grids):
-        copy(i, 0).start()
-        copy(i, 1).start()
 
     def mask(i, carry):
-        copy(i, 0).wait()
-        copy(i, 1).wait()
         tiles = owner_tiles(levels_ref, i)
         for k in range(TILES):
             at = tile_rows(i, k)
-            near_ref[at, :] = jnp.where(tiles[k], held[0, at, :], 0.0)
-            far_ref[at, :] = jnp.where(tiles[k], held[1, at, :], 0.0)
+            near_ref[at, :] = jnp.where(tiles[k], cell_tile(surplus_ref, i, k, 0), 0.0)
+            far_ref[at, :] = jnp.where(tiles[k], cell_tile(surplus_ref, i, k, 1), 0.0)
         return carry
 
     lax.fori_loop(0, grids, mask, 0)
@@ -154,9 +170,9 @@
             jax.ShapeDtypeStruct(half, jnp.float32),
             jax.ShapeDtypeStruct((grids, grids), jnp.float32),
         ),
-        in_specs=[SMEM, ANY],
+        in_specs=[SMEM, VMEM],
         out_specs=(VMEM, VMEM),
-        scratch_shapes=[*held_scratch(grids), pltpu.VMEM(half, jnp.float32)],
+        scratch_shapes=[pltpu.VMEM(half, jnp.float32)],
     )(levels, surplus)
 
 
@@ -241,13 +257,13 @@
 
 def solve_kernel(parts_ref, out_ref):
     solution_rows, on_diagonal = eliminate(parts_ref)
-    out_ref[...] = jnp.sum(jnp.where(on_diagonal, solution_rows, 0.0), axis=0, keepdims=True)
+    out_ref[...] = jnp.sum(jnp.where(on_diagonal, solution_rows, 0.0), axis=0, keepdims=True)[:, : out_ref.shape[1]]
 
 
 def solve_parts(parts):
     return pl.pallas_call(
         solve_kernel,
-        out_shape=jax.ShapeDtypeStruct((1, LANES), jnp.float32),
+        out_shape=jax.ShapeDtypeStruct((1, 2 * parts.shape[1]), jnp.float32),
         in_specs=[VMEM],
         out_specs=VMEM,
     )(parts)
@@ -261,8 +277,6 @@
     got_far_ref,
     updated_ref,
     out_ref,
-    held,
-    sems,
     head,
     head_sem,
     weights,
@@ -271,21 +285,15 @@
 ):
     grids = surplus_ref.shape[0]
     side = lax.axis_index("grp")
-    copy = half_copies(surplus_ref, held, sems)
     fetch = pltpu.make_async_copy(got_near_ref.at[0:HEAD, :], head, head_sem)
     fetch.start()
-    for i in range(grids):
-        copy(i, 0).start()
-        copy(i, 1).start()
     solution_rows, on_diagonal = eliminate(parts_ref)
-    out_ref[...] = jnp.sum(jnp.where(on_diagonal, solution_rows, 0.0), axis=0, keepdims=True)
+    out_ref[...] = jnp.sum(jnp.where(on_diagonal, solution_rows, 0.0), axis=0, keepdims=True)[:, : out_ref.shape[1]]
     weights[...] = solution_rows
     fetch.wait()
 
     def add(i, carry):
         start, sums = carry
-        copy(i, 0).wait()
-        copy(i, 1).wait()
         rows, stop = positions(head, i, start)
         own_tiles = owner_tiles(levels_ref, i)
         other_tiles = owner_tiles(head, i)
@@ -294,7 +302,7 @@
         added = []
         for slot, got in ((0, got_near_ref), (1, got_far_ref)):
             for k in range(TILES):
-                mine = jnp.where(own_tiles[k], held[slot, tile_rows(i, k), :], 0.0)
+                mine = jnp.where(own_tiles[k], cell_tile(surplus_ref, i, k, slot), 0.0)
                 theirs = jnp.where(other_tiles[k], packed_tile(got, rows, k), 0.0)
                 added.append(sums[slot * TILES + k] + own * mine + other * theirs)
         return stop, tuple(added)
@@ -303,9 +311,8 @@
     _, sums = lax.fori_loop(0, grids, add, (jnp.int32(HEAD), (zero,) * (2 * TILES)))
 
     def put(i, slot):
-        lanes = pl.ds(pl.multiple_of((1 - side if slot else side) * LANES, LANES), LANES)
         rows = pl.ds(i * SUBSPACES, SUBSPACES)
-        return pltpu.make_async_copy(result.at[slot, rows, :], updated_ref.at[i, :, lanes], out_sems.at[slot, i])
+        return pltpu.make_async_copy(result.at[slot, rows, :], updated_ref.at[i, :, half_lanes(slot)], out_sems.at[slot, i])
 
     def spread(i, carry):
         tiles = owner_tiles(levels_ref, i)
@@ -327,16 +334,16 @@
         finish_kernel,
         out_shape=(
             jax.ShapeDtypeStruct(surplus.shape, jnp.float32),
-            jax.ShapeDtypeStruct((1, LANES), jnp.float32),
+            jax.ShapeDtypeStruct((1, 2 * grids), jnp.float32),
         ),
-        in_specs=[SMEM, VMEM, ANY, VMEM, VMEM],
+        in_specs=[SMEM, VMEM, VMEM, VMEM, VMEM],
         out_specs=(ANY, VMEM),
         scratch_shapes=[
-            *held_scratch(grids),
             pltpu.SMEM((HEAD, LANES), jnp.float32),
             pltpu.SemaphoreType.DMA,
             pltpu.VMEM((2 * grids, LANES), jnp.float32),
-            *held_scratch(grids),
+            pltpu.VMEM((2, grids * SUBSPACES, LANES), jnp.float32),
+            pltpu.SemaphoreType.DMA((2, grids)),
         ],
     )(levels, parts, surplus, got_near, got_far)
 
@@ -389,11 +396,11 @@
     return lax.all_to_all(copies, axes, split_axis=0, concat_axis=0, tiled=True)
 
 
-def shards(surplus, levels):
-    grids = surplus.shape[0]
+def whole(surplus, levels):
     levels = levels.T
-    far, near = pack(levels, surplus)
+    far = pack_far(levels, surplus)
     got_near = lax.ppermute(far, "grp", SWAP)
+    near = pack_near(levels, surplus)
     got_far = lax.ppermute(near, "grp", SWAP)
     own, block = own_products(levels, surplus)
     parts, full = cross_products(levels, own, block, got_near, lax.axis_size(STAGES[0]))
@@ -410,16 +417,16 @@
         lambda: dense_finish(levels, parts, surplus),
         lambda: tuple(finish(levels, parts, surplus, got_near, got_far)),
     )
-    return updated, coefficients[0, : 2 * grids]
+    return updated, coefficients.reshape(-1)
 
 
 def solution(mesh):
     torus = Mesh(
-        mesh.devices.reshape(mesh.shape["grp"], 8, 8, 2, 2),
+        mesh.devices.reshape(mesh.shape["grp"], 4, 2, 4, 2, 2, 2),
         ("grp", *DOM),
     )
     return jax.shard_map(
-        shards,
+        whole,
         mesh=torus,
         in_specs=(P("grp", None, DOM), P("grp", None)),
         out_specs=(P("grp", None, DOM), P()),

time: 77.2 us -> 79.9 us (1.035)
  waiting for transfers between devices: 5.53 us -> 10.1 us
  starting transfers between devices: 20 us -> 15.8 us
  blocking collectives: 27.4 us -> 29.5 us
    ppermute x2, waiting for transfers between devices: 1 us -> 6.84 us  [the longest x1 4.77 us: whole(): got_far = lax.ppermute(near, 'grp', SWAP)]
    all_to_all x1, starting transfers between devices: 12.9 us -> 8.59 us  [exchanged(): return lax.all_to_all(copies, axes, split_axis=0, concat_axis=0, tiled=True)]
    pallas_call x1 -> x2, Pallas kernels: 4.07 us -> 6.2 us  [the longest x1 3.69 us: pack_far(): pl.pallas_call(pack_far_kernel, out_shape=jax.ShapeDtypeStruct((ROWS, LAN...]
    all_to_all x2 -> x1, blocking collectives: 27.4 us -> 29.5 us  [exchanged(): return lax.all_to_all(copies, axes, split_axis=0, concat_axis=0, tiled=True)]
    all_to_all x1, waiting for transfers between devices: 4.53 us -> 3.29 us  [exchanged(): return lax.all_to_all(copies, axes, split_axis=0, concat_axis=0, tiled=True)]
    pallas_call x1, Pallas kernels: 3.45 us -> 2.38 us  [own_products(): pl.pallas_call(own_kernel, out_shape=(jax.ShapeDtypeStruct(half, jnp.floa...]
    pallas_call x1, Pallas kernels: 5.32 us -> 4.49 us  [cross_products(): pl.pallas_call(cross_kernel, out_shape=(jax.ShapeDtypeStruct((copies, gri...]
  transfers between devices with their start and end apart: 3 -> 3, of which waited for: 2 -> 3; matrix products, arithmetic and copies ran while one was open for 0% -> 0% of each run, Pallas kernels for 4% -> 6%
where the time goes in v4:
time: 79.9 us; the launch traced here: 79.6 us
  blocking collectives  29.5 us (37%)
  Pallas kernels  22 us (28%)
  starting transfers between devices  15.8 us (20%)
  waiting for transfers between devices  10.1 us (13%)
  between operations  1.37 us (2%)
    all_to_all x1, blocking collectives, exchanged(): return lax.all_to_all(copies, axes, split_axis=0, concat_axis=0, tiled=True)  29.5 us
    pallas_call x1, Pallas kernels, finish(): pl.pallas_call(finish_kernel, out_shape=(jax.ShapeDtypeStruct(surplus.sha...  8.9 us
    all_to_all x1, starting transfers between devices, exchanged(): return lax.all_to_all(copies, axes, split_axis=0, concat_axis=0, tiled=True)  8.59 us
    ppermute x1, waiting for transfers between devices, whole(): got_far = lax.ppermute(near, 'grp', SWAP)  4.77 us
    pallas_call x1, Pallas kernels, cross_products(): pl.pallas_call(cross_kernel, out_shape=(jax.ShapeDtypeStruct((copies, gri...  4.49 us
    ppermute x1, starting transfers between devices, whole(): got_near = lax.ppermute(far, 'grp', SWAP)  3.94 us
    pallas_call x1, Pallas kernels, pack_far(): pl.pallas_call(pack_far_kernel, out_shape=jax.ShapeDtypeStruct((ROWS, LAN...  3.69 us
    all_to_all x1, waiting for transfers between devices, exchanged(): return lax.all_to_all(copies, axes, split_axis=0, concat_axis=0, tiled=True)  3.29 us
  transfers between devices with their start and end apart: 3, of which 3 were waited for; matrix products, arithmetic and copies ran while one was open for 0% of the time, Pallas kernels for 6%

profile of v4, /device:TPU:1, one launch (start us, length us, event | category | flops | bytes accessed | tf_op | source)
XLA Modules:
  0.0 79.6 jit_solution(16119050256307787839)
XLA Ops:
  0.6 0.0 copy-start
  0.6 0.0 copy-start.1
  0.6 3.7 %shard_map.42 = f32[608,128]{1,0:T(8,128)} custom-call(s32[3,24]{1,0:T(4,128)} %bitcast.13, f32[24,64,256]{2,1,0:T(8,128)} %surplus_ref.5), custom_call_target="tpu_custom_call" | custom-call | tf_op jit(solution)/shard_map/pallas_call | solution.py:95
  4.3 3.9 %collective-permute-start.3 = (f32[608,128]{1,0:T(8,128)}, f32[608,128]{1,0:T(8,128)S(1)}, u32[]{:S(2)}, u32[]{:S(2)}) collective-permute-start(f32[608,128]{1,0:T(8,128)} %shard_map.42), channel_id=1, source_target_pairs={{0,256},{256,0},{1,257},{257,1},{2,258},{258,2},{3,259},{259,3},{4... | collective-permute-start | bytes 933896 | tf_op jit(solution)/shard_map/ppermute | solution.py:402
  8.3 0.0 copy-done
  8.3 0.0 copy-done.1
  8.3 2.4 %shard_map.41 = (f32[1536,128]{1,0:T(8,128)}, f32[24,24]{1,0:T(8,128)S(1)}) custom-call(s32[3,24]{1,0:T(4,128)S(1)} %bitcast.14, f32[24,64,256]{2,1,0:T(8,128)S(1)} %copy-done), custom_call_target="tpu_custom_call" | custom-call | tf_op jit(solution)/shard_map/pallas_call | solution.py:167
  10.7 2.1 %collective-permute-done.3.got_ref = f32[608,128]{1,0:T(8,128)S(1)} collective-permute-done((f32[608,128]{1,0:T(8,128)}, f32[608,128]{1,0:T(8,128)S(1)}, u32[]{:S(2)}, u32[]{:S(2)}) %collective-permute-start.3) | collective-permute-done | bytes 311328 | tf_op jit(solution)/shard_map/ppermute | solution.py:402
  12.8 4.5 %shard_map.43 = (f32[16,24,128]{2,1,0:T(8,128)S(1)}, s32[1]{0:T(128)}) custom-call(s32[3,24]{1,0:T(4,128)S(1)} %bitcast.15, f32[1536,128]{1,0:T(8,128)} %get-tuple-element.48.near_ref, f32[24,24]{1,0:T(8,128)S(1)} %get-tuple-element.49.block_ref, f32[608,128]{1,0:T(8,128)S(1)} %collective-permute-done.3.got_ref), custom_call_target="tpu_custom_call" | custom-call | tf_op jit(solution)/shard_map/pallas_call | solution.py:220
  17.9 29.5 %all_to_all.10 = f32[16,24,128]{2,1,0:T(8,128)S(1)} all-to-all(f32[16,24,128]{2,1,0:T(8,128)S(1)} %get-tuple-element.80), channel_id=1, replica_groups=mesh['grp'=2,'z_hi'=4,'z_lo'=2,'y_hi'=4,'y_lo'=2,'x_hi'=2,'core'=2] {'z_..., dimensions={0} | all-to-all | bytes 393216 | tf_op jit(solution)/shard_map/all_to_all | solution.py:396
  47.4 0.8 broadcast_in_dim.8
  48.2 8.6 %all-to-all-start.1 = ((f32[32,24,128]{2,1,0:T(8,128)}), f32[32,24,128]{2,1,0:T(8,128)S(1)}, u32[]{:S(2)}, u32[]{:S(2)}) async-start(f32[32,24,128]{2,1,0:T(8,128)} %broadcast_in_dim.8), calls=%async_computation.1 | async-start | bytes 786432 | tf_op jit(solution)/shard_map/all_to_all | solution.py:396
  56.8 2.5 %shard_map.44 = f32[608,128]{1,0:T(8,128)} custom-call(s32[3,24]{1,0:T(4,128)S(1)} %bitcast.17, f32[24,64,256]{2,1,0:T(8,128)S(1)} %copy-done), custom_call_target="tpu_custom_call" | custom-call | tf_op jit(solution)/shard_map/pallas_call | solution.py:121
  59.3 3.3 %collective-permute-start.4 = (f32[608,128]{1,0:T(8,128)}, f32[608,128]{1,0:T(8,128)S(1)}, u32[]{:S(2)}, u32[]{:S(2)}) collective-permute-start(f32[608,128]{1,0:T(8,128)} %shard_map.44), channel_id=1, source_target_pairs={{0,256},{256,0},{1,257},{257,1},{2,258},{258,2},{3,259},{259,3},{4... | collective-permute-start | bytes 933896 | tf_op jit(solution)/shard_map/ppermute | solution.py:404
  62.6 3.3 %all-to-all-done.1 = f32[32,24,128]{2,1,0:T(8,128)S(1)} async-done(((f32[32,24,128]{2,1,0:T(8,128)}), f32[32,24,128]{2,1,0:T(8,128)S(1)}, u32[]{:S(2)}, u32[]{:S(2)}) %all-to-all-start.1) | async-done | bytes 393248 | tf_op jit(solution)/shard_map/all_to_all | solution.py:396
  65.9 4.8 %collective-permute-done.4 = f32[608,128]{1,0:T(8,128)S(1)} collective-permute-done((f32[608,128]{1,0:T(8,128)}, f32[608,128]{1,0:T(8,128)S(1)}, u32[]{:S(2)}, u32[]{:S(2)}) %collective-permute-start.4) | collective-permute-done | bytes 311328 | tf_op jit(solution)/shard_map/ppermute | solution.py:404
  70.7 8.9 %conditional.3 = ((f32[24,64,256]{2,1,0:T(8,128)}, f32[1,48]{1,0:T(1,128)})) conditional(s32[]{:T(128)} %bitcast.5, (s32[3,24]{1,0:T(4,128)S(1)}, f32[32,24,128]{2,1,0:T(8,128)S(1)}, f32[24,64,256]{2,1,0:T(8,128)S(1)}, f32[608,128]{1,0:T(8,128)S(1)}, f32[608,128]{1,0:T(8,128)S(1)}) %tuple.49, (s32[3,24]{1,0:T(4,128)S(1)}, ...), branch_computations={%region_4.5_spmd, %region_5.9_spmd} | conditional | flops 2780532 | bytes 17721104 | solution.py:415
  70.7 8.9 %branch_0_fun.1 = (f32[24,64,256]{2,1,0:T(8,128)}, f32[1,48]{1,0:T(1,128)}) custom-call(s32[3,24]{1,0:T(4,128)S(1)} %get-tuple-element.32.levels_ref, f32[32,24,128]{2,1,0:T(8,128)S(1)} %get-tuple-element.33.parts_ref, f32[24,64,256]{2,1,0:T(8,128)S(1)} %get-tuple-element.34.surplus_ref, f32[608,128]{1,0:T(8,128)S(1)} %get-tuple-element.35.got_near_ref, ...), custom_call_target="tpu_custom_call" | custom-call | tf_op jit(solution)/shard_map/cond/branch_0_fun/pallas_call | solution.py:333
  (2 shorter events, 0.0 us)
Async XLA Ops:
  0.6 7.7 %copy-start = (f32[24,64,256]{2,1,0:T(8,128)S(1)}, f32[24,64,256]{2,1,0:T(8,128)}, u32[]{:S(2)}) copy-start(f32[24,64,256]{2,1,0:T(8,128)} %surplus_ref.5) | copy-start | bytes 4718596
  0.6 7.7 %copy-start.1 = (s32[24,3]{0,1:T(4,128)S(1)}, s32[24,3]{0,1:T(4,128)}, u32[]{:S(2)}) copy-start(s32[24,3]{0,1:T(4,128)} %param.7) | copy-start | bytes 868
  4.3 8.4 %collective-permute-start.3 = (f32[608,128]{1,0:T(8,128)}, f32[608,128]{1,0:T(8,128)S(1)}, u32[]{:S(2)}, u32[]{:S(2)}) collective-permute-start(f32[608,128]{1,0:T(8,128)} %shard_map.42), channel_id=1, source_target_pairs={{0,256},{256,0},{1,257},{257,1},{2,258},{258,2},{3,259},{259,3},{4... | collective-permute-start | bytes 933896 | tf_op jit(solution)/shard_map/ppermute | solution.py:402
  48.2 17.7 %all-to-all-start.1 = ((f32[32,24,128]{2,1,0:T(8,128)}), f32[32,24,128]{2,1,0:T(8,128)S(1)}, u32[]{:S(2)}, u32[]{:S(2)}) async-start(f32[32,24,128]{2,1,0:T(8,128)} %broadcast_in_dim.8), calls=%async_computation.1 | async-start | bytes 786432 | tf_op jit(solution)/shard_map/all_to_all | solution.py:396
  59.3 11.3 %collective-permute-start.4 = (f32[608,128]{1,0:T(8,128)}, f32[608,128]{1,0:T(8,128)S(1)}, u32[]{:S(2)}, u32[]{:S(2)}) collective-permute-start(f32[608,128]{1,0:T(8,128)} %shard_map.44), channel_id=1, source_target_pairs={{0,256},{256,0},{1,257},{257,1},{2,258},{258,2},{3,259},{259,3},{4... | collective-permute-start | bytes 933896 | tf_op jit(solution)/shard_map/ppermute | solution.py:404

commit v5 on v4

--- a/solution.py
+++ b/solution.py
@@ -6,29 +6,32 @@
 from jax.sharding import Mesh
 from jax.sharding import PartitionSpec as P
 
-DOM = ("z_hi", "z_lo", "y_hi", "y_lo", "x_hi", "core")
-STAGES = (("z_hi", "y_hi"), ("grp", "x_hi", "core", "z_lo", "y_lo"))
+DOM = ("z", "y", "x_hi", "core")
+STAGES = (("z",), ("y",), ("grp", "x_hi", "core"))
 SWAP = ((0, 1), (1, 0))
 LANES = 128
 SUBSPACES = 64
 TILES = 8
 HEAD = 8
-ROOM = 592
-ROWS = HEAD + ROOM + 8
+ROOM = 576
+ROWS = HEAD + ROOM + 24
 VMEM = pl.BlockSpec(memory_space=pltpu.VMEM)
 SMEM = pl.BlockSpec(memory_space=pltpu.SMEM)
 ANY = pl.BlockSpec(memory_space=pl.ANY)
+HBM = pl.BlockSpec(memory_space=pltpu.HBM)
 
 
 def positions(levels, i, start):
     l0, l1, l2 = (levels[d, i].astype(jnp.int32) for d in range(3))
     width = l2 + 1
+    block = (l1 + 1) * width
     rows = []
-    for a in range(4):
-        for b in range(4):
-            at = jnp.minimum(start + (a * (l1 + 1) + b) * width, HEAD + ROOM)
-            rows.append(jnp.where((a <= l0) & (b <= l1), at, HEAD + ROOM))
-    return rows, start + (l0 + 1) * (l1 + 1) * width
+    at = start
+    for _ in range(4):
+        base = jnp.minimum(at, HEAD + ROOM)
+        rows += [base, base + width, base + 2 * width, base + 3 * width]
+        at = at + block
+    return rows, start + (l0 + 1) * block
 
 
 def owner_tiles(levels, i):
@@ -126,27 +129,23 @@
     )(levels, surplus)
 
 
-def products(left_ref, right_ref, grids):
-    def split(ref, s):
-        rows = [ref[pl.ds(s + k, grids, stride=SUBSPACES), :] for k in range(8)]
-        rows = jnp.concatenate(rows, axis=1)
-        high = rows.astype(jnp.bfloat16)
-        return high, (rows - high.astype(jnp.float32)).astype(jnp.bfloat16)
-
-    total = jnp.zeros((grids, grids), jnp.float32)
-    for s in range(0, SUBSPACES, 8):
-        left_high, left_low = split(left_ref, s)
-        right_high, right_low = (left_high, left_low) if left_ref is right_ref else split(right_ref, s)
-        total = total + lax.dot_general(
-            jnp.concatenate([left_high, left_high, left_low], axis=1),
-            jnp.concatenate([right_high, right_low, right_high], axis=1),
-            (((1,), (1,)), ((), ())),
-            preferred_element_type=jnp.float32,
-        )
-    return total
-
-
-def own_kernel(levels_ref, surplus_ref, near_ref, block_ref, far_ref):
+def split(ref, s, grids):
+    rows = [ref[pl.ds(s + k, grids, stride=SUBSPACES), :] for k in range(8)]
+    rows = jnp.concatenate(rows, axis=1)
+    high = rows.astype(jnp.bfloat16)
+    return high, (rows - high.astype(jnp.float32)).astype(jnp.bfloat16)
+
+
+def inner(left, right):
+    return lax.dot_general(
+        jnp.concatenate([left[0], left[0], left[1]], axis=1),
+        jnp.concatenate([right[0], right[1], right[0]], axis=1),
+        (((1,), (1,)), ((), ())),
+        preferred_element_type=jnp.float32,
+    )
+
+
+def own_kernel(levels_ref, surplus_ref, high_ref, low_ref, block_ref, near_ref, far_ref):
     grids = surplus_ref.shape[0]
 
     def mask(i, carry):
@@ -158,21 +157,26 @@
         return carry
 
     lax.fori_loop(0, grids, mask, 0)
-    block_ref[...] = products(near_ref, near_ref, grids) + products(far_ref, far_ref, grids)
+    total = jnp.zeros((grids, grids), jnp.float32)
+    for s in range(0, SUBSPACES, 8):
+        near = split(near_ref, s, grids)
+        far = split(far_ref, s, grids)
+        high_ref[:, s * LANES : (s + 8) * LANES] = near[0]
+        low_ref[:, s * LANES : (s + 8) * LANES] = near[1]
+        total = total + inner(near, near) + inner(far, far)
+    block_ref[...] = total
 
 
 def own_products(levels, surplus):
     grids = surplus.shape[0]
-    half = (grids * SUBSPACES, LANES)
+    part = jax.ShapeDtypeStruct((grids, SUBSPACES * LANES), jnp.bfloat16)
+    half = pltpu.VMEM((grids * SUBSPACES, LANES), jnp.float32)
     return pl.pallas_call(
         own_kernel,
-        out_shape=(
-            jax.ShapeDtypeStruct(half, jnp.float32),
-            jax.ShapeDtypeStruct((grids, grids), jnp.float32),
-        ),
+        out_shape=(part, part, jax.ShapeDtypeStruct((grids, grids), jnp.float32)),
         in_specs=[SMEM, VMEM],
-        out_specs=(VMEM, VMEM),
-        scratch_shapes=[pltpu.VMEM(half, jnp.float32)],
+        out_specs=(VMEM, VMEM, VMEM),
+        scratch_shapes=[half, half],
     )(levels, surplus)
 
 
@@ -190,10 +194,16 @@
     )
 
 
-def cross_kernel(levels_ref, near_ref, block_ref, got_ref, parts_ref, full_ref, other_ref, head, sem):
+def cross_kernel(
+    levels_ref, high_ref, low_ref, block_ref, got_ref, parts_ref, full_ref, other_ref, high, low, head, sems
+):
     grids = block_ref.shape[0]
-    fetch = pltpu.make_async_copy(got_ref.at[0:HEAD, :], head, sem)
+    fetch = pltpu.make_async_copy(got_ref.at[0:HEAD, :], head, sems.at[0])
+    fetch_high = pltpu.make_async_copy(high_ref, high, sems.at[1])
+    fetch_low = pltpu.make_async_copy(low_ref, low, sems.at[2])
     fetch.start()
+    fetch_high.start()
+    fetch_low.start()
     own = jnp.int32(HEAD)
     for i in range(grids):
         own = own + (levels_ref[0, i] + 1) * (levels_ref[1, i] + 1) * (levels_ref[2, i] + 1)
@@ -209,13 +219,18 @@
 
     stop = lax.fori_loop(0, grids, unpack, jnp.int32(HEAD))
     full_ref[0] = (jnp.maximum(own, stop) > HEAD + ROOM).astype(jnp.int32)
-    cross = products(near_ref, other_ref, grids)
+    fetch_high.wait()
+    fetch_low.wait()
+    cross = jnp.zeros((grids, grids), jnp.float32)
+    for s in range(0, SUBSPACES, 8):
+        at = slice(s * LANES, (s + 8) * LANES)
+        cross = cross + inner((high[:, at], low[:, at]), split(other_ref, s, grids))
     folded = fold(block_ref[...], cross, cross.T, lax.axis_index("grp") == 1)
     for k in range(parts_ref.shape[0]):
         parts_ref[k] = folded
 
 
-def cross_products(levels, near, block, got, copies):
+def cross_products(levels, high, low, block, got, copies):
     grids = block.shape[0]
     return pl.pallas_call(
         cross_kernel,
@@ -223,14 +238,16 @@
             jax.ShapeDtypeStruct((copies, grids, LANES), jnp.float32),
             jax.ShapeDtypeStruct((1,), jnp.int32),
         ),
-        in_specs=[SMEM, VMEM, VMEM, VMEM],
+        in_specs=[SMEM, HBM, HBM, VMEM, VMEM],
         out_specs=(VMEM, SMEM),
         scratch_shapes=[
             pltpu.VMEM((grids * SUBSPACES, LANES), jnp.float32),
+            pltpu.VMEM(high.shape, high.dtype),
+            pltpu.VMEM(low.shape, low.dtype),
             pltpu.SMEM((HEAD, LANES), jnp.float32),
-            pltpu.SemaphoreType.DMA,
+            pltpu.SemaphoreType.DMA((3,)),
         ],
-    )(levels, near, block, got)
+    )(levels, high, low, block, got)
 
 
 def eliminate(parts_ref):
@@ -245,11 +262,18 @@
     diagonal = jnp.sum(jnp.where(on_diagonal, gram, 0.0), axis=1, keepdims=True) + 1e-06
     system = jnp.where(lanes < number, gram, 0.0) + jnp.where(on_diagonal, 0.1 * diagonal, 0.0)
     system = jnp.where(lanes == number, diagonal, system)
-    for k in range(number):
-        row = system[k : k + 1, :]
-        column = jnp.broadcast_to(system[:, k : k + 1], system.shape)
-        scaled = row * (1.0 / column[k : k + 1, :])
-        system = system - jnp.where(rows == k, 0.0, column) * jnp.broadcast_to(scaled, system.shape)
+    for first in range(0, number, 8):
+        columns = [
+            jnp.broadcast_to(system[:, k : k + 1], system.shape) for k in range(first, first + 8)
+        ]
+        for j in range(8):
+            k = first + j
+            inverse = 1.0 / columns[j][k : k + 1, :]
+            column = jnp.where(rows == k, 0.0, columns[j])
+            system = system - column * (system[k : k + 1, :] * inverse)
+            for q in range(j + 1, 8):
+                scale = columns[j][first + q : first + q + 1, :] * inverse
+                columns[q] = columns[q] - column * scale
     last = jnp.broadcast_to(system[:, number : number + 1], system.shape)
     solved = jnp.where(on_diagonal, last / system, 0.0)
     return jnp.broadcast_to(jnp.sum(solved, axis=1, keepdims=True), system.shape), on_diagonal
@@ -402,8 +426,8 @@
     got_near = lax.ppermute(far, "grp", SWAP)
     near = pack_near(levels, surplus)
     got_far = lax.ppermute(near, "grp", SWAP)
-    own, block = own_products(levels, surplus)
-    parts, full = cross_products(levels, own, block, got_near, lax.axis_size(STAGES[0]))
+    high, low, block = own_products(levels, surplus)
+    parts, full = cross_products(levels, high, low, block, got_near, lax.axis_size(STAGES[0]))
     dense = full[0] > 0
     parts = lax.cond(
         dense, lambda: dense_parts(levels, surplus, block, parts.shape[0]), lambda: parts
@@ -422,7 +446,7 @@
 
 def solution(mesh):
     torus = Mesh(
-        mesh.devices.reshape(mesh.shape["grp"], 4, 2, 4, 2, 2, 2),
+        mesh.devices.reshape(mesh.shape["grp"], 8, 8, 2, 2),
         ("grp", *DOM),
     )
     return jax.shard_map(

time: 79.9 us -> 70.1 us (0.88)
  waiting for transfers between devices: 10.1 us -> 4.17 us
  Pallas kernels: 22 us -> 16.9 us
  starting transfers between devices: 15.8 us -> 19.8 us
  blocking collectives: 29.5 us -> 27.4 us
    ppermute x1, waiting for transfers between devices: 4.77 us -> 0.01 us  [whole(): got_far = lax.ppermute(near, 'grp', SWAP)]
    all_to_all x1, starting transfers between devices: 8.59 us -> 12.8 us  [exchanged(): return lax.all_to_all(copies, axes, split_axis=0, concat_axis=0, tiled=True)]
    pallas_call x1, Pallas kernels: 8.9 us -> 5.46 us  [finish(): pl.pallas_call(finish_kernel, out_shape=(jax.ShapeDtypeStruct(surplus.sha...]
    all_to_all x1 -> x2, blocking collectives: 29.5 us -> 27.4 us  [exchanged(): return lax.all_to_all(copies, axes, split_axis=0, concat_axis=0, tiled=True)]
    pallas_call x1, Pallas kernels: 4.49 us -> 3.58 us  [cross_products(): pl.pallas_call(cross_kernel, out_shape=(jax.ShapeDtypeStruct((copies, gri...]
  transfers between devices with their start and end apart: 3 -> 3, of which waited for: 3 -> 2; matrix products, arithmetic and copies ran while one was open for 0% -> 0% of each run, Pallas kernels for 6% -> 7%
where the time goes in v5:
time: 70.1 us; the launch traced here: 69.8 us
  blocking collectives  27.4 us (39%)
  starting transfers between devices  19.8 us (28%)
  Pallas kernels  16.9 us (24%)
  waiting for transfers between devices  4.17 us (6%)
  between operations  1.38 us (2%)
    all_to_all x2, blocking collectives, exchanged(): return lax.all_to_all(copies, axes, split_axis=0, concat_axis=0, tiled=True)  27.4 us
    all_to_all x1, starting transfers between devices, exchanged(): return lax.all_to_all(copies, axes, split_axis=0, concat_axis=0, tiled=True)  12.8 us
    pallas_call x1, Pallas kernels, finish(): pl.pallas_call(finish_kernel, out_shape=(jax.ShapeDtypeStruct(surplus.sha...  5.46 us
    ppermute x1, starting transfers between devices, whole(): got_near = lax.ppermute(far, 'grp', SWAP)  3.94 us
    pallas_call x1, Pallas kernels, cross_products(): pl.pallas_call(cross_kernel, out_shape=(jax.ShapeDtypeStruct((copies, gri...  3.58 us
    ppermute x1, starting transfers between devices, whole(): got_far = lax.ppermute(near, 'grp', SWAP)  3.1 us
    pallas_call x1, Pallas kernels, pack_far(): pl.pallas_call(pack_far_kernel, out_shape=jax.ShapeDtypeStruct((ROWS, LAN...  3.02 us
    pallas_call x1, Pallas kernels, own_products(): pl.pallas_call(own_kernel, out_shape=(part, part, jax.ShapeDtypeStruct((g...  2.93 us
  transfers between devices with their start and end apart: 3, of which 2 were waited for; matrix products, arithmetic and copies ran while one was open for 0% of the time, Pallas kernels for 7%

profile of v5, /device:TPU:1, one launch (start us, length us, event | category | flops | bytes accessed | tf_op | source)
XLA Modules:
  0.0 69.8 jit_solution(8551683081660799726)
XLA Ops:
  0.6 0.0 copy-start
  0.6 0.0 copy-start.1
  0.6 3.0 %shard_map.42 = f32[608,128]{1,0:T(8,128)} custom-call(s32[3,24]{1,0:T(4,128)} %bitcast.13, f32[24,64,256]{2,1,0:T(8,128)} %surplus_ref.5), custom_call_target="tpu_custom_call" | custom-call | tf_op jit(solution)/shard_map/pallas_call | solution.py:98
  3.7 3.9 %collective-permute-start.3 = (f32[608,128]{1,0:T(8,128)}, f32[608,128]{1,0:T(8,128)S(1)}, u32[]{:S(2)}, u32[]{:S(2)}) collective-permute-start(f32[608,128]{1,0:T(8,128)} %shard_map.42), channel_id=1, source_target_pairs={{0,256},{256,0},{1,257},{257,1},{2,258},{258,2},{3,259},{259,3},{4... | collective-permute-start | bytes 933896 | tf_op jit(solution)/shard_map/ppermute | solution.py:426
  7.6 0.0 copy-done
  7.6 0.0 copy-done.1
  7.6 2.9 %shard_map.41 = (bf16[24,8192]{1,0:T(8,128)(2,1)}, bf16[24,8192]{1,0:T(8,128)(2,1)}, f32[24,24]{1,0:T(8,128)S(1)}) custom-call(s32[3,24]{1,0:T(4,128)S(1)} %bitcast.14, f32[24,64,256]{2,1,0:T(8,128)S(1)} %copy-done), custom_call_target="tpu_custom_call" | custom-call | tf_op jit(solution)/shard_map/pallas_call | solution.py:174
  10.6 1.5 %collective-permute-done.3.got_ref = f32[608,128]{1,0:T(8,128)S(1)} collective-permute-done((f32[608,128]{1,0:T(8,128)}, f32[608,128]{1,0:T(8,128)S(1)}, u32[]{:S(2)}, u32[]{:S(2)}) %collective-permute-start.3) | collective-permute-done | bytes 311328 | tf_op jit(solution)/shard_map/ppermute | solution.py:426
  12.1 3.6 %shard_map.43 = (f32[8,24,128]{2,1,0:T(8,128)}, s32[1]{0:T(128)}) custom-call(s32[3,24]{1,0:T(4,128)S(1)} %bitcast.15, bf16[24,8192]{1,0:T(8,128)(2,1)} %get-tuple-element.49.high_ref, bf16[24,8192]{1,0:T(8,128)(2,1)} %get-tuple-element.50.low_ref, f32[24,24]{1,0:T(8,128)S(1)} %get-tuple-element.51.block_ref, f32[608,128]{1,0:T(8,128)S(1)} %collective-permute-done.3.got_ref), custom_call_target="tpu_custom_call" | custom-call | tf_op jit(solution)/shard_map/pallas_call | solution.py:235
  16.4 12.8 %all-to-all-start = ((f32[8,24,128]{2,1,0:T(8,128)}), f32[8,24,128]{2,1,0:T(8,128)S(1)}, u32[]{:S(2)}, u32[]{:S(2)}) async-start(f32[8,24,128]{2,1,0:T(8,128)} %get-tuple-element.82), calls=%async_computation | async-start | bytes 196608 | tf_op jit(solution)/shard_map/all_to_all | solution.py:420
  29.2 1.9 %shard_map.44 = f32[608,128]{1,0:T(8,128)} custom-call(s32[3,24]{1,0:T(4,128)S(1)} %bitcast.17, f32[24,64,256]{2,1,0:T(8,128)S(1)} %copy-done), custom_call_target="tpu_custom_call" | custom-call | tf_op jit(solution)/shard_map/pallas_call | solution.py:124
  31.1 3.1 %collective-permute-start.4 = (f32[608,128]{1,0:T(8,128)}, f32[608,128]{1,0:T(8,128)S(1)}, u32[]{:S(2)}, u32[]{:S(2)}) collective-permute-start(f32[608,128]{1,0:T(8,128)} %shard_map.44), channel_id=1, source_target_pairs={{0,256},{256,0},{1,257},{257,1},{2,258},{258,2},{3,259},{259,3},{4... | collective-permute-start | bytes 933896 | tf_op jit(solution)/shard_map/ppermute | solution.py:428
  34.2 2.6 %all-to-all-done = f32[8,24,128]{2,1,0:T(8,128)S(1)} async-done(((f32[8,24,128]{2,1,0:T(8,128)}), f32[8,24,128]{2,1,0:T(8,128)S(1)}, u32[]{:S(2)}, u32[]{:S(2)}) %all-to-all-start) | async-done | bytes 98336 | tf_op jit(solution)/shard_map/all_to_all | solution.py:420
  36.8 14.2 %all_to_all.15 = f32[8,24,128]{2,1,0:T(8,128)S(1)} all-to-all(f32[8,24,128]{2,1,0:T(8,128)S(1)} %broadcast_in_dim.10), channel_id=1, replica_groups=mesh['grp'=2,'z'=8,'y'=8,'x_hi'=2,'core'=2] {'y'}, dimensions={0} | all-to-all | bytes 196608 | tf_op jit(solution)/shard_map/all_to_all | solution.py:420
  51.1 13.2 %all_to_all.16 = f32[8,24,128]{2,1,0:T(8,128)S(1)} all-to-all(f32[8,24,128]{2,1,0:T(8,128)S(1)} %broadcast_in_dim.11), channel_id=1, replica_groups=mesh['grp'=2,'z'=8,'y'=8,'x_hi'=2,'core'=2] {'grp','x_hi','core'}, dimensions={0} | all-to-all | bytes 196608 | tf_op jit(solution)/shard_map/all_to_all | solution.py:420
  64.3 0.0 collective-permute-done.4
  64.3 5.5 %conditional.3 = ((f32[24,64,256]{2,1,0:T(8,128)}, f32[1,48]{1,0:T(1,128)})) conditional(s32[]{:T(128)} %bitcast.5, (s32[3,24]{1,0:T(4,128)S(1)}, f32[8,24,128]{2,1,0:T(8,128)S(1)}, f32[24,64,256]{2,1,0:T(8,128)S(1)}, f32[608,128]{1,0:T(8,128)S(1)}, f32[608,128]{1,0:T(8,128)S(1)}) %tuple.49, (s32[3,24]{1,0:T(4,128)S(1)}, ...), branch_computations={%region_5.6_spmd, %region_6.10_spmd} | conditional | flops 2780532 | bytes 17721104 | solution.py:439
  64.3 5.5 %branch_0_fun.1 = (f32[24,64,256]{2,1,0:T(8,128)}, f32[1,48]{1,0:T(1,128)}) custom-call(s32[3,24]{1,0:T(4,128)S(1)} %get-tuple-element.32.levels_ref, f32[8,24,128]{2,1,0:T(8,128)S(1)} %get-tuple-element.33.parts_ref, f32[24,64,256]{2,1,0:T(8,128)S(1)} %get-tuple-element.34.surplus_ref, f32[608,128]{1,0:T(8,128)S(1)} %get-tuple-element.35.got_near_ref, ...), custom_call_target="tpu_custom_call" | custom-call | tf_op jit(solution)/shard_map/cond/branch_0_fun/pallas_call | solution.py:357
  (5 shorter events, 0.0 us)
Async XLA Ops:
  0.6 7.0 %copy-start = (f32[24,64,256]{2,1,0:T(8,128)S(1)}, f32[24,64,256]{2,1,0:T(8,128)}, u32[]{:S(2)}) copy-start(f32[24,64,256]{2,1,0:T(8,128)} %surplus_ref.5) | copy-start | bytes 4718596
  0.6 7.0 %copy-start.1 = (s32[24,3]{0,1:T(4,128)S(1)}, s32[24,3]{0,1:T(4,128)}, u32[]{:S(2)}) copy-start(s32[24,3]{0,1:T(4,128)} %param.7) | copy-start | bytes 868
  3.7 8.4 %collective-permute-start.3 = (f32[608,128]{1,0:T(8,128)}, f32[608,128]{1,0:T(8,128)S(1)}, u32[]{:S(2)}, u32[]{:S(2)}) collective-permute-start(f32[608,128]{1,0:T(8,128)} %shard_map.42), channel_id=1, source_target_pairs={{0,256},{256,0},{1,257},{257,1},{2,258},{258,2},{3,259},{259,3},{4... | collective-permute-start | bytes 933896 | tf_op jit(solution)/shard_map/ppermute | solution.py:426
  16.4 20.4 %all-to-all-start = ((f32[8,24,128]{2,1,0:T(8,128)}), f32[8,24,128]{2,1,0:T(8,128)S(1)}, u32[]{:S(2)}, u32[]{:S(2)}) async-start(f32[8,24,128]{2,1,0:T(8,128)} %get-tuple-element.82), calls=%async_computation | async-start | bytes 196608 | tf_op jit(solution)/shard_map/all_to_all | solution.py:420
  31.1 33.2 %collective-permute-start.4 = (f32[608,128]{1,0:T(8,128)}, f32[608,128]{1,0:T(8,128)S(1)}, u32[]{:S(2)}, u32[]{:S(2)}) collective-permute-start(f32[608,128]{1,0:T(8,128)} %shard_map.44), channel_id=1, source_target_pairs={{0,256},{256,0},{1,257},{257,1},{2,258},{258,2},{3,259},{259,3},{4... | collective-permute-start | bytes 933896 | tf_op jit(solution)/shard_map/ppermute | solution.py:428

commit v6 on v5

--- a/solution.py
+++ b/solution.py
@@ -180,18 +180,36 @@
     )(levels, surplus)
 
 
-def fold(block, cross, turned, second):
-    zero = jnp.zeros_like(block)
-    return jnp.concatenate(
-        [
-            jnp.where(second, zero, block),
-            jnp.where(second, turned, cross),
-            jnp.where(second, cross, turned),
-            jnp.where(second, block, zero),
-            jnp.zeros((block.shape[0], LANES - 4 * block.shape[0]), jnp.float32),
-        ],
-        axis=1,
-    )
+def fold(block, cross):
+    grids = block.shape[0]
+    strips = range(0, grids, 8)
+    pieces = [block[r : r + 8, r:] for r in strips] + [cross[r : r + 8, :] for r in strips]
+    used = sum(piece.shape[1] for piece in pieces)
+    return jnp.concatenate([*pieces, jnp.zeros((8, LANES - used), jnp.float32)], axis=1)
+
+
+def unfold(first, last, grids):
+    def upper(folded):
+        strips, at = [], 0
+        for r in range(0, grids, 8):
+            strip = folded[:, at : at + grids - r]
+            strips.append(jnp.concatenate([jnp.zeros((8, r), jnp.float32), strip], axis=1) if r else strip)
+            at += grids - r
+        return jnp.concatenate(strips, axis=0), at
+
+    top, at = upper(first)
+    low, _ = upper(last)
+    both = first + last
+    cross = jnp.concatenate(
+        [both[:, at + n * grids : at + (n + 1) * grids] for n in range(grids // 8)], axis=0
+    )
+    half = jnp.concatenate(
+        [jnp.concatenate([top, cross], axis=1), jnp.concatenate([jnp.zeros_like(low), low], axis=1)], axis=0
+    )
+    rows = lax.broadcasted_iota(jnp.int32, half.shape, 0) >> 3
+    columns = lax.broadcasted_iota(jnp.int32, half.shape, 1) >> 3
+    gram = jnp.where(rows <= columns, half, half.T)
+    return jnp.concatenate([gram, jnp.zeros((2 * grids, LANES - 2 * grids), jnp.float32)], axis=1)
 
 
 def cross_kernel(
@@ -225,7 +243,7 @@
     for s in range(0, SUBSPACES, 8):
         at = slice(s * LANES, (s + 8) * LANES)
         cross = cross + inner((high[:, at], low[:, at]), split(other_ref, s, grids))
-    folded = fold(block_ref[...], cross, cross.T, lax.axis_index("grp") == 1)
+    folded = fold(block_ref[...], jnp.where(lax.axis_index("grp") == 1, cross.T, cross))
     for k in range(parts_ref.shape[0]):
         parts_ref[k] = folded
 
@@ -235,7 +253,7 @@
     return pl.pallas_call(
         cross_kernel,
         out_shape=(
-            jax.ShapeDtypeStruct((copies, grids, LANES), jnp.float32),
+            jax.ShapeDtypeStruct((copies, 8, LANES), jnp.float32),
             jax.ShapeDtypeStruct((1,), jnp.int32),
         ),
         in_specs=[SMEM, HBM, HBM, VMEM, VMEM],
@@ -250,17 +268,19 @@
     )(levels, high, low, block, got)
 
 
-def eliminate(parts_ref):
-    number = 2 * parts_ref.shape[1]
-    folded = parts_ref[0]
-    for k in range(1, parts_ref.shape[0]):
-        folded = folded + parts_ref[k]
-    gram = jnp.concatenate([folded, pltpu.roll(folded, LANES - number, 1)], axis=0)
+def eliminate(parts_ref, grids):
+    number = 2 * grids
+    senders = parts_ref.shape[0] // 2
+    first, last = parts_ref[0], parts_ref[senders]
+    for k in range(1, senders):
+        first = first + parts_ref[k]
+        last = last + parts_ref[senders + k]
+    gram = unfold(first, last, grids)
     rows = lax.broadcasted_iota(jnp.int32, gram.shape, 0)
     lanes = lax.broadcasted_iota(jnp.int32, gram.shape, 1)
     on_diagonal = rows == lanes
     diagonal = jnp.sum(jnp.where(on_diagonal, gram, 0.0), axis=1, keepdims=True) + 1e-06
-    system = jnp.where(lanes < number, gram, 0.0) + jnp.where(on_diagonal, 0.1 * diagonal, 0.0)
+    system = gram + jnp.where(on_diagonal, 0.1 * diagonal, 0.0)
     system = jnp.where(lanes == number, diagonal, system)
     for first in range(0, number, 8):
         columns = [
@@ -280,14 +300,14 @@
 
 
 def solve_kernel(parts_ref, out_ref):
-    solution_rows, on_diagonal = eliminate(parts_ref)
+    solution_rows, on_diagonal = eliminate(parts_ref, out_ref.shape[1] // 2)
     out_ref[...] = jnp.sum(jnp.where(on_diagonal, solution_rows, 0.0), axis=0, keepdims=True)[:, : out_ref.shape[1]]
 
 
-def solve_parts(parts):
+def solve_parts(parts, grids):
     return pl.pallas_call(
         solve_kernel,
-        out_shape=jax.ShapeDtypeStruct((1, 2 * parts.shape[1]), jnp.float32),
+        out_shape=jax.ShapeDtypeStruct((1, 2 * grids), jnp.float32),
         in_specs=[VMEM],
         out_specs=VMEM,
     )(parts)
@@ -311,7 +331,7 @@
     side = lax.axis_index("grp")
     fetch = pltpu.make_async_copy(got_near_ref.at[0:HEAD, :], head, head_sem)
     fetch.start()
-    solution_rows, on_diagonal = eliminate(parts_ref)
+    solution_rows, on_diagonal = eliminate(parts_ref, grids)
     out_ref[...] = jnp.sum(jnp.where(on_diagonal, solution_rows, 0.0), axis=0, keepdims=True)[:, : out_ref.shape[1]]
     weights[...] = solution_rows
     fetch.wait()
@@ -385,27 +405,30 @@
     return jnp.where(second, high, low), jnp.where(second, low, high)
 
 
-def dense_parts(levels, surplus, block, copies):
-    near, far = halves(levels, surplus)
-    cross = lax.dot_general(
-        near,
-        lax.ppermute(far, "grp", SWAP),
-        (((1, 2), (1, 2)), ((), ())),
-        precision=lax.Precision.HIGHEST,
-        preferred_element_type=jnp.float32,
-    )
-    folded = fold(block, cross, cross.T, lax.axis_index("grp") == 1)
-    return jnp.broadcast_to(folded, (copies, *folded.shape))
-
-
-def dense_finish(levels, parts, surplus):
+def dense_finish(levels, surplus):
     grids = surplus.shape[0]
     second = lax.axis_index("grp") == 1
     near, far = halves(levels, surplus)
     got_near = lax.ppermute(far, "grp", SWAP)
     got_far = lax.ppermute(near, "grp", SWAP)
-    coefficients = solve_parts(parts)
-    start, stop = coefficients[0, :grids], coefficients[0, grids : 2 * grids]
+
+    def products(left, right):
+        return lax.dot_general(
+            left,
+            right,
+            (((1, 2), (1, 2)), ((), ())),
+            precision=lax.Precision.HIGHEST,
+            preferred_element_type=jnp.float32,
+        )
+
+    cross = products(near, got_near)
+    own = products(near, near) + products(far, far)
+    folded = fold(own, jnp.where(second, cross.T, cross))
+    pair = jnp.stack([jnp.where(second, 0.0, folded), jnp.where(second, folded, 0.0)])
+    for axis in ("grp", *DOM):
+        pair = lax.psum(pair, axis)
+    coefficients = solve_parts(pair, grids)
+    start, stop = coefficients[0, :grids], coefficients[0, grids:]
     own = jnp.where(second, stop, start)[:, None, None]
     other = jnp.where(second, start, stop)[:, None, None]
     sum_near = jnp.sum(own * near + other * got_near, axis=0)
@@ -428,17 +451,13 @@
     got_far = lax.ppermute(near, "grp", SWAP)
     high, low, block = own_products(levels, surplus)
     parts, full = cross_products(levels, high, low, block, got_near, lax.axis_size(STAGES[0]))
-    dense = full[0] > 0
-    parts = lax.cond(
-        dense, lambda: dense_parts(levels, surplus, block, parts.shape[0]), lambda: parts
-    )
     for axes, following in zip(STAGES, STAGES[1:]):
         folded = jnp.sum(exchanged(parts, axes), axis=0)
         parts = jnp.broadcast_to(folded, (lax.axis_size(following), *folded.shape))
     parts = exchanged(parts, STAGES[-1])
     updated, coefficients = lax.cond(
-        dense,
-        lambda: dense_finish(levels, parts, surplus),
+        full[0] > 0,
+        lambda: dense_finish(levels, surplus),
         lambda: tuple(finish(levels, parts, surplus, got_near, got_far)),
     )
     return updated, coefficients.reshape(-1)

time: 70.1 us -> 70.1 us (level)
  starting transfers between devices: 19.8 us -> 15.7 us
  blocking collectives: 27.4 us -> 30.8 us
  local copies, waits for them, and re-layouts: 0.03 us -> 1.14 us
    all_to_all x2, blocking collectives: 27.4 us -> 30.8 us  [exchanged(): return lax.all_to_all(copies, axes, split_axis=0, concat_axis=0, tiled=True)]
    all_to_all x1, starting transfers between devices: 12.8 us -> 9.82 us  [exchanged(): return lax.all_to_all(copies, axes, split_axis=0, concat_axis=0, tiled=True)]
    ppermute x1, waiting for transfers between devices: 1.53 us -> 0.01 us  [whole(): got_near = lax.ppermute(far, 'grp', SWAP)]
    all_to_all x1, waiting for transfers between devices: 2.64 us -> 3.97 us  [exchanged(): return lax.all_to_all(copies, axes, split_axis=0, concat_axis=0, tiled=True)]
    ppermute x1, starting transfers between devices: 3.1 us -> 1.91 us  [whole(): got_far = lax.ppermute(near, 'grp', SWAP)]
  transfers between devices with their start and end apart: 3 -> 3, of which waited for: 2 -> 1; matrix products, arithmetic and copies ran while one was open for 0% -> 1% of each run, Pallas kernels for 7% -> 12%
where the time goes in v6:
time: 70.1 us; the launch traced here: 69.7 us
  blocking collectives  30.8 us (44%)
  Pallas kernels  16.7 us (24%)
  starting transfers between devices  15.7 us (22%)
  waiting for transfers between devices  3.97 us (6%)
  between operations  1.38 us (2%)
  local copies, waits for them, and re-layouts  1.14 us (2%)
    all_to_all x2, blocking collectives, exchanged(): return lax.all_to_all(copies, axes, split_axis=0, concat_axis=0, tiled=True)  30.8 us
    all_to_all x1, starting transfers between devices, exchanged(): return lax.all_to_all(copies, axes, split_axis=0, concat_axis=0, tiled=True)  9.82 us
    pallas_call x1, Pallas kernels, finish(): pl.pallas_call(finish_kernel, out_shape=(jax.ShapeDtypeStruct(surplus.sha...  5.1 us
    all_to_all x1, waiting for transfers between devices, exchanged(): return lax.all_to_all(copies, axes, split_axis=0, concat_axis=0, tiled=True)  3.97 us
    ppermute x1, starting transfers between devices, whole(): got_near = lax.ppermute(far, 'grp', SWAP)  3.94 us
    pallas_call x1, Pallas kernels, cross_products(): pl.pallas_call(cross_kernel, out_shape=(jax.ShapeDtypeStruct((copies, 8,...  3.68 us
    pallas_call x1, Pallas kernels, pack_far(): pl.pallas_call(pack_far_kernel, out_shape=jax.ShapeDtypeStruct((ROWS, LAN...  3.04 us
    pallas_call x1, Pallas kernels, own_products(): pl.pallas_call(own_kernel, out_shape=(part, part, jax.ShapeDtypeStruct((g...  2.97 us
  transfers between devices with their start and end apart: 3, of which 1 were waited for; matrix products, arithmetic and copies ran while one was open for 1% of the time, Pallas kernels for 12%

profile of v6, /device:TPU:1, one launch (start us, length us, event | category | flops | bytes accessed | tf_op | source)
XLA Modules:
  0.0 69.7 jit_solution(7395267918917465696)
XLA Ops:
  0.6 0.0 copy-start
  0.6 0.0 copy-start.1
  0.6 3.0 %shard_map.42 = f32[608,128]{1,0:T(8,128)} custom-call(s32[3,24]{1,0:T(4,128)} %bitcast.35, f32[24,64,256]{2,1,0:T(8,128)} %surplus_ref.5), custom_call_target="tpu_custom_call" | custom-call | tf_op jit(solution)/shard_map/pallas_call | solution.py:98
  3.7 3.9 %collective-permute-start.2 = (f32[608,128]{1,0:T(8,128)}, f32[608,128]{1,0:T(8,128)S(1)}, u32[]{:S(2)}, u32[]{:S(2)}) collective-permute-start(f32[608,128]{1,0:T(8,128)} %shard_map.42), channel_id=1, source_target_pairs={{0,256},{256,0},{1,257},{257,1},{2,258},{258,2},{3,259},{259,3},{4... | collective-permute-start | bytes 933896 | tf_op jit(solution)/shard_map/ppermute | solution.py:449
  7.6 0.0 copy-done
  7.7 0.0 copy-done.1
  7.7 1.9 %shard_map.44 = f32[608,128]{1,0:T(8,128)} custom-call(s32[3,24]{1,0:T(4,128)S(1)} %bitcast.36, f32[24,64,256]{2,1,0:T(8,128)S(1)} %copy-done), custom_call_target="tpu_custom_call" | custom-call | tf_op jit(solution)/shard_map/pallas_call | solution.py:124
  9.6 1.9 %collective-permute-start.3 = (f32[608,128]{1,0:T(8,128)}, f32[608,128]{1,0:T(8,128)S(1)}, u32[]{:S(2)}, u32[]{:S(2)}) collective-permute-start(f32[608,128]{1,0:T(8,128)} %shard_map.44), channel_id=1, source_target_pairs={{0,256},{256,0},{1,257},{257,1},{2,258},{258,2},{3,259},{259,3},{4... | collective-permute-start | bytes 933896 | tf_op jit(solution)/shard_map/ppermute | solution.py:451
  11.5 3.0 %shard_map.41 = (bf16[24,8192]{1,0:T(8,128)(2,1)}, bf16[24,8192]{1,0:T(8,128)(2,1)}, f32[24,24]{1,0:T(8,128)}) custom-call(s32[3,24]{1,0:T(4,128)S(1)} %bitcast.37, f32[24,64,256]{2,1,0:T(8,128)S(1)} %copy-done), custom_call_target="tpu_custom_call" | custom-call | tf_op jit(solution)/shard_map/pallas_call | solution.py:174
  14.5 0.0 collective-permute-done.2.got_ref
  14.5 3.7 %shard_map.43 = (f32[8,8,128]{2,1,0:T(8,128)}, s32[1]{0:T(128)}) custom-call(s32[3,24]{1,0:T(4,128)S(1)} %bitcast.38, bf16[24,8192]{1,0:T(8,128)(2,1)} %get-tuple-element.33.high_ref, bf16[24,8192]{1,0:T(8,128)(2,1)} %get-tuple-element.34.low_ref, f32[24,24]{1,0:T(8,128)} %get-tuple-element.35.block_ref, f32[608,128]{1,0:T(8,128)S(1)} %collective-permute-done.2.got_ref), custom_call_target="tpu_custom_call" | custom-call | tf_op jit(solution)/shard_map/pallas_call | solution.py:253
  18.1 17.3 %all_to_all.15 = f32[8,8,128]{2,1,0:T(8,128)S(1)} all-to-all(f32[8,8,128]{2,1,0:T(8,128)} %get-tuple-element.37), channel_id=1, replica_groups=mesh['grp'=2,'z'=8,'y'=8,'x_hi'=2,'core'=2] {'z'}, dimensions={0} | all-to-all | bytes 65536 | tf_op jit(solution)/shard_map/all_to_all | solution.py:443
  35.5 13.5 %all_to_all.16 = f32[8,8,128]{2,1,0:T(8,128)S(1)} all-to-all(f32[8,8,128]{2,1,0:T(8,128)S(1)} %broadcast_in_dim.10), channel_id=1, replica_groups=mesh['grp'=2,'z'=8,'y'=8,'x_hi'=2,'core'=2] {'y'}, dimensions={0} | all-to-all | bytes 65536 | tf_op jit(solution)/shard_map/all_to_all | solution.py:443
  49.0 0.6 broadcast_in_dim.11
  49.6 9.8 %all-to-all-start.2 = ((f32[8,8,128]{2,1,0:T(8,128)}), f32[8,8,128]{2,1,0:T(8,128)S(1)}, u32[]{:S(2)}, u32[]{:S(2)}) async-start(f32[8,8,128]{2,1,0:T(8,128)} %broadcast_in_dim.11), calls=%async_computation.2 | async-start | bytes 65536 | tf_op jit(solution)/shard_map/all_to_all | solution.py:443
  60.1 0.0 collective-permute-done.3
  60.1 4.0 %all-to-all-done.2 = f32[8,8,128]{2,1,0:T(8,128)S(1)} async-done(((f32[8,8,128]{2,1,0:T(8,128)}), f32[8,8,128]{2,1,0:T(8,128)S(1)}, u32[]{:S(2)}, u32[]{:S(2)}) %all-to-all-start.2) | async-done | bytes 32800 | tf_op jit(solution)/shard_map/all_to_all | solution.py:443
  64.1 5.1 %conditional.1 = (f32[1,48]{1,0:T(1,128)S(1)}, f32[24,64,256]{2,1,0:T(8,128)}) conditional(s32[]{:T(128)} %bitcast.13, (s32[3,24]{1,0:T(4,128)S(1)}, f32[8,8,128]{2,1,0:T(8,128)S(1)}, f32[24,64,256]{2,1,0:T(8,128)S(1)}, f32[608,128]{1,0:T(8,128)S(1)}, f32[608,128]{1,0:T(8,128)S(1)}) %tuple.42, (s32[3,24]{1,0:T(4,128)S(1)}, ...), branch_computations={%region_2.0_spmd, %region_3.12_spmd} | conditional | flops 172665328 | bytes 24173096 | solution.py:458
  64.1 5.1 %branch_0_fun.1 = (f32[24,64,256]{2,1,0:T(8,128)}, f32[1,48]{1,0:T(1,128)S(1)}) custom-call(s32[3,24]{1,0:T(4,128)S(1)} %get-tuple-element.17.levels_ref, f32[8,8,128]{2,1,0:T(8,128)S(1)} %get-tuple-element.18.parts_ref, f32[24,64,256]{2,1,0:T(8,128)S(1)} %get-tuple-element.19.surplus_ref, f32[608,128]{1,0:T(8,128)S(1)} %get-tuple-element.20.got_near_ref, ...), custom_call_target="tpu_custom_call" | custom-call | tf_op jit(solution)/shard_map/cond/branch_0_fun/pallas_call | solution.py:377
  69.2 0.0 copy-start.4
  69.2 0.5 copy-done.4
  (3 shorter events, 0.0 us)
Async XLA Ops:
  0.6 7.0 %copy-start = (f32[24,64,256]{2,1,0:T(8,128)S(1)}, f32[24,64,256]{2,1,0:T(8,128)}, u32[]{:S(2)}) copy-start(f32[24,64,256]{2,1,0:T(8,128)} %surplus_ref.5) | copy-start | bytes 4718596
  0.6 7.0 %copy-start.1 = (s32[24,3]{0,1:T(4,128)S(1)}, s32[24,3]{0,1:T(4,128)}, u32[]{:S(2)}) copy-start(s32[24,3]{0,1:T(4,128)} %param.5) | copy-start | bytes 868
  3.7 10.8 %collective-permute-start.2 = (f32[608,128]{1,0:T(8,128)}, f32[608,128]{1,0:T(8,128)S(1)}, u32[]{:S(2)}, u32[]{:S(2)}) collective-permute-start(f32[608,128]{1,0:T(8,128)} %shard_map.42), channel_id=1, source_target_pairs={{0,256},{256,0},{1,257},{257,1},{2,258},{258,2},{3,259},{259,3},{4... | collective-permute-start | bytes 933896 | tf_op jit(solution)/shard_map/ppermute | solution.py:449
  9.6 50.5 %collective-permute-start.3 = (f32[608,128]{1,0:T(8,128)}, f32[608,128]{1,0:T(8,128)S(1)}, u32[]{:S(2)}, u32[]{:S(2)}) collective-permute-start(f32[608,128]{1,0:T(8,128)} %shard_map.44), channel_id=1, source_target_pairs={{0,256},{256,0},{1,257},{257,1},{2,258},{258,2},{3,259},{259,3},{4... | collective-permute-start | bytes 933896 | tf_op jit(solution)/shard_map/ppermute | solution.py:451
  49.6 14.4 %all-to-all-start.2 = ((f32[8,8,128]{2,1,0:T(8,128)}), f32[8,8,128]{2,1,0:T(8,128)S(1)}, u32[]{:S(2)}, u32[]{:S(2)}) async-start(f32[8,8,128]{2,1,0:T(8,128)} %broadcast_in_dim.11), calls=%async_computation.2 | async-start | bytes 65536 | tf_op jit(solution)/shard_map/all_to_all | solution.py:443
  69.2 0.5 copy-start.4

commit v7 on v6

--- a/solution.py
+++ b/solution.py
@@ -7,7 +7,7 @@
 from jax.sharding import PartitionSpec as P
 
 DOM = ("z", "y", "x_hi", "core")
-STAGES = (("z",), ("y",), ("grp", "x_hi", "core"))
+STAGES = (("z",), ("grp", "y", "x_hi", "core"))
 SWAP = ((0, 1), (1, 0))
 LANES = 128
 SUBSPACES = 64
@@ -164,7 +164,7 @@
         high_ref[:, s * LANES : (s + 8) * LANES] = near[0]
         low_ref[:, s * LANES : (s + 8) * LANES] = near[1]
         total = total + inner(near, near) + inner(far, far)
-    block_ref[...] = total
+    block_ref[...] = fold_own(total)
 
 
 def own_products(levels, surplus):
@@ -173,49 +173,58 @@
     half = pltpu.VMEM((grids * SUBSPACES, LANES), jnp.float32)
     return pl.pallas_call(
         own_kernel,
-        out_shape=(part, part, jax.ShapeDtypeStruct((grids, grids), jnp.float32)),
+        out_shape=(part, part, jax.ShapeDtypeStruct((8, LANES), jnp.float32)),
         in_specs=[SMEM, VMEM],
         out_specs=(VMEM, VMEM, VMEM),
         scratch_shapes=[half, half],
     )(levels, surplus)
 
 
-def fold(block, cross):
-    grids = block.shape[0]
-    strips = range(0, grids, 8)
-    pieces = [block[r : r + 8, r:] for r in strips] + [cross[r : r + 8, :] for r in strips]
-    used = sum(piece.shape[1] for piece in pieces)
-    return jnp.concatenate([*pieces, jnp.zeros((8, LANES - used), jnp.float32)], axis=1)
+def fold_own(block):
+    strips = [block[r : r + 8, r:] for r in range(0, block.shape[0], 8)]
+    used = sum(strip.shape[1] for strip in strips)
+    return jnp.concatenate([*strips, jnp.zeros((8, LANES - used), jnp.float32)], axis=1)
+
+
+def fold_cross(cross):
+    grids = cross.shape[0]
+    strips = [cross[r : r + 8, :] for r in range(0, grids, 8)]
+    ahead = sum(range(8, grids + 8, 8))
+    behind = LANES - ahead - grids * len(strips)
+    zeros = [jnp.zeros((8, width), jnp.float32) for width in (ahead, behind)]
+    return jnp.concatenate([zeros[0], *strips, zeros[1]], axis=1)
 
 
 def unfold(first, last, grids):
-    def upper(folded):
-        strips, at = [], 0
+    def strips(folded):
+        own, at = [], 0
         for r in range(0, grids, 8):
             strip = folded[:, at : at + grids - r]
-            strips.append(jnp.concatenate([jnp.zeros((8, r), jnp.float32), strip], axis=1) if r else strip)
+            own.append(jnp.concatenate([jnp.zeros((8, r), jnp.float32), strip], axis=1) if r else strip)
             at += grids - r
-        return jnp.concatenate(strips, axis=0), at
-
-    top, at = upper(first)
-    low, _ = upper(last)
-    both = first + last
-    cross = jnp.concatenate(
-        [both[:, at + n * grids : at + (n + 1) * grids] for n in range(grids // 8)], axis=0
-    )
+        cross = [folded[:, at + n * grids : at + (n + 1) * grids] for n in range(grids // 8)]
+        return own, cross
+
+    own_first, cross_first = strips(first)
+    own_last, cross_last = strips(last)
     half = jnp.concatenate(
-        [jnp.concatenate([top, cross], axis=1), jnp.concatenate([jnp.zeros_like(low), low], axis=1)], axis=0
-    )
-    rows = lax.broadcasted_iota(jnp.int32, half.shape, 0) >> 3
-    columns = lax.broadcasted_iota(jnp.int32, half.shape, 1) >> 3
-    gram = jnp.where(rows <= columns, half, half.T)
+        [jnp.concatenate(pair, axis=1) for pair in zip(own_first, cross_first)]
+        + [jnp.concatenate(pair, axis=1) for pair in zip(cross_last, own_last)],
+        axis=0,
+    )
+    turned = half.T
+    rows = lax.broadcasted_iota(jnp.int32, half.shape, 0)
+    columns = lax.broadcasted_iota(jnp.int32, half.shape, 1)
+    between = (rows < grids) != (columns < grids)
+    gram = jnp.where(rows >> 3 <= columns >> 3, half, turned)
+    gram = jnp.where(between, half + turned, gram)
     return jnp.concatenate([gram, jnp.zeros((2 * grids, LANES - 2 * grids), jnp.float32)], axis=1)
 
 
 def cross_kernel(
     levels_ref, high_ref, low_ref, block_ref, got_ref, parts_ref, full_ref, other_ref, high, low, head, sems
 ):
-    grids = block_ref.shape[0]
+    grids = high.shape[0]
     fetch = pltpu.make_async_copy(got_ref.at[0:HEAD, :], head, sems.at[0])
     fetch_high = pltpu.make_async_copy(high_ref, high, sems.at[1])
     fetch_low = pltpu.make_async_copy(low_ref, low, sems.at[2])
@@ -243,13 +252,13 @@
     for s in range(0, SUBSPACES, 8):
         at = slice(s * LANES, (s + 8) * LANES)
         cross = cross + inner((high[:, at], low[:, at]), split(other_ref, s, grids))
-    folded = fold(block_ref[...], jnp.where(lax.axis_index("grp") == 1, cross.T, cross))
+    folded = block_ref[...] + fold_cross(cross)
     for k in range(parts_ref.shape[0]):
         parts_ref[k] = folded
 
 
 def cross_products(levels, high, low, block, got, copies):
-    grids = block.shape[0]
+    grids = high.shape[0]
     return pl.pallas_call(
         cross_kernel,
         out_shape=(
@@ -324,6 +333,8 @@
     head,
     head_sem,
     weights,
+    line,
+    line_sem,
     result,
     out_sems,
 ):
@@ -332,8 +343,10 @@
     fetch = pltpu.make_async_copy(got_near_ref.at[0:HEAD, :], head, head_sem)
     fetch.start()
     solution_rows, on_diagonal = eliminate(parts_ref, grids)
-    out_ref[...] = jnp.sum(jnp.where(on_diagonal, solution_rows, 0.0), axis=0, keepdims=True)[:, : out_ref.shape[1]]
     weights[...] = solution_rows
+    line[...] = jnp.sum(jnp.where(on_diagonal, solution_rows, 0.0), axis=0, keepdims=True)[:, : line.shape[1]]
+    send_line = pltpu.make_async_copy(line, out_ref, line_sem)
+    send_line.start()
     fetch.wait()
 
     def add(i, carry):
@@ -367,6 +380,7 @@
         return carry
 
     lax.fori_loop(0, grids, spread, 0)
+    send_line.wait()
     for i in range(grids):
         put(i, 0).wait()
         put(i, 1).wait()
@@ -381,11 +395,13 @@
             jax.ShapeDtypeStruct((1, 2 * grids), jnp.float32),
         ),
         in_specs=[SMEM, VMEM, VMEM, VMEM, VMEM],
-        out_specs=(ANY, VMEM),
+        out_specs=(HBM, HBM),
         scratch_shapes=[
             pltpu.SMEM((HEAD, LANES), jnp.float32),
             pltpu.SemaphoreType.DMA,
             pltpu.VMEM((2 * grids, LANES), jnp.float32),
+            pltpu.VMEM((1, 2 * grids), jnp.float32),
+            pltpu.SemaphoreType.DMA,
             pltpu.VMEM((2, grids * SUBSPACES, LANES), jnp.float32),
             pltpu.SemaphoreType.DMA((2, grids)),
         ],
@@ -423,7 +439,7 @@
 
     cross = products(near, got_near)
     own = products(near, near) + products(far, far)
-    folded = fold(own, jnp.where(second, cross.T, cross))
+    folded = fold_own(own) + fold_cross(cross)
     pair = jnp.stack([jnp.where(second, 0.0, folded), jnp.where(second, folded, 0.0)])
     for axis in ("grp", *DOM):
         pair = lax.psum(pair, axis)

time: 70.1 us -> 69.7 us (level)
  blocking collectives: 30.8 us -> 19.7 us
  waiting for transfers between devices: 3.97 us -> 9.89 us
  starting transfers between devices: 15.7 us -> 20.4 us
    all_to_all x2 -> x1, blocking collectives: 30.8 us -> 19.7 us  [exchanged(): return lax.all_to_all(copies, axes, split_axis=0, concat_axis=0, tiled=True)]
    ppermute x1, waiting for transfers between devices: 0.01 us -> 8.48 us  [whole(): got_far = lax.ppermute(near, 'grp', SWAP)]
    all_to_all x1, waiting for transfers between devices: 3.97 us -> 0.01 us  [exchanged(): return lax.all_to_all(copies, axes, split_axis=0, concat_axis=0, tiled=True)]
    all_to_all x1, starting transfers between devices: 9.82 us -> 13.1 us  [exchanged(): return lax.all_to_all(copies, axes, split_axis=0, concat_axis=0, tiled=True)]
    ppermute x1, starting transfers between devices: 1.91 us -> 3.35 us  [whole(): got_far = lax.ppermute(near, 'grp', SWAP)]
    ppermute x1, waiting for transfers between devices: 0.01 us -> 1.41 us  [whole(): got_near = lax.ppermute(far, 'grp', SWAP)]
  transfers between devices with their start and end apart: 3 -> 3, of which waited for: 1 -> 2; matrix products, arithmetic and copies ran while one was open for 1% -> 0% of each run, Pallas kernels for 12% -> 7%
where the time goes in v7:
time: 69.7 us; the launch traced here: 69.3 us
  starting transfers between devices  20.4 us (29%)
  blocking collectives  19.7 us (28%)
  Pallas kernels  16.7 us (24%)
  waiting for transfers between devices  9.89 us (14%)
  between operations  1.37 us (2%)
  local copies, waits for them, and re-layouts  1.23 us (2%)
    all_to_all x1, blocking collectives, exchanged(): return lax.all_to_all(copies, axes, split_axis=0, concat_axis=0, tiled=True)  19.7 us
    all_to_all x1, starting transfers between devices, exchanged(): return lax.all_to_all(copies, axes, split_axis=0, concat_axis=0, tiled=True)  13.1 us
    ppermute x1, waiting for transfers between devices, whole(): got_far = lax.ppermute(near, 'grp', SWAP)  8.48 us
    pallas_call x1, Pallas kernels, finish(): pl.pallas_call(finish_kernel, out_shape=(jax.ShapeDtypeStruct(surplus.sha...  5.16 us
    ppermute x1, starting transfers between devices, whole(): got_near = lax.ppermute(far, 'grp', SWAP)  3.94 us
    pallas_call x1, Pallas kernels, cross_products(): pl.pallas_call(cross_kernel, out_shape=(jax.ShapeDtypeStruct((copies, 8,...  3.6 us
    ppermute x1, starting transfers between devices, whole(): got_far = lax.ppermute(near, 'grp', SWAP)  3.35 us
    pallas_call x1, Pallas kernels, own_products(): pl.pallas_call(own_kernel, out_shape=(part, part, jax.ShapeDtypeStruct((8...  3.05 us
  transfers between devices with their start and end apart: 3, of which 2 were waited for; matrix products, arithmetic and copies ran while one was open for 0% of the time, Pallas kernels for 7%

profile of v7, /device:TPU:1, one launch (start us, length us, event | category | flops | bytes accessed | tf_op | source)
XLA Modules:
  0.0 69.3 jit_solution(10390212150020631568)
XLA Ops:
  0.6 0.0 copy-start
  0.6 0.0 copy-start.1
  0.6 3.0 %shard_map.42 = f32[608,128]{1,0:T(8,128)} custom-call(s32[3,24]{1,0:T(4,128)} %bitcast.33, f32[24,64,256]{2,1,0:T(8,128)} %surplus_ref.5), custom_call_target="tpu_custom_call" | custom-call | tf_op jit(solution)/shard_map/pallas_call | solution.py:98
  3.7 3.9 %collective-permute-start.2 = (f32[608,128]{1,0:T(8,128)}, f32[608,128]{1,0:T(8,128)S(1)}, u32[]{:S(2)}, u32[]{:S(2)}) collective-permute-start(f32[608,128]{1,0:T(8,128)} %shard_map.42), channel_id=1, source_target_pairs={{0,256},{256,0},{1,257},{257,1},{2,258},{258,2},{3,259},{259,3},{4... | collective-permute-start | bytes 933896 | tf_op jit(solution)/shard_map/ppermute | solution.py:465
  7.6 0.0 copy-done
  7.6 0.0 copy-done.1
  7.7 3.1 %shard_map.41 = (bf16[24,8192]{1,0:T(8,128)(2,1)}, bf16[24,8192]{1,0:T(8,128)(2,1)}, f32[8,128]{1,0:T(8,128)}) custom-call(s32[3,24]{1,0:T(4,128)S(1)} %bitcast.34, f32[24,64,256]{2,1,0:T(8,128)S(1)} %copy-done), custom_call_target="tpu_custom_call" | custom-call | tf_op jit(solution)/shard_map/pallas_call | solution.py:174
  10.7 1.4 %collective-permute-done.2.got_ref = f32[608,128]{1,0:T(8,128)S(1)} collective-permute-done((f32[608,128]{1,0:T(8,128)}, f32[608,128]{1,0:T(8,128)S(1)}, u32[]{:S(2)}, u32[]{:S(2)}) %collective-permute-start.2) | collective-permute-done | bytes 311328 | tf_op jit(solution)/shard_map/ppermute | solution.py:465
  12.1 3.6 %shard_map.43 = (f32[8,8,128]{2,1,0:T(8,128)}, s32[1]{0:T(128)}) custom-call(s32[3,24]{1,0:T(4,128)S(1)} %bitcast.35, bf16[24,8192]{1,0:T(8,128)(2,1)} %get-tuple-element.33.high_ref, bf16[24,8192]{1,0:T(8,128)(2,1)} %get-tuple-element.34.low_ref, f32[8,128]{1,0:T(8,128)} %get-tuple-element.35.block_ref, f32[608,128]{1,0:T(8,128)S(1)} %collective-permute-done.2.got_ref), custom_call_target="tpu_custom_call" | custom-call | tf_op jit(solution)/shard_map/pallas_call | solution.py:262
  15.7 19.7 %all_to_all.10 = f32[8,8,128]{2,1,0:T(8,128)S(1)} all-to-all(f32[8,8,128]{2,1,0:T(8,128)} %get-tuple-element.37), channel_id=1, replica_groups=mesh['grp'=2,'z'=8,'y'=8,'x_hi'=2,'core'=2] {'z'}, dimensions={0} | all-to-all | bytes 65536 | tf_op jit(solution)/shard_map/all_to_all | solution.py:459
  35.4 0.7 %broadcast_in_dim.8 = f32[64,8,128]{2,1,0:T(8,128)} broadcast(f32[8,128]{1,0:T(8,128)S(1)} %reduce_sum.27), dimensions={1,2} | broadcast | bytes 266240 | tf_op jit(solution)/shard_map/broadcast_in_dim | solution.py:472
  36.1 13.1 %all-to-all-start.1 = ((f32[64,8,128]{2,1,0:T(8,128)}), f32[64,8,128]{2,1,0:T(8,128)S(1)}, u32[]{:S(2)}, u32[]{:S(2)}) async-start(f32[64,8,128]{2,1,0:T(8,128)} %broadcast_in_dim.8), calls=%async_computation.1 | async-start | bytes 524288 | tf_op jit(solution)/shard_map/all_to_all | solution.py:459
  49.2 1.9 %shard_map.44 = f32[608,128]{1,0:T(8,128)} custom-call(s32[3,24]{1,0:T(4,128)S(1)} %bitcast.36, f32[24,64,256]{2,1,0:T(8,128)S(1)} %copy-done), custom_call_target="tpu_custom_call" | custom-call | tf_op jit(solution)/shard_map/pallas_call | solution.py:124
  51.1 3.4 %collective-permute-start.3 = (f32[608,128]{1,0:T(8,128)}, f32[608,128]{1,0:T(8,128)S(1)}, u32[]{:S(2)}, u32[]{:S(2)}) collective-permute-start(f32[608,128]{1,0:T(8,128)} %shard_map.44), channel_id=1, source_target_pairs={{0,256},{256,0},{1,257},{257,1},{2,258},{258,2},{3,259},{259,3},{4... | collective-permute-start | bytes 933896 | tf_op jit(solution)/shard_map/ppermute | solution.py:467
  55.1 8.5 %collective-permute-done.3 = f32[608,128]{1,0:T(8,128)S(1)} collective-permute-done((f32[608,128]{1,0:T(8,128)}, f32[608,128]{1,0:T(8,128)S(1)}, u32[]{:S(2)}, u32[]{:S(2)}) %collective-permute-start.3) | collective-permute-done | bytes 311328 | tf_op jit(solution)/shard_map/ppermute | solution.py:467
  63.6 0.0 all-to-all-done.1
  63.6 5.2 %conditional.1 = (f32[1,48]{1,0:T(1,128)S(1)}, f32[24,64,256]{2,1,0:T(8,128)}) conditional(s32[]{:T(128)} %bitcast.12, (s32[3,24]{1,0:T(4,128)S(1)}, f32[64,8,128]{2,1,0:T(8,128)S(1)}, f32[24,64,256]{2,1,0:T(8,128)S(1)}, f32[608,128]{1,0:T(8,128)S(1)}, f32[608,128]{1,0:T(8,128)S(1)}) %tuple.42, (s32[3,24]{1,0:T(4,128)S(1)}, ...), branch_computations={%region_1.0_spmd, %region_2.11_spmd} | conditional | flops 172668848 | bytes 24174516 | solution.py:474
  63.6 5.2 %branch_0_fun.1 = (f32[24,64,256]{2,1,0:T(8,128)}, f32[1,48]{1,0:T(1,128)S(1)}) custom-call(s32[3,24]{1,0:T(4,128)S(1)} %get-tuple-element.17.levels_ref, f32[64,8,128]{2,1,0:T(8,128)S(1)} %get-tuple-element.18.parts_ref, f32[24,64,256]{2,1,0:T(8,128)S(1)} %get-tuple-element.19.surplus_ref, f32[608,128]{1,0:T(8,128)S(1)} %get-tuple-element.20.got_near_ref, ...), custom_call_target="tpu_custom_call" | custom-call | tf_op jit(solution)/shard_map/cond/branch_0_fun/pallas_call | solution.py:391
  68.8 0.0 copy-start.4
  68.8 0.5 copy-done.4
  (1 shorter events, 0.0 us)
Async XLA Ops:
  0.6 7.0 %copy-start = (f32[24,64,256]{2,1,0:T(8,128)S(1)}, f32[24,64,256]{2,1,0:T(8,128)}, u32[]{:S(2)}) copy-start(f32[24,64,256]{2,1,0:T(8,128)} %surplus_ref.5) | copy-start | bytes 4718596
  0.6 7.0 %copy-start.1 = (s32[24,3]{0,1:T(4,128)S(1)}, s32[24,3]{0,1:T(4,128)}, u32[]{:S(2)}) copy-start(s32[24,3]{0,1:T(4,128)} %param.5) | copy-start | bytes 868
  3.7 8.4 %collective-permute-start.2 = (f32[608,128]{1,0:T(8,128)}, f32[608,128]{1,0:T(8,128)S(1)}, u32[]{:S(2)}, u32[]{:S(2)}) collective-permute-start(f32[608,128]{1,0:T(8,128)} %shard_map.42), channel_id=1, source_target_pairs={{0,256},{256,0},{1,257},{257,1},{2,258},{258,2},{3,259},{259,3},{4... | collective-permute-start | bytes 933896 | tf_op jit(solution)/shard_map/ppermute | solution.py:465
  36.1 27.5 %all-to-all-start.1 = ((f32[64,8,128]{2,1,0:T(8,128)}), f32[64,8,128]{2,1,0:T(8,128)S(1)}, u32[]{:S(2)}, u32[]{:S(2)}) async-start(f32[64,8,128]{2,1,0:T(8,128)} %broadcast_in_dim.8), calls=%async_computation.1 | async-start | bytes 524288 | tf_op jit(solution)/shard_map/all_to_all | solution.py:459
  51.1 12.5 %collective-permute-start.3 = (f32[608,128]{1,0:T(8,128)}, f32[608,128]{1,0:T(8,128)S(1)}, u32[]{:S(2)}, u32[]{:S(2)}) collective-permute-start(f32[608,128]{1,0:T(8,128)} %shard_map.44), channel_id=1, source_target_pairs={{0,256},{256,0},{1,257},{257,1},{2,258},{258,2},{3,259},{259,3},{4... | collective-permute-start | bytes 933896 | tf_op jit(solution)/shard_map/ppermute | solution.py:467
  68.8 0.5 copy-start.4

commit v8 on v7

--- a/solution.py
+++ b/solution.py
@@ -18,7 +18,7 @@
 VMEM = pl.BlockSpec(memory_space=pltpu.VMEM)
 SMEM = pl.BlockSpec(memory_space=pltpu.SMEM)
 ANY = pl.BlockSpec(memory_space=pl.ANY)
-HBM = pl.BlockSpec(memory_space=pltpu.HBM)
+GRANT = pltpu.CompilerParams(vmem_limit_bytes=12 << 20)
 
 
 def positions(levels, i, start):
@@ -97,6 +97,7 @@
     grids = surplus.shape[0]
     return pl.pallas_call(
         pack_far_kernel,
+        compiler_params=GRANT,
         out_shape=jax.ShapeDtypeStruct((ROWS, LANES), jnp.float32),
         in_specs=[SMEM, ANY],
         out_specs=VMEM,
@@ -123,6 +124,7 @@
 def pack_near(levels, surplus):
     return pl.pallas_call(
         pack_near_kernel,
+        compiler_params=GRANT,
         out_shape=jax.ShapeDtypeStruct((ROWS, LANES), jnp.float32),
         in_specs=[SMEM, VMEM],
         out_specs=VMEM,
@@ -173,6 +175,7 @@
     half = pltpu.VMEM((grids * SUBSPACES, LANES), jnp.float32)
     return pl.pallas_call(
         own_kernel,
+        compiler_params=GRANT,
         out_shape=(part, part, jax.ShapeDtypeStruct((8, LANES), jnp.float32)),
         in_specs=[SMEM, VMEM],
         out_specs=(VMEM, VMEM, VMEM),
@@ -222,15 +225,11 @@
 
 
 def cross_kernel(
-    levels_ref, high_ref, low_ref, block_ref, got_ref, parts_ref, full_ref, other_ref, high, low, head, sems
+    levels_ref, high_ref, low_ref, block_ref, got_ref, parts_ref, full_ref, other_ref, head, sem
 ):
-    grids = high.shape[0]
-    fetch = pltpu.make_async_copy(got_ref.at[0:HEAD, :], head, sems.at[0])
-    fetch_high = pltpu.make_async_copy(high_ref, high, sems.at[1])
-    fetch_low = pltpu.make_async_copy(low_ref, low, sems.at[2])
+    grids = high_ref.shape[0]
+    fetch = pltpu.make_async_copy(got_ref.at[0:HEAD, :], head, sem)
     fetch.start()
-    fetch_high.start()
-    fetch_low.start()
     own = jnp.int32(HEAD)
     for i in range(grids):
         own = own + (levels_ref[0, i] + 1) * (levels_ref[1, i] + 1) * (levels_ref[2, i] + 1)
@@ -246,12 +245,10 @@
 
     stop = lax.fori_loop(0, grids, unpack, jnp.int32(HEAD))
     full_ref[0] = (jnp.maximum(own, stop) > HEAD + ROOM).astype(jnp.int32)
-    fetch_high.wait()
-    fetch_low.wait()
     cross = jnp.zeros((grids, grids), jnp.float32)
     for s in range(0, SUBSPACES, 8):
         at = slice(s * LANES, (s + 8) * LANES)
-        cross = cross + inner((high[:, at], low[:, at]), split(other_ref, s, grids))
+        cross = cross + inner((high_ref[:, at], low_ref[:, at]), split(other_ref, s, grids))
     folded = block_ref[...] + fold_cross(cross)
     for k in range(parts_ref.shape[0]):
         parts_ref[k] = folded
@@ -261,18 +258,17 @@
     grids = high.shape[0]
     return pl.pallas_call(
         cross_kernel,
+        compiler_params=GRANT,
         out_shape=(
             jax.ShapeDtypeStruct((copies, 8, LANES), jnp.float32),
             jax.ShapeDtypeStruct((1,), jnp.int32),
         ),
-        in_specs=[SMEM, HBM, HBM, VMEM, VMEM],
+        in_specs=[SMEM, VMEM, VMEM, VMEM, VMEM],
         out_specs=(VMEM, SMEM),
         scratch_shapes=[
             pltpu.VMEM((grids * SUBSPACES, LANES), jnp.float32),
-            pltpu.VMEM(high.shape, high.dtype),
-            pltpu.VMEM(low.shape, low.dtype),
             pltpu.SMEM((HEAD, LANES), jnp.float32),
-            pltpu.SemaphoreType.DMA((3,)),
+            pltpu.SemaphoreType.DMA,
         ],
     )(levels, high, low, block, got)
 
@@ -316,6 +312,7 @@
 def solve_parts(parts, grids):
     return pl.pallas_call(
         solve_kernel,
+        compiler_params=GRANT,
         out_shape=jax.ShapeDtypeStruct((1, 2 * grids), jnp.float32),
         in_specs=[VMEM],
         out_specs=VMEM,
@@ -333,8 +330,6 @@
     head,
     head_sem,
     weights,
-    line,
-    line_sem,
     result,
     out_sems,
 ):
@@ -344,9 +339,7 @@
     fetch.start()
     solution_rows, on_diagonal = eliminate(parts_ref, grids)
     weights[...] = solution_rows
-    line[...] = jnp.sum(jnp.where(on_diagonal, solution_rows, 0.0), axis=0, keepdims=True)[:, : line.shape[1]]
-    send_line = pltpu.make_async_copy(line, out_ref, line_sem)
-    send_line.start()
+    out_ref[...] = jnp.sum(jnp.where(on_diagonal, solution_rows, 0.0), axis=0, keepdims=True)[:, : out_ref.shape[1]]
     fetch.wait()
 
     def add(i, carry):
@@ -380,7 +373,6 @@
         return carry
 
     lax.fori_loop(0, grids, spread, 0)
-    send_line.wait()
     for i in range(grids):
         put(i, 0).wait()
         put(i, 1).wait()
@@ -390,18 +382,17 @@
     grids = surplus.shape[0]
     return pl.pallas_call(
         finish_kernel,
+        compiler_params=GRANT,
         out_shape=(
             jax.ShapeDtypeStruct(surplus.shape, jnp.float32),
             jax.ShapeDtypeStruct((1, 2 * grids), jnp.float32),
         ),
         in_specs=[SMEM, VMEM, VMEM, VMEM, VMEM],
-        out_specs=(HBM, HBM),
+        out_specs=(ANY, VMEM),
         scratch_shapes=[
             pltpu.SMEM((HEAD, LANES), jnp.float32),
             pltpu.SemaphoreType.DMA,
             pltpu.VMEM((2 * grids, LANES), jnp.float32),
-            pltpu.VMEM((1, 2 * grids), jnp.float32),
-            pltpu.SemaphoreType.DMA,
             pltpu.VMEM((2, grids * SUBSPACES, LANES), jnp.float32),
             pltpu.SemaphoreType.DMA((2, grids)),
         ],

time: 69.7 us -> 67.1 us (0.963)
  Pallas kernels: 16.7 us -> 13.9 us
    pallas_call x5, Pallas kernels: 16.7 us -> 13.9 us  [the longest x1 5.15 us: finish(): pl.pallas_call(finish_kernel, compiler_params=GRANT, out_shape=(jax.Shape...]
  transfers between devices with their start and end apart: 3 -> 3, of which waited for: 2 -> 2; matrix products, arithmetic and copies ran while one was open for 0% -> 0% of each run, Pallas kernels for 7% -> 5%
where the time goes in v8:
time: 67.1 us; the launch traced here: 66.8 us
  starting transfers between devices  20.4 us (30%)
  blocking collectives  19.5 us (29%)
  Pallas kernels  13.9 us (21%)
  waiting for transfers between devices  10.5 us (16%)
  between operations  1.38 us (2%)
  local copies, waits for them, and re-layouts  1.24 us (2%)
    all_to_all x1, blocking collectives, exchanged(): return lax.all_to_all(copies, axes, split_axis=0, concat_axis=0, tiled=True)  19.5 us
    all_to_all x1, starting transfers between devices, exchanged(): return lax.all_to_all(copies, axes, split_axis=0, concat_axis=0, tiled=True)  13.1 us
    ppermute x1, waiting for transfers between devices, whole(): got_far = lax.ppermute(near, 'grp', SWAP)  8.62 us
    pallas_call x1, Pallas kernels, finish(): pl.pallas_call(finish_kernel, compiler_params=GRANT, out_shape=(jax.Shape...  5.15 us
    ppermute x1, starting transfers between devices, whole(): got_near = lax.ppermute(far, 'grp', SWAP)  3.94 us
    ppermute x1, starting transfers between devices, whole(): got_far = lax.ppermute(near, 'grp', SWAP)  3.37 us
    pallas_call x1, Pallas kernels, cross_products(): pl.pallas_call(cross_kernel, compiler_params=GRANT, out_shape=(jax.ShapeD...  2.81 us
    pallas_call x1, Pallas kernels, own_products(): pl.pallas_call(own_kernel, compiler_params=GRANT, out_shape=(part, part,...  2.42 us
  transfers between devices with their start and end apart: 3, of which 2 were waited for; matrix products, arithmetic and copies ran while one was open for 0% of the time, Pallas kernels for 5%

profile of v8, /device:TPU:1, one launch (start us, length us, event | category | flops | bytes accessed | tf_op | source)
XLA Modules:
  0.0 66.8 jit_solution(15261876522059982689)
XLA Ops:
  0.6 0.0 copy-start
  0.6 0.0 copy-start.1
  0.6 2.3 %shard_map.42 = f32[608,128]{1,0:T(8,128)S(1)} custom-call(s32[3,24]{1,0:T(4,128)} %bitcast.33, f32[24,64,256]{2,1,0:T(8,128)} %surplus_ref.5), custom_call_target="tpu_custom_call" | custom-call | tf_op jit(solution)/shard_map/pallas_call | solution.py:98
  3.0 3.9 %collective-permute-start.2 = (f32[608,128]{1,0:T(8,128)S(1)}, f32[608,128]{1,0:T(8,128)S(1)}, u32[]{:S(2)}, u32[]{:S(2)}) collective-permute-start(f32[608,128]{1,0:T(8,128)S(1)} %shard_map.42), channel_id=1, source_target_pairs={{0,256},{256,0},{1,257},{257,1},{2,258},{258,2},{3,259},{259,3},{4... | collective-permute-start | bytes 933896 | tf_op jit(solution)/shard_map/ppermute | solution.py:456
  6.9 0.0 copy-done
  6.9 0.0 copy-done.1
  6.9 2.4 %shard_map.41 = (bf16[24,8192]{1,0:T(8,128)(2,1)S(1)}, bf16[24,8192]{1,0:T(8,128)(2,1)S(1)}, f32[8,128]{1,0:T(8,128)S(1)}) custom-call(s32[3,24]{1,0:T(4,128)S(1)} %bitcast.34, f32[24,64,256]{2,1,0:T(8,128)S(1)} %copy-done), custom_call_target="tpu_custom_call" | custom-call | tf_op jit(solution)/shard_map/pallas_call | solution.py:176
  9.4 1.8 %collective-permute-done.2.got_ref = f32[608,128]{1,0:T(8,128)S(1)} collective-permute-done((f32[608,128]{1,0:T(8,128)S(1)}, f32[608,128]{1,0:T(8,128)S(1)}, u32[]{:S(2)}, u32[]{:S(2)}) %collective-permute-start.2) | collective-permute-done | bytes 311328 | tf_op jit(solution)/shard_map/ppermute | solution.py:456
  11.2 2.8 %shard_map.43 = (f32[8,8,128]{2,1,0:T(8,128)S(1)}, s32[1]{0:T(128)}) custom-call(s32[3,24]{1,0:T(4,128)S(1)} %bitcast.35, bf16[24,8192]{1,0:T(8,128)(2,1)S(1)} %get-tuple-element.33.high_ref, bf16[24,8192]{1,0:T(8,128)(2,1)S(1)} %get-tuple-element.34.low_ref, f32[8,128]{1,0:T(8,128)S(1)} %get-tuple-element.35.block_ref, ...), custom_call_target="tpu_custom_call" | custom-call | tf_op jit(solution)/shard_map/pallas_call | solution.py:259
  14.0 19.5 %all_to_all.10 = f32[8,8,128]{2,1,0:T(8,128)S(1)} all-to-all(f32[8,8,128]{2,1,0:T(8,128)S(1)} %get-tuple-element.37), channel_id=1, replica_groups=mesh['grp'=2,'z'=8,'y'=8,'x_hi'=2,'core'=2] {'z'}, dimensions={0} | all-to-all | bytes 65536 | tf_op jit(solution)/shard_map/all_to_all | solution.py:450
  33.5 0.7 %broadcast_in_dim.8 = f32[64,8,128]{2,1,0:T(8,128)} broadcast(f32[8,128]{1,0:T(8,128)S(1)} %reduce_sum.27), dimensions={1,2} | broadcast | bytes 266240 | tf_op jit(solution)/shard_map/broadcast_in_dim | solution.py:463
  34.2 13.1 %all-to-all-start.1 = ((f32[64,8,128]{2,1,0:T(8,128)}), f32[64,8,128]{2,1,0:T(8,128)S(1)}, u32[]{:S(2)}, u32[]{:S(2)}) async-start(f32[64,8,128]{2,1,0:T(8,128)} %broadcast_in_dim.8), calls=%async_computation.1 | async-start | bytes 524288 | tf_op jit(solution)/shard_map/all_to_all | solution.py:450
  47.3 1.2 %shard_map.44 = f32[608,128]{1,0:T(8,128)S(1)} custom-call(s32[3,24]{1,0:T(4,128)S(1)} %bitcast.36, f32[24,64,256]{2,1,0:T(8,128)S(1)} %copy-done), custom_call_target="tpu_custom_call" | custom-call | tf_op jit(solution)/shard_map/pallas_call | solution.py:125
  48.5 3.4 %collective-permute-start.3 = (f32[608,128]{1,0:T(8,128)S(1)}, f32[608,128]{1,0:T(8,128)S(1)}, u32[]{:S(2)}, u32[]{:S(2)}) collective-permute-start(f32[608,128]{1,0:T(8,128)S(1)} %shard_map.44), channel_id=1, source_target_pairs={{0,256},{256,0},{1,257},{257,1},{2,258},{258,2},{3,259},{259,3},{4... | collective-permute-start | bytes 933896 | tf_op jit(solution)/shard_map/ppermute | solution.py:458
  52.5 8.6 %collective-permute-done.3 = f32[608,128]{1,0:T(8,128)S(1)} collective-permute-done((f32[608,128]{1,0:T(8,128)S(1)}, f32[608,128]{1,0:T(8,128)S(1)}, u32[]{:S(2)}, u32[]{:S(2)}) %collective-permute-start.3) | collective-permute-done | bytes 311328 | tf_op jit(solution)/shard_map/ppermute | solution.py:458
  61.1 0.0 all-to-all-done.1
  61.1 5.2 %conditional.1 = (f32[1,48]{1,0:T(1,128)S(1)}, f32[24,64,256]{2,1,0:T(8,128)}) conditional(s32[]{:T(128)} %bitcast.12, (s32[3,24]{1,0:T(4,128)S(1)}, f32[64,8,128]{2,1,0:T(8,128)S(1)}, f32[24,64,256]{2,1,0:T(8,128)S(1)}, f32[608,128]{1,0:T(8,128)S(1)}, f32[608,128]{1,0:T(8,128)S(1)}) %tuple.42, (s32[3,24]{1,0:T(4,128)S(1)}, ...), branch_computations={%region_1.0_spmd, %region_2.11_spmd} | conditional | flops 172668848 | bytes 24174516 | solution.py:465
  61.1 5.1 %branch_0_fun.1 = (f32[24,64,256]{2,1,0:T(8,128)}, f32[1,48]{1,0:T(1,128)S(1)}) custom-call(s32[3,24]{1,0:T(4,128)S(1)} %get-tuple-element.17.levels_ref, f32[64,8,128]{2,1,0:T(8,128)S(1)} %get-tuple-element.18.parts_ref, f32[24,64,256]{2,1,0:T(8,128)S(1)} %get-tuple-element.19.surplus_ref, f32[608,128]{1,0:T(8,128)S(1)} %get-tuple-element.20.got_near_ref, ...), custom_call_target="tpu_custom_call" | custom-call | tf_op jit(solution)/shard_map/cond/branch_0_fun/pallas_call | solution.py:383
  66.3 0.0 copy-start.4
  66.3 0.5 copy-done.4
  (1 shorter events, 0.0 us)
Async XLA Ops:
  0.6 6.3 %copy-start = (f32[24,64,256]{2,1,0:T(8,128)S(1)}, f32[24,64,256]{2,1,0:T(8,128)}, u32[]{:S(2)}) copy-start(f32[24,64,256]{2,1,0:T(8,128)} %surplus_ref.5) | copy-start | bytes 4718596
  0.6 6.3 %copy-start.1 = (s32[24,3]{0,1:T(4,128)S(1)}, s32[24,3]{0,1:T(4,128)}, u32[]{:S(2)}) copy-start(s32[24,3]{0,1:T(4,128)} %param.5) | copy-start | bytes 868
  3.0 8.2 %collective-permute-start.2 = (f32[608,128]{1,0:T(8,128)S(1)}, f32[608,128]{1,0:T(8,128)S(1)}, u32[]{:S(2)}, u32[]{:S(2)}) collective-permute-start(f32[608,128]{1,0:T(8,128)S(1)} %shard_map.42), channel_id=1, source_target_pairs={{0,256},{256,0},{1,257},{257,1},{2,258},{258,2},{3,259},{259,3},{4... | collective-permute-start | bytes 933896 | tf_op jit(solution)/shard_map/ppermute | solution.py:456
  34.2 26.9 %all-to-all-start.1 = ((f32[64,8,128]{2,1,0:T(8,128)}), f32[64,8,128]{2,1,0:T(8,128)S(1)}, u32[]{:S(2)}, u32[]{:S(2)}) async-start(f32[64,8,128]{2,1,0:T(8,128)} %broadcast_in_dim.8), calls=%async_computation.1 | async-start | bytes 524288 | tf_op jit(solution)/shard_map/all_to_all | solution.py:450
  48.5 12.6 %collective-permute-start.3 = (f32[608,128]{1,0:T(8,128)S(1)}, f32[608,128]{1,0:T(8,128)S(1)}, u32[]{:S(2)}, u32[]{:S(2)}) collective-permute-start(f32[608,128]{1,0:T(8,128)S(1)} %shard_map.44), channel_id=1, source_target_pairs={{0,256},{256,0},{1,257},{257,1},{2,258},{258,2},{3,259},{259,3},{4... | collective-permute-start | bytes 933896 | tf_op jit(solution)/shard_map/ppermute | solution.py:458
  66.3 0.5 copy-start.4

commit v9 on v8

--- a/solution.py
+++ b/solution.py
@@ -90,7 +90,7 @@
             store_packed(out_ref, rows, k, held[tile_rows(i, k), :])
         return stop
 
-    lax.fori_loop(0, grids, pack, jnp.int32(HEAD))
+    over_grids(grids, pack, jnp.int32(HEAD))
 
 
 def pack_far(levels, surplus):
@@ -118,7 +118,7 @@
             store_packed(out_ref, rows, k, cell_tile(surplus_ref, i, k, 0))
         return stop
 
-    lax.fori_loop(0, grids, pack, jnp.int32(HEAD))
+    over_grids(grids, pack, jnp.int32(HEAD))
 
 
 def pack_near(levels, surplus):
@@ -131,23 +131,33 @@
     )(levels, surplus)
 
 
+def over_grids(grids, body, init):
+    def step(n, carry):
+        return body(2 * n + 1, body(2 * n, carry))
+
+    return lax.fori_loop(0, grids // 2, step, init)
+
+
 def split(ref, s, grids):
     rows = [ref[pl.ds(s + k, grids, stride=SUBSPACES), :] for k in range(8)]
     rows = jnp.concatenate(rows, axis=1)
-    high = rows.astype(jnp.bfloat16)
-    return high, (rows - high.astype(jnp.float32)).astype(jnp.bfloat16)
+    high = rows.astype(jnp.bfloat16).astype(jnp.float32)
+    return jnp.concatenate([high, rows - high], axis=0).astype(jnp.bfloat16)
 
 
 def inner(left, right):
     return lax.dot_general(
-        jnp.concatenate([left[0], left[0], left[1]], axis=1),
-        jnp.concatenate([right[0], right[1], right[0]], axis=1),
-        (((1,), (1,)), ((), ())),
-        preferred_element_type=jnp.float32,
-    )
-
-
-def own_kernel(levels_ref, surplus_ref, high_ref, low_ref, block_ref, near_ref, far_ref):
+        left, right, (((1,), (1,)), ((), ())), preferred_element_type=jnp.float32
+    )
+
+
+def whole_products(total):
+    grids = total.shape[0] // 2
+    rows = total[:grids, :] + total[grids:, :]
+    return rows[:, :grids] + rows[:, grids:]
+
+
+def own_kernel(levels_ref, surplus_ref, both_ref, block_ref, near_ref, far_ref):
     grids = surplus_ref.shape[0]
 
     def mask(i, carry):
@@ -158,27 +168,26 @@
             far_ref[at, :] = jnp.where(tiles[k], cell_tile(surplus_ref, i, k, 1), 0.0)
         return carry
 
-    lax.fori_loop(0, grids, mask, 0)
-    total = jnp.zeros((grids, grids), jnp.float32)
+    over_grids(grids, mask, 0)
+    total = jnp.zeros((2 * grids, 2 * grids), jnp.float32)
     for s in range(0, SUBSPACES, 8):
         near = split(near_ref, s, grids)
         far = split(far_ref, s, grids)
-        high_ref[:, s * LANES : (s + 8) * LANES] = near[0]
-        low_ref[:, s * LANES : (s + 8) * LANES] = near[1]
+        both_ref[:, s * LANES : (s + 8) * LANES] = near
         total = total + inner(near, near) + inner(far, far)
-    block_ref[...] = fold_own(total)
+    block_ref[...] = fold_own(whole_products(total))
 
 
 def own_products(levels, surplus):
     grids = surplus.shape[0]
-    part = jax.ShapeDtypeStruct((grids, SUBSPACES * LANES), jnp.bfloat16)
+    both = jax.ShapeDtypeStruct((2 * grids, SUBSPACES * LANES), jnp.bfloat16)
     half = pltpu.VMEM((grids * SUBSPACES, LANES), jnp.float32)
     return pl.pallas_call(
         own_kernel,
         compiler_params=GRANT,
-        out_shape=(part, part, jax.ShapeDtypeStruct((8, LANES), jnp.float32)),
+        out_shape=(both, jax.ShapeDtypeStruct((8, LANES), jnp.float32)),
         in_specs=[SMEM, VMEM],
-        out_specs=(VMEM, VMEM, VMEM),
+        out_specs=(VMEM, VMEM),
         scratch_shapes=[half, half],
     )(levels, surplus)
 
@@ -225,9 +234,9 @@
 
 
 def cross_kernel(
-    levels_ref, high_ref, low_ref, block_ref, got_ref, parts_ref, full_ref, other_ref, head, sem
+    levels_ref, both_ref, block_ref, got_ref, parts_ref, full_ref, other_ref, head, sem
 ):
-    grids = high_ref.shape[0]
+    grids = both_ref.shape[0] // 2
     fetch = pltpu.make_async_copy(got_ref.at[0:HEAD, :], head, sem)
     fetch.start()
     own = jnp.int32(HEAD)
@@ -243,19 +252,19 @@
             other_ref[tile_rows(i, k), :] = jnp.where(tiles[k], tile, 0.0)
         return stop
 
-    stop = lax.fori_loop(0, grids, unpack, jnp.int32(HEAD))
+    stop = over_grids(grids, unpack, jnp.int32(HEAD))
     full_ref[0] = (jnp.maximum(own, stop) > HEAD + ROOM).astype(jnp.int32)
-    cross = jnp.zeros((grids, grids), jnp.float32)
+    total = jnp.zeros((2 * grids, 2 * grids), jnp.float32)
     for s in range(0, SUBSPACES, 8):
         at = slice(s * LANES, (s + 8) * LANES)
-        cross = cross + inner((high_ref[:, at], low_ref[:, at]), split(other_ref, s, grids))
-    folded = block_ref[...] + fold_cross(cross)
+        total = total + inner(both_ref[:, at], split(other_ref, s, grids))
+    folded = block_ref[...] + fold_cross(whole_products(total))
     for k in range(parts_ref.shape[0]):
         parts_ref[k] = folded
 
 
-def cross_products(levels, high, low, block, got, copies):
-    grids = high.shape[0]
+def cross_products(levels, both, block, got, copies):
+    grids = both.shape[0] // 2
     return pl.pallas_call(
         cross_kernel,
         compiler_params=GRANT,
@@ -263,14 +272,14 @@
             jax.ShapeDtypeStruct((copies, 8, LANES), jnp.float32),
             jax.ShapeDtypeStruct((1,), jnp.int32),
         ),
-        in_specs=[SMEM, VMEM, VMEM, VMEM, VMEM],
+        in_specs=[SMEM, VMEM, VMEM, VMEM],
         out_specs=(VMEM, SMEM),
         scratch_shapes=[
             pltpu.VMEM((grids * SUBSPACES, LANES), jnp.float32),
             pltpu.SMEM((HEAD, LANES), jnp.float32),
             pltpu.SemaphoreType.DMA,
         ],
-    )(levels, high, low, block, got)
+    )(levels, both, block, got)
 
 
 def eliminate(parts_ref, grids):
@@ -358,7 +367,7 @@
         return stop, tuple(added)
 
     zero = jnp.zeros((8, LANES), jnp.float32)
-    _, sums = lax.fori_loop(0, grids, add, (jnp.int32(HEAD), (zero,) * (2 * TILES)))
+    _, sums = over_grids(grids, add, (jnp.int32(HEAD), (zero,) * (2 * TILES)))
 
     def put(i, slot):
         rows = pl.ds(i * SUBSPACES, SUBSPACES)
@@ -372,7 +381,7 @@
             put(i, slot).start()
         return carry
 
-    lax.fori_loop(0, grids, spread, 0)
+    over_grids(grids, spread, 0)
     for i in range(grids):
         put(i, 0).wait()
         put(i, 1).wait()
@@ -456,8 +465,8 @@
     got_near = lax.ppermute(far, "grp", SWAP)
     near = pack_near(levels, surplus)
     got_far = lax.ppermute(near, "grp", SWAP)
-    high, low, block = own_products(levels, surplus)
-    parts, full = cross_products(levels, high, low, block, got_near, lax.axis_size(STAGES[0]))
+    both, block = own_products(levels, surplus)
+    parts, full = cross_products(levels, both, block, got_near, lax.axis_size(STAGES[0]))
     for axes, following in zip(STAGES, STAGES[1:]):
         folded = jnp.sum(exchanged(parts, axes), axis=0)
         parts = jnp.broadcast_to(folded, (lax.axis_size(following), *folded.shape))

time: 67.1 us -> 66.8 us (level)
  no operation moved by 1% of the time
where the time goes in v9:
time: 66.8 us; the launch traced here: 66.4 us
  starting transfers between devices  20.4 us (31%)
  blocking collectives  19.4 us (29%)
  Pallas kernels  13.4 us (20%)
  waiting for transfers between devices  10.6 us (16%)
  between operations  1.38 us (2%)
  local copies, waits for them, and re-layouts  1.24 us (2%)
    all_to_all x1, blocking collectives, exchanged(): return lax.all_to_all(copies, axes, split_axis=0, concat_axis=0, tiled=True)  19.4 us
    all_to_all x1, starting transfers between devices, exchanged(): return lax.all_to_all(copies, axes, split_axis=0, concat_axis=0, tiled=True)  13.1 us
    ppermute x1, waiting for transfers between devices, whole(): got_far = lax.ppermute(near, 'grp', SWAP)  8.73 us
    pallas_call x1, Pallas kernels, finish(): pl.pallas_call(finish_kernel, compiler_params=GRANT, out_shape=(jax.Shape...  5.01 us
    ppermute x1, starting transfers between devices, whole(): got_near = lax.ppermute(far, 'grp', SWAP)  3.94 us
    ppermute x1, starting transfers between devices, whole(): got_far = lax.ppermute(near, 'grp', SWAP)  3.37 us
    pallas_call x1, Pallas kernels, cross_products(): pl.pallas_call(cross_kernel, compiler_params=GRANT, out_shape=(jax.ShapeD...  2.6 us
    pallas_call x1, Pallas kernels, own_products(): pl.pallas_call(own_kernel, compiler_params=GRANT, out_shape=(both, jax.Sh...  2.43 us
  transfers between devices with their start and end apart: 3, of which 2 were waited for; matrix products, arithmetic and copies ran while one was open for 0% of the time, Pallas kernels for 5%

profile of v9, /device:TPU:1, one launch (start us, length us, event | category | flops | bytes accessed | tf_op | source)
XLA Modules:
  0.0 66.4 jit_solution(6070217057240951203)
XLA Ops:
  0.6 0.0 copy-start
  0.6 0.0 copy-start.1
  0.6 2.3 %shard_map.42 = f32[608,128]{1,0:T(8,128)S(1)} custom-call(s32[3,24]{1,0:T(4,128)} %bitcast.33, f32[24,64,256]{2,1,0:T(8,128)} %surplus_ref.5), custom_call_target="tpu_custom_call" | custom-call | tf_op jit(solution)/shard_map/pallas_call | solution.py:98
  3.0 3.9 %collective-permute-start.2 = (f32[608,128]{1,0:T(8,128)S(1)}, f32[608,128]{1,0:T(8,128)S(1)}, u32[]{:S(2)}, u32[]{:S(2)}) collective-permute-start(f32[608,128]{1,0:T(8,128)S(1)} %shard_map.42), channel_id=1, source_target_pairs={{0,256},{256,0},{1,257},{257,1},{2,258},{258,2},{3,259},{259,3},{4... | collective-permute-start | bytes 933896 | tf_op jit(solution)/shard_map/ppermute | solution.py:465
  6.9 0.0 copy-done
  6.9 0.0 copy-done.1
  6.9 2.4 %shard_map.41 = (bf16[48,8192]{1,0:T(8,128)(2,1)S(1)}, f32[8,128]{1,0:T(8,128)S(1)}) custom-call(s32[3,24]{1,0:T(4,128)S(1)} %bitcast.34, f32[24,64,256]{2,1,0:T(8,128)S(1)} %copy-done), custom_call_target="tpu_custom_call" | custom-call | tf_op jit(solution)/shard_map/pallas_call | solution.py:185
  9.4 1.8 %collective-permute-done.2.got_ref = f32[608,128]{1,0:T(8,128)S(1)} collective-permute-done((f32[608,128]{1,0:T(8,128)S(1)}, f32[608,128]{1,0:T(8,128)S(1)}, u32[]{:S(2)}, u32[]{:S(2)}) %collective-permute-start.2) | collective-permute-done | bytes 311328 | tf_op jit(solution)/shard_map/ppermute | solution.py:465
  11.2 2.6 %shard_map.43 = (f32[8,8,128]{2,1,0:T(8,128)S(1)}, s32[1]{0:T(128)}) custom-call(s32[3,24]{1,0:T(4,128)S(1)} %bitcast.35, bf16[48,8192]{1,0:T(8,128)(2,1)S(1)} %get-tuple-element.32.both_ref, f32[8,128]{1,0:T(8,128)S(1)} %get-tuple-element.33.block_ref, f32[608,128]{1,0:T(8,128)S(1)} %collective-permute-done.2.got_ref), custom_call_target="tpu_custom_call" | custom-call | tf_op jit(solution)/shard_map/pallas_call | solution.py:268
  13.8 19.4 %all_to_all.10 = f32[8,8,128]{2,1,0:T(8,128)S(1)} all-to-all(f32[8,8,128]{2,1,0:T(8,128)S(1)} %get-tuple-element.35), channel_id=1, replica_groups=mesh['grp'=2,'z'=8,'y'=8,'x_hi'=2,'core'=2] {'z'}, dimensions={0} | all-to-all | bytes 65536 | tf_op jit(solution)/shard_map/all_to_all | solution.py:459
  33.2 0.7 %broadcast_in_dim.8 = f32[64,8,128]{2,1,0:T(8,128)} broadcast(f32[8,128]{1,0:T(8,128)S(1)} %reduce_sum.27), dimensions={1,2} | broadcast | bytes 266240 | tf_op jit(solution)/shard_map/broadcast_in_dim | solution.py:472
  34.0 13.1 %all-to-all-start.1 = ((f32[64,8,128]{2,1,0:T(8,128)}), f32[64,8,128]{2,1,0:T(8,128)S(1)}, u32[]{:S(2)}, u32[]{:S(2)}) async-start(f32[64,8,128]{2,1,0:T(8,128)} %broadcast_in_dim.8), calls=%async_computation.1 | async-start | bytes 524288 | tf_op jit(solution)/shard_map/all_to_all | solution.py:459
  47.1 1.1 %shard_map.44 = f32[608,128]{1,0:T(8,128)S(1)} custom-call(s32[3,24]{1,0:T(4,128)S(1)} %bitcast.36, f32[24,64,256]{2,1,0:T(8,128)S(1)} %copy-done), custom_call_target="tpu_custom_call" | custom-call | tf_op jit(solution)/shard_map/pallas_call | solution.py:125
  48.1 3.4 %collective-permute-start.3 = (f32[608,128]{1,0:T(8,128)S(1)}, f32[608,128]{1,0:T(8,128)S(1)}, u32[]{:S(2)}, u32[]{:S(2)}) collective-permute-start(f32[608,128]{1,0:T(8,128)S(1)} %shard_map.44), channel_id=1, source_target_pairs={{0,256},{256,0},{1,257},{257,1},{2,258},{258,2},{3,259},{259,3},{4... | collective-permute-start | bytes 933896 | tf_op jit(solution)/shard_map/ppermute | solution.py:467
  52.2 8.7 %collective-permute-done.3 = f32[608,128]{1,0:T(8,128)S(1)} collective-permute-done((f32[608,128]{1,0:T(8,128)S(1)}, f32[608,128]{1,0:T(8,128)S(1)}, u32[]{:S(2)}, u32[]{:S(2)}) %collective-permute-start.3) | collective-permute-done | bytes 311328 | tf_op jit(solution)/shard_map/ppermute | solution.py:467
  60.9 0.0 all-to-all-done.1
  60.9 5.0 %conditional.1 = (f32[1,48]{1,0:T(1,128)S(1)}, f32[24,64,256]{2,1,0:T(8,128)}) conditional(s32[]{:T(128)} %bitcast.12, (s32[3,24]{1,0:T(4,128)S(1)}, f32[64,8,128]{2,1,0:T(8,128)S(1)}, f32[24,64,256]{2,1,0:T(8,128)S(1)}, f32[608,128]{1,0:T(8,128)S(1)}, f32[608,128]{1,0:T(8,128)S(1)}) %tuple.42, (s32[3,24]{1,0:T(4,128)S(1)}, ...), branch_computations={%region_1.0_spmd, %region_2.11_spmd} | conditional | flops 172668848 | bytes 24174516 | solution.py:474
  60.9 5.0 %branch_0_fun.1 = (f32[24,64,256]{2,1,0:T(8,128)}, f32[1,48]{1,0:T(1,128)S(1)}) custom-call(s32[3,24]{1,0:T(4,128)S(1)} %get-tuple-element.17.levels_ref, f32[64,8,128]{2,1,0:T(8,128)S(1)} %get-tuple-element.18.parts_ref, f32[24,64,256]{2,1,0:T(8,128)S(1)} %get-tuple-element.19.surplus_ref, f32[608,128]{1,0:T(8,128)S(1)} %get-tuple-element.20.got_near_ref, ...), custom_call_target="tpu_custom_call" | custom-call | tf_op jit(solution)/shard_map/cond/branch_0_fun/pallas_call | solution.py:392
  65.9 0.0 copy-start.4
  65.9 0.5 copy-done.4
  (1 shorter events, 0.0 us)
Async XLA Ops:
  0.6 6.3 %copy-start = (f32[24,64,256]{2,1,0:T(8,128)S(1)}, f32[24,64,256]{2,1,0:T(8,128)}, u32[]{:S(2)}) copy-start(f32[24,64,256]{2,1,0:T(8,128)} %surplus_ref.5) | copy-start | bytes 4718596
  0.6 6.3 %copy-start.1 = (s32[24,3]{0,1:T(4,128)S(1)}, s32[24,3]{0,1:T(4,128)}, u32[]{:S(2)}) copy-start(s32[24,3]{0,1:T(4,128)} %param.5) | copy-start | bytes 868
  3.0 8.2 %collective-permute-start.2 = (f32[608,128]{1,0:T(8,128)S(1)}, f32[608,128]{1,0:T(8,128)S(1)}, u32[]{:S(2)}, u32[]{:S(2)}) collective-permute-start(f32[608,128]{1,0:T(8,128)S(1)} %shard_map.42), channel_id=1, source_target_pairs={{0,256},{256,0},{1,257},{257,1},{2,258},{258,2},{3,259},{259,3},{4... | collective-permute-start | bytes 933896 | tf_op jit(solution)/shard_map/ppermute | solution.py:465
  34.0 26.9 %all-to-all-start.1 = ((f32[64,8,128]{2,1,0:T(8,128)}), f32[64,8,128]{2,1,0:T(8,128)S(1)}, u32[]{:S(2)}, u32[]{:S(2)}) async-start(f32[64,8,128]{2,1,0:T(8,128)} %broadcast_in_dim.8), calls=%async_computation.1 | async-start | bytes 524288 | tf_op jit(solution)/shard_map/all_to_all | solution.py:459
  48.1 12.8 %collective-permute-start.3 = (f32[608,128]{1,0:T(8,128)S(1)}, f32[608,128]{1,0:T(8,128)S(1)}, u32[]{:S(2)}, u32[]{:S(2)}) collective-permute-start(f32[608,128]{1,0:T(8,128)S(1)} %shard_map.44), channel_id=1, source_target_pairs={{0,256},{256,0},{1,257},{257,1},{2,258},{258,2},{3,259},{259,3},{4... | collective-permute-start | bytes 933896 | tf_op jit(solution)/shard_map/ppermute | solution.py:467
  65.9 0.5 copy-start.4

commit v10 on v9

--- a/solution.py
+++ b/solution.py
@@ -7,7 +7,7 @@
 from jax.sharding import PartitionSpec as P
 
 DOM = ("z", "y", "x_hi", "core")
-STAGES = (("z",), ("grp", "y", "x_hi", "core"))
+WIDE = ("grp", "y", "x_hi", "core")
 SWAP = ((0, 1), (1, 0))
 LANES = 128
 SUBSPACES = 64
@@ -284,11 +284,10 @@
 
 def eliminate(parts_ref, grids):
     number = 2 * grids
-    senders = parts_ref.shape[0] // 2
-    first, last = parts_ref[0], parts_ref[senders]
-    for k in range(1, senders):
-        first = first + parts_ref[k]
-        last = last + parts_ref[senders + k]
+    first, last = parts_ref[0, 0], parts_ref[0, 1]
+    for k in range(1, parts_ref.shape[0]):
+        first = first + parts_ref[k, 0]
+        last = last + parts_ref[k, 1]
     gram = unfold(first, last, grids)
     rows = lax.broadcasted_iota(jnp.int32, gram.shape, 0)
     lanes = lax.broadcasted_iota(jnp.int32, gram.shape, 1)
@@ -443,7 +442,7 @@
     pair = jnp.stack([jnp.where(second, 0.0, folded), jnp.where(second, folded, 0.0)])
     for axis in ("grp", *DOM):
         pair = lax.psum(pair, axis)
-    coefficients = solve_parts(pair, grids)
+    coefficients = solve_parts(pair[None], grids)
     start, stop = coefficients[0, :grids], coefficients[0, grids:]
     own = jnp.where(second, stop, start)[:, None, None]
     other = jnp.where(second, start, stop)[:, None, None]
@@ -466,11 +465,10 @@
     near = pack_near(levels, surplus)
     got_far = lax.ppermute(near, "grp", SWAP)
     both, block = own_products(levels, surplus)
-    parts, full = cross_products(levels, both, block, got_near, lax.axis_size(STAGES[0]))
-    for axes, following in zip(STAGES, STAGES[1:]):
-        folded = jnp.sum(exchanged(parts, axes), axis=0)
-        parts = jnp.broadcast_to(folded, (lax.axis_size(following), *folded.shape))
-    parts = exchanged(parts, STAGES[-1])
+    parts, full = cross_products(levels, both, block, got_near, lax.axis_size(WIDE))
+    parts = exchanged(parts, WIDE)
+    sums = jnp.sum(parts.reshape(2, -1, *parts.shape[1:]), axis=1)
+    parts = exchanged(jnp.broadcast_to(sums, (lax.axis_size("z"), *sums.shape)), "z")
     updated, coefficients = lax.cond(
         full[0] > 0,
         lambda: dense_finish(levels, surplus),

time: 66.8 us -> 65.9 us (0.987)
  blocking collectives: 19.4 us -> 0 us
  starting transfers between devices: 20.4 us -> 31.7 us
  waiting for transfers between devices: 10.6 us -> 16.7 us
  Pallas kernels: 13.4 us -> 14.1 us
    all_to_all x1 -> x0, blocking collectives: 19.4 us -> none  [exchanged(): return lax.all_to_all(copies, axes, split_axis=0, concat_axis=0, tiled=True)]
    all_to_all x1 -> x2, waiting for transfers between devices: 0.01 us -> 14.8 us  [exchanged(): return lax.all_to_all(copies, axes, split_axis=0, concat_axis=0, tiled=True)]
    all_to_all x1 -> x2, starting transfers between devices: 13.1 us -> 24.4 us  [exchanged(): return lax.all_to_all(copies, axes, split_axis=0, concat_axis=0, tiled=True)]
    ppermute x1, waiting for transfers between devices: 8.73 us -> 0.01 us  [whole(): got_far = lax.ppermute(near, 'grp', SWAP)]
    pallas_call x1, Pallas kernels: 2.6 us -> 3.32 us  [cross_products(): pl.pallas_call(cross_kernel, compiler_params=GRANT, out_shape=(jax.ShapeD...]
  transfers between devices with their start and end apart: 3 -> 4, of which waited for: 2 -> 3; matrix products, arithmetic and copies ran while one was open for 0% -> 1% of each run, Pallas kernels for 5% -> 5%
where the time goes in v10:
time: 65.9 us; the launch traced here: 65.1 us
  starting transfers between devices  31.7 us (48%)
  waiting for transfers between devices  16.7 us (25%)
  Pallas kernels  14.1 us (21%)
  between operations  1.39 us (2%)
  local copies, waits for them, and re-layouts  1.15 us (2%)
    all_to_all x2, starting transfers between devices, exchanged(): return lax.all_to_all(copies, axes, split_axis=0, concat_axis=0, tiled=True)  24.4 us
    all_to_all x2, waiting for transfers between devices, exchanged(): return lax.all_to_all(copies, axes, split_axis=0, concat_axis=0, tiled=True)  14.8 us
    pallas_call x1, Pallas kernels, finish(): pl.pallas_call(finish_kernel, compiler_params=GRANT, out_shape=(jax.Shape...  4.98 us
    ppermute x1, starting transfers between devices, whole(): got_near = lax.ppermute(far, 'grp', SWAP)  3.94 us
    ppermute x1, starting transfers between devices, whole(): got_far = lax.ppermute(near, 'grp', SWAP)  3.37 us
    pallas_call x1, Pallas kernels, cross_products(): pl.pallas_call(cross_kernel, compiler_params=GRANT, out_shape=(jax.ShapeD...  3.32 us
    pallas_call x1, Pallas kernels, own_products(): pl.pallas_call(own_kernel, compiler_params=GRANT, out_shape=(both, jax.Sh...  2.43 us
    pallas_call x1, Pallas kernels, pack_far(): pl.pallas_call(pack_far_kernel, compiler_params=GRANT, out_shape=jax.Shap...  2.3 us
  transfers between devices with their start and end apart: 4, of which 3 were waited for; matrix products, arithmetic and copies ran while one was open for 1% of the time, Pallas kernels for 5%

profile of v10, /device:TPU:1, one launch (start us, length us, event | category | flops | bytes accessed | tf_op | source)
XLA Modules:
  0.0 65.1 jit_solution(8060127641392688153)
XLA Ops:
  0.6 0.0 copy-start
  0.6 0.0 copy-start.1
  0.6 2.3 %shard_map.42 = f32[608,128]{1,0:T(8,128)S(1)} custom-call(s32[3,24]{1,0:T(4,128)} %bitcast.36, f32[24,64,256]{2,1,0:T(8,128)} %surplus_ref.5), custom_call_target="tpu_custom_call" | custom-call | tf_op jit(solution)/shard_map/pallas_call | solution.py:98
  3.0 3.9 %collective-permute-start.2 = (f32[608,128]{1,0:T(8,128)S(1)}, f32[608,128]{1,0:T(8,128)S(1)}, u32[]{:S(2)}, u32[]{:S(2)}) collective-permute-start(f32[608,128]{1,0:T(8,128)S(1)} %shard_map.42), channel_id=1, source_target_pairs={{0,256},{256,0},{1,257},{257,1},{2,258},{258,2},{3,259},{259,3},{4... | collective-permute-start | bytes 933896 | tf_op jit(solution)/shard_map/ppermute | solution.py:464
  6.9 0.0 copy-done
  6.9 0.0 copy-done.1
  6.9 2.4 %shard_map.41 = (bf16[48,8192]{1,0:T(8,128)(2,1)S(1)}, f32[8,128]{1,0:T(8,128)S(1)}) custom-call(s32[3,24]{1,0:T(4,128)S(1)} %bitcast.37, f32[24,64,256]{2,1,0:T(8,128)S(1)} %copy-done), custom_call_target="tpu_custom_call" | custom-call | tf_op jit(solution)/shard_map/pallas_call | solution.py:185
  9.4 1.8 %collective-permute-done.2.got_ref = f32[608,128]{1,0:T(8,128)S(1)} collective-permute-done((f32[608,128]{1,0:T(8,128)S(1)}, f32[608,128]{1,0:T(8,128)S(1)}, u32[]{:S(2)}, u32[]{:S(2)}) %collective-permute-start.2) | collective-permute-done | bytes 311328 | tf_op jit(solution)/shard_map/ppermute | solution.py:464
  11.2 3.3 %shard_map.43 = (f32[64,8,128]{2,1,0:T(8,128)}, s32[1]{0:T(128)}) custom-call(s32[3,24]{1,0:T(4,128)S(1)} %bitcast.38, bf16[48,8192]{1,0:T(8,128)(2,1)S(1)} %get-tuple-element.32.both_ref, f32[8,128]{1,0:T(8,128)S(1)} %get-tuple-element.33.block_ref, f32[608,128]{1,0:T(8,128)S(1)} %collective-permute-done.2.got_ref), custom_call_target="tpu_custom_call" | custom-call | tf_op jit(solution)/shard_map/pallas_call | solution.py:268
  14.5 14.4 %all-to-all-start = ((f32[64,8,128]{2,1,0:T(8,128)}), f32[64,8,128]{2,1,0:T(8,128)S(1)}, u32[]{:S(2)}, u32[]{:S(2)}) async-start(f32[64,8,128]{2,1,0:T(8,128)} %get-tuple-element.35), calls=%async_computation | async-start | bytes 524288 | tf_op jit(solution)/shard_map/all_to_all | solution.py:458
  28.9 1.1 %shard_map.44 = f32[608,128]{1,0:T(8,128)S(1)} custom-call(s32[3,24]{1,0:T(4,128)S(1)} %bitcast.39, f32[24,64,256]{2,1,0:T(8,128)S(1)} %copy-done), custom_call_target="tpu_custom_call" | custom-call | tf_op jit(solution)/shard_map/pallas_call | solution.py:125
  30.0 3.4 %collective-permute-start.3 = (f32[608,128]{1,0:T(8,128)S(1)}, f32[608,128]{1,0:T(8,128)S(1)}, u32[]{:S(2)}, u32[]{:S(2)}) collective-permute-start(f32[608,128]{1,0:T(8,128)S(1)} %shard_map.44), channel_id=1, source_target_pairs={{0,256},{256,0},{1,257},{257,1},{2,258},{258,2},{3,259},{259,3},{4... | collective-permute-start | bytes 933896 | tf_op jit(solution)/shard_map/ppermute | solution.py:466
  33.4 8.3 %all-to-all-done = f32[64,8,128]{2,1,0:T(8,128)S(1)} async-done(((f32[64,8,128]{2,1,0:T(8,128)}), f32[64,8,128]{2,1,0:T(8,128)S(1)}, u32[]{:S(2)}, u32[]{:S(2)}) %all-to-all-start) | async-done | bytes 262176 | tf_op jit(solution)/shard_map/all_to_all | solution.py:458
  41.8 0.6 broadcast_in_dim.10
  42.4 10.0 %all-to-all-start.1 = ((f32[8,2,8,128]{3,2,1,0:T(8,128)}), f32[8,2,8,128]{3,2,1,0:T(8,128)S(1)}, u32[]{:S(2)}, u32[]{:S(2)}) async-start(f32[8,2,8,128]{3,2,1,0:T(8,128)} %broadcast_in_dim.10), calls=%async_computation.1 | async-start | bytes 131072 | tf_op jit(solution)/shard_map/all_to_all | solution.py:458
  53.1 0.0 collective-permute-done.3
  53.1 6.5 %all-to-all-done.1 = f32[8,2,8,128]{3,2,1,0:T(8,128)S(1)} async-done(((f32[8,2,8,128]{3,2,1,0:T(8,128)}), f32[8,2,8,128]{3,2,1,0:T(8,128)S(1)}, u32[]{:S(2)}, u32[]{:S(2)}) %all-to-all-start.1) | async-done | bytes 65568 | tf_op jit(solution)/shard_map/all_to_all | solution.py:458
  59.6 5.0 %conditional.1 = (f32[1,48]{1,0:T(1,128)S(1)}, f32[24,64,256]{2,1,0:T(8,128)}) conditional(s32[]{:T(128)} %bitcast.13, (s32[3,24]{1,0:T(4,128)S(1)}, f32[8,2,8,128]{3,2,1,0:T(8,128)S(1)}, f32[24,64,256]{2,1,0:T(8,128)S(1)}, f32[608,128]{1,0:T(8,128)S(1)}, f32[608,128]{1,0:T(8,128)S(1)}) %tuple.42, (s32[3,24]{1,0:T(4,128)S(1)}, ...), branch_computations={%region_1.0_spmd, %region_2.11_spmd} | conditional | flops 172668848 | bytes 24174516 | solution.py:472
  59.6 5.0 %branch_0_fun.1 = (f32[24,64,256]{2,1,0:T(8,128)}, f32[1,48]{1,0:T(1,128)S(1)}) custom-call(s32[3,24]{1,0:T(4,128)S(1)} %get-tuple-element.17.levels_ref, f32[8,2,8,128]{3,2,1,0:T(8,128)S(1)} %get-tuple-element.18.parts_ref, f32[24,64,256]{2,1,0:T(8,128)S(1)} %get-tuple-element.19.surplus_ref, f32[608,128]{1,0:T(8,128)S(1)} %get-tuple-element.20.got_near_ref, ...), custom_call_target="tpu_custom_call" | custom-call | tf_op jit(solution)/shard_map/cond/branch_0_fun/pallas_call | solution.py:391
  64.6 0.0 copy-start.4
  64.6 0.5 copy-done.4
  (1 shorter events, 0.0 us)
Async XLA Ops:
  0.6 6.3 %copy-start = (f32[24,64,256]{2,1,0:T(8,128)S(1)}, f32[24,64,256]{2,1,0:T(8,128)}, u32[]{:S(2)}) copy-start(f32[24,64,256]{2,1,0:T(8,128)} %surplus_ref.5) | copy-start | bytes 4718596
  0.6 6.3 %copy-start.1 = (s32[24,3]{0,1:T(4,128)S(1)}, s32[24,3]{0,1:T(4,128)}, u32[]{:S(2)}) copy-start(s32[24,3]{0,1:T(4,128)} %param.5) | copy-start | bytes 868
  3.0 8.2 %collective-permute-start.2 = (f32[608,128]{1,0:T(8,128)S(1)}, f32[608,128]{1,0:T(8,128)S(1)}, u32[]{:S(2)}, u32[]{:S(2)}) collective-permute-start(f32[608,128]{1,0:T(8,128)S(1)} %shard_map.42), channel_id=1, source_target_pairs={{0,256},{256,0},{1,257},{257,1},{2,258},{258,2},{3,259},{259,3},{4... | collective-permute-start | bytes 933896 | tf_op jit(solution)/shard_map/ppermute | solution.py:464
  14.5 27.2 %all-to-all-start = ((f32[64,8,128]{2,1,0:T(8,128)}), f32[64,8,128]{2,1,0:T(8,128)S(1)}, u32[]{:S(2)}, u32[]{:S(2)}) async-start(f32[64,8,128]{2,1,0:T(8,128)} %get-tuple-element.35), calls=%async_computation | async-start | bytes 524288 | tf_op jit(solution)/shard_map/all_to_all | solution.py:458
  30.0 23.1 %collective-permute-start.3 = (f32[608,128]{1,0:T(8,128)S(1)}, f32[608,128]{1,0:T(8,128)S(1)}, u32[]{:S(2)}, u32[]{:S(2)}) collective-permute-start(f32[608,128]{1,0:T(8,128)S(1)} %shard_map.44), channel_id=1, source_target_pairs={{0,256},{256,0},{1,257},{257,1},{2,258},{258,2},{3,259},{259,3},{4... | collective-permute-start | bytes 933896 | tf_op jit(solution)/shard_map/ppermute | solution.py:466
  42.4 17.2 %all-to-all-start.1 = ((f32[8,2,8,128]{3,2,1,0:T(8,128)}), f32[8,2,8,128]{3,2,1,0:T(8,128)S(1)}, u32[]{:S(2)}, u32[]{:S(2)}) async-start(f32[8,2,8,128]{3,2,1,0:T(8,128)} %broadcast_in_dim.10), calls=%async_computation.1 | async-start | bytes 131072 | tf_op jit(solution)/shard_map/all_to_all | solution.py:458
  64.6 0.5 copy-start.4

commit v11 on v10

--- a/solution.py
+++ b/solution.py
@@ -7,7 +7,7 @@
 from jax.sharding import PartitionSpec as P
 
 DOM = ("z", "y", "x_hi", "core")
-WIDE = ("grp", "y", "x_hi", "core")
+WIDE = ("grp", "z", "x_hi", "core")
 SWAP = ((0, 1), (1, 0))
 LANES = 128
 SUBSPACES = 64
@@ -462,13 +462,14 @@
     levels = levels.T
     far = pack_far(levels, surplus)
     got_near = lax.ppermute(far, "grp", SWAP)
-    near = pack_near(levels, surplus)
+    both, block = own_products(levels, surplus)
+    later, block = lax.optimization_barrier((levels, block))
+    near = pack_near(later, surplus)
     got_far = lax.ppermute(near, "grp", SWAP)
-    both, block = own_products(levels, surplus)
     parts, full = cross_products(levels, both, block, got_near, lax.axis_size(WIDE))
     parts = exchanged(parts, WIDE)
     sums = jnp.sum(parts.reshape(2, -1, *parts.shape[1:]), axis=1)
-    parts = exchanged(jnp.broadcast_to(sums, (lax.axis_size("z"), *sums.shape)), "z")
+    parts = exchanged(jnp.broadcast_to(sums, (lax.axis_size("y"), *sums.shape)), "y")
     updated, coefficients = lax.cond(
         full[0] > 0,
         lambda: dense_finish(levels, surplus),

time: 65.9 us -> 65.4 us (level)
  no operation moved by 1% of the time
where the time goes in v11:
time: 65.4 us; the launch traced here: 65.1 us
  starting transfers between devices  31.7 us (48%)
  waiting for transfers between devices  16.7 us (26%)
  Pallas kernels  14.1 us (22%)
  between operations  1.39 us (2%)
  local copies, waits for them, and re-layouts  1.15 us (2%)
    all_to_all x2, starting transfers between devices, exchanged(): return lax.all_to_all(copies, axes, split_axis=0, concat_axis=0, tiled=True)  24.4 us
    all_to_all x2, waiting for transfers between devices, exchanged(): return lax.all_to_all(copies, axes, split_axis=0, concat_axis=0, tiled=True)  14.8 us
    pallas_call x1, Pallas kernels, finish(): pl.pallas_call(finish_kernel, compiler_params=GRANT, out_shape=(jax.Shape...  4.98 us
    ppermute x1, starting transfers between devices, whole(): got_near = lax.ppermute(far, 'grp', SWAP)  3.94 us
    ppermute x1, starting transfers between devices, whole(): got_far = lax.ppermute(near, 'grp', SWAP)  3.37 us
    pallas_call x1, Pallas kernels, cross_products(): pl.pallas_call(cross_kernel, compiler_params=GRANT, out_shape=(jax.ShapeD...  3.32 us
    pallas_call x1, Pallas kernels, own_products(): pl.pallas_call(own_kernel, compiler_params=GRANT, out_shape=(both, jax.Sh...  2.43 us
    pallas_call x1, Pallas kernels, pack_far(): pl.pallas_call(pack_far_kernel, compiler_params=GRANT, out_shape=jax.Shap...  2.3 us
  transfers between devices with their start and end apart: 4, of which 3 were waited for; matrix products, arithmetic and copies ran while one was open for 1% of the time, Pallas kernels for 5%

profile of v11, /device:TPU:1, one launch (start us, length us, event | category | flops | bytes accessed | tf_op | source)
XLA Modules:
  0.0 65.1 jit_solution(8347133602007000303)
XLA Ops:
  0.6 0.0 copy-start
  0.6 0.0 copy-start.1
  0.6 2.3 %shard_map.42 = f32[608,128]{1,0:T(8,128)S(1)} custom-call(s32[3,24]{1,0:T(4,128)} %bitcast.36, f32[24,64,256]{2,1,0:T(8,128)} %surplus_ref.5), custom_call_target="tpu_custom_call" | custom-call | tf_op jit(solution)/shard_map/pallas_call | solution.py:98
  3.0 3.9 %collective-permute-start.2 = (f32[608,128]{1,0:T(8,128)S(1)}, f32[608,128]{1,0:T(8,128)S(1)}, u32[]{:S(2)}, u32[]{:S(2)}) collective-permute-start(f32[608,128]{1,0:T(8,128)S(1)} %shard_map.42), channel_id=1, source_target_pairs={{0,256},{256,0},{1,257},{257,1},{2,258},{258,2},{3,259},{259,3},{4... | collective-permute-start | bytes 933896 | tf_op jit(solution)/shard_map/ppermute | solution.py:464
  6.9 0.0 copy-done
  6.9 0.0 copy-done.1
  6.9 2.4 %shard_map.41 = (bf16[48,8192]{1,0:T(8,128)(2,1)S(1)}, f32[8,128]{1,0:T(8,128)S(1)}) custom-call(s32[3,24]{1,0:T(4,128)S(1)} %bitcast.37, f32[24,64,256]{2,1,0:T(8,128)S(1)} %copy-done), custom_call_target="tpu_custom_call" | custom-call | tf_op jit(solution)/shard_map/pallas_call | solution.py:185
  9.4 1.8 %collective-permute-done.2.got_ref = f32[608,128]{1,0:T(8,128)S(1)} collective-permute-done((f32[608,128]{1,0:T(8,128)S(1)}, f32[608,128]{1,0:T(8,128)S(1)}, u32[]{:S(2)}, u32[]{:S(2)}) %collective-permute-start.2) | collective-permute-done | bytes 311328 | tf_op jit(solution)/shard_map/ppermute | solution.py:464
  11.2 3.3 %shard_map.43 = (f32[64,8,128]{2,1,0:T(8,128)}, s32[1]{0:T(128)}) custom-call(s32[3,24]{1,0:T(4,128)S(1)} %bitcast.38, bf16[48,8192]{1,0:T(8,128)(2,1)S(1)} %get-tuple-element.34.both_ref, f32[8,128]{1,0:T(8,128)S(1)} %get-tuple-element.36.block_ref, f32[608,128]{1,0:T(8,128)S(1)} %collective-permute-done.2.got_ref), custom_call_target="tpu_custom_call" | custom-call | tf_op jit(solution)/shard_map/pallas_call | solution.py:268
  14.5 17.6 %all-to-all-start = ((f32[64,8,128]{2,1,0:T(8,128)}), f32[64,8,128]{2,1,0:T(8,128)S(1)}, u32[]{:S(2)}, u32[]{:S(2)}) async-start(f32[64,8,128]{2,1,0:T(8,128)} %get-tuple-element.38), calls=%async_computation | async-start | bytes 524288 | tf_op jit(solution)/shard_map/all_to_all | solution.py:458
  32.1 1.1 %shard_map.44 = f32[608,128]{1,0:T(8,128)S(1)} custom-call(s32[3,24]{1,0:T(4,128)S(1)} %bitcast.39, f32[24,64,256]{2,1,0:T(8,128)S(1)} %copy-done), custom_call_target="tpu_custom_call" | custom-call | tf_op jit(solution)/shard_map/pallas_call | solution.py:125
  33.2 3.4 %collective-permute-start.3 = (f32[608,128]{1,0:T(8,128)S(1)}, f32[608,128]{1,0:T(8,128)S(1)}, u32[]{:S(2)}, u32[]{:S(2)}) collective-permute-start(f32[608,128]{1,0:T(8,128)S(1)} %shard_map.44), channel_id=1, source_target_pairs={{0,256},{256,0},{1,257},{257,1},{2,258},{258,2},{3,259},{259,3},{4... | collective-permute-start | bytes 933896 | tf_op jit(solution)/shard_map/ppermute | solution.py:468
  36.6 8.3 %all-to-all-done = f32[64,8,128]{2,1,0:T(8,128)S(1)} async-done(((f32[64,8,128]{2,1,0:T(8,128)}), f32[64,8,128]{2,1,0:T(8,128)S(1)}, u32[]{:S(2)}, u32[]{:S(2)}) %all-to-all-start) | async-done | bytes 262176 | tf_op jit(solution)/shard_map/all_to_all | solution.py:458
  45.0 0.6 broadcast_in_dim.10
  45.6 6.8 %all-to-all-start.1 = ((f32[8,2,8,128]{3,2,1,0:T(8,128)}), f32[8,2,8,128]{3,2,1,0:T(8,128)S(1)}, u32[]{:S(2)}, u32[]{:S(2)}) async-start(f32[8,2,8,128]{3,2,1,0:T(8,128)} %broadcast_in_dim.10), calls=%async_computation.1 | async-start | bytes 131072 | tf_op jit(solution)/shard_map/all_to_all | solution.py:458
  53.1 0.0 collective-permute-done.3
  53.1 6.5 %all-to-all-done.1 = f32[8,2,8,128]{3,2,1,0:T(8,128)S(1)} async-done(((f32[8,2,8,128]{3,2,1,0:T(8,128)}), f32[8,2,8,128]{3,2,1,0:T(8,128)S(1)}, u32[]{:S(2)}, u32[]{:S(2)}) %all-to-all-start.1) | async-done | bytes 65568 | tf_op jit(solution)/shard_map/all_to_all | solution.py:458
  59.6 5.0 %conditional.1 = (f32[1,48]{1,0:T(1,128)S(1)}, f32[24,64,256]{2,1,0:T(8,128)}) conditional(s32[]{:T(128)} %bitcast.13, (s32[3,24]{1,0:T(4,128)S(1)}, f32[8,2,8,128]{3,2,1,0:T(8,128)S(1)}, f32[24,64,256]{2,1,0:T(8,128)S(1)}, f32[608,128]{1,0:T(8,128)S(1)}, f32[608,128]{1,0:T(8,128)S(1)}) %tuple.44, (s32[3,24]{1,0:T(4,128)S(1)}, ...), branch_computations={%region_1.0_spmd, %region_2.11_spmd} | conditional | flops 172668848 | bytes 24174516 | solution.py:473
  59.6 5.0 %branch_0_fun.1 = (f32[24,64,256]{2,1,0:T(8,128)}, f32[1,48]{1,0:T(1,128)S(1)}) custom-call(s32[3,24]{1,0:T(4,128)S(1)} %get-tuple-element.17.levels_ref, f32[8,2,8,128]{3,2,1,0:T(8,128)S(1)} %get-tuple-element.18.parts_ref, f32[24,64,256]{2,1,0:T(8,128)S(1)} %get-tuple-element.19.surplus_ref, f32[608,128]{1,0:T(8,128)S(1)} %get-tuple-element.20.got_near_ref, ...), custom_call_target="tpu_custom_call" | custom-call | tf_op jit(solution)/shard_map/cond/branch_0_fun/pallas_call | solution.py:391
  64.6 0.0 copy-start.4
  64.6 0.5 copy-done.4
  (1 shorter events, 0.0 us)
Async XLA Ops:
  0.6 6.3 %copy-start = (f32[24,64,256]{2,1,0:T(8,128)S(1)}, f32[24,64,256]{2,1,0:T(8,128)}, u32[]{:S(2)}) copy-start(f32[24,64,256]{2,1,0:T(8,128)} %surplus_ref.5) | copy-start | bytes 4718596
  0.6 6.3 %copy-start.1 = (s32[24,3]{0,1:T(4,128)S(1)}, s32[24,3]{0,1:T(4,128)}, u32[]{:S(2)}) copy-start(s32[24,3]{0,1:T(4,128)} %param.5) | copy-start | bytes 868
  3.0 8.2 %collective-permute-start.2 = (f32[608,128]{1,0:T(8,128)S(1)}, f32[608,128]{1,0:T(8,128)S(1)}, u32[]{:S(2)}, u32[]{:S(2)}) collective-permute-start(f32[608,128]{1,0:T(8,128)S(1)} %shard_map.42), channel_id=1, source_target_pairs={{0,256},{256,0},{1,257},{257,1},{2,258},{258,2},{3,259},{259,3},{4... | collective-permute-start | bytes 933896 | tf_op jit(solution)/shard_map/ppermute | solution.py:464
  14.5 30.4 %all-to-all-start = ((f32[64,8,128]{2,1,0:T(8,128)}), f32[64,8,128]{2,1,0:T(8,128)S(1)}, u32[]{:S(2)}, u32[]{:S(2)}) async-start(f32[64,8,128]{2,1,0:T(8,128)} %get-tuple-element.38), calls=%async_computation | async-start | bytes 524288 | tf_op jit(solution)/shard_map/all_to_all | solution.py:458
  33.2 19.9 %collective-permute-start.3 = (f32[608,128]{1,0:T(8,128)S(1)}, f32[608,128]{1,0:T(8,128)S(1)}, u32[]{:S(2)}, u32[]{:S(2)}) collective-permute-start(f32[608,128]{1,0:T(8,128)S(1)} %shard_map.44), channel_id=1, source_target_pairs={{0,256},{256,0},{1,257},{257,1},{2,258},{258,2},{3,259},{259,3},{4... | collective-permute-start | bytes 933896 | tf_op jit(solution)/shard_map/ppermute | solution.py:468
  45.6 14.0 %all-to-all-start.1 = ((f32[8,2,8,128]{3,2,1,0:T(8,128)}), f32[8,2,8,128]{3,2,1,0:T(8,128)S(1)}, u32[]{:S(2)}, u32[]{:S(2)}) async-start(f32[8,2,8,128]{3,2,1,0:T(8,128)} %broadcast_in_dim.10), calls=%async_computation.1 | async-start | bytes 131072 | tf_op jit(solution)/shard_map/all_to_all | solution.py:458
  64.6 0.5 copy-start.4
